TPU v7x, 32 devices: a whole 2x2x4 slice. The times are simulated.
32 devices in a mesh: gz: 16 (over z, y, x), xy: 2 (over core).
Axes of the slice: x: 2, y: 2, z: 4, core: 2. Of those that a mesh axis runs over, the one named last changes fastest.
Arguments:
- right_side: float32 [2, 16, 16, 2048], P(None, 'gz', 'xy')
- stiff_across: float32 [16, 16, 2048], P('gz', 'xy'), may hold values from 0.3 to 3
- stiff_down: float32 [16, 16, 2048], P('gz', 'xy'), may hold values from 0.3 to 3
- anchor: float32 [16, 16, 2048], P('gz', 'xy'), may hold values from 0.02 to 0.2
- source_node: int32 [16, 2, 1024], P('gz', 'xy'), may hold values from 0 to 16383
- target_cell: int32 [16, 2, 1024], P('gz', 'xy'), may hold values from 0 to 14334, as said below
- corner_weight: float32 [4, 16, 2, 1024], P(None, 'gz', 'xy'), may hold values from 0 to 1, as said below
- block_count: int32 [16, 2], P('gz', 'xy'), may hold values from 1 to 8, as said below
Outputs:
- solution_field: float32 [2, 16, 16, 2048], P(None, 'gz', 'xy')
- residual: float32 [2, 16, 16, 2048], P(None, 'gz', 'xy')
Inputs may be any that keep to these rules, and one draw needn't show every extreme that they name: `target_cell`: each target cell's row is below 7 and its column below 2047 within the block, so all four corners lie in the same block. `corner_weight`: the weights of a slot are nonnegative and sum to 1. `block_count`: some device holds exactly 8 used blocks.
All inputs are finite; a program needn't handle non-finite values.
Results may differ from a plain program's by a relative error of at most 0.00013.
Values sent between devices are 32-bit elements; how exact they have to be, the bound alone decides.
No kernel may reach another device: no remote copies, remote signals or barrier semaphores. Data moves between devices by JAX's collectives and lax.ppermute only.
A program may use at most 64 MiB of HBM per device.

v0:
```python
import jax
import jax.numpy as jnp
from jax import lax
from jax.sharding import PartitionSpec as P

BLOCK = 128
ITERS = 3


def passed_along(block, axis, distance):
    devices = range(lax.axis_size(axis))
    route = [(i - distance, i) for i in devices if i - distance in devices]
    return lax.ppermute(block, axis, route)


def padded_2(cells, sides, width):
    for axis, dim in sides:
        count = lax.axis_size(axis)
        ends = count - 1
        head = lax.slice_in_dim(cells, 0, width, axis=dim)
        tail = lax.slice_in_dim(cells, cells.shape[dim] - width, cells.shape[dim], axis=dim)
        cells = jnp.concatenate(
            [
                lax.ppermute(tail, axis, [(i, (i + 1) % count) for i in range(ends)]),
                cells,
                lax.ppermute(head, axis, [((i + 1) % count, i) for i in range(ends)]),
            ],
            axis=dim,
        )
    return cells


def two_products(residual, image):
    return lax.psum((jnp.sum(residual * residual), jnp.sum(residual * image)), ("gz", "xy"))


def body(
    right_side,
    stiff_across,
    stiff_down,
    anchor,
    source_node,
    target_cell,
    corner_weight,
    block_count,
):
    rows = stiff_across.shape[1]
    cols = stiff_across.shape[2]
    rhs = right_side[:, 0]
    across = stiff_across[0]
    down = stiff_down[0]
    hold = anchor[0]
    source = source_node[0, 0]
    target = target_cell[0, 0]
    weights = corner_weight[:, 0, 0]
    count = block_count[0, 0]
    slots = source.shape[0]
    has_next = lax.axis_index("gz") < lax.axis_size("gz") - 1
    live = ((jnp.arange(slots, dtype=jnp.int32) < count * BLOCK) & has_next).astype(jnp.float32)
    offsets = jnp.array([0, 1, cols, cols + 1], dtype=jnp.int32)
    corners = target[None, :] + offsets[:, None]
    rim = passed_along(down[-1:, :], "xy", 1)
    down_above = jnp.concatenate([rim, down[:-1]], 0)
    across_left = jnp.concatenate([jnp.zeros((rows, 1), jnp.float32), across[:, :-1]], 1)

    def springs(field):
        padded = padded_2(field, (("xy", 1),), 1)
        upper = padded[:, :-2]
        lower = padded[:, 2:]
        zero_col = jnp.zeros((2, rows, 1), jnp.float32)
        right = jnp.concatenate([field[:, :, 1:], zero_col], 2)
        left = jnp.concatenate([zero_col, field[:, :, :-1]], 2)
        return (
            across * (field - right)
            + across_left * (field - left)
            + down * (field - lower)
            + down_above * (field - upper)
            + hold * field
        )

    def links(field):
        flat = field.reshape(2, rows * cols)
        own_values = flat[:, source]
        empty = jnp.zeros((2, rows * cols), jnp.float32)
        following = passed_along(flat, "gz", -1)
        interp = jnp.sum(weights[None] * following[:, corners], 1)
        error = (interp - own_values) * live[None]
        spread = empty.at[:, corners.reshape(-1)].add(
            (weights[None] * error[:, None, :]).reshape(2, -1)
        )
        onward = passed_along(spread, "gz", 1)
        own = empty.at[:, source].add(-error)
        return (own + onward).reshape(2, rows, cols)

    def operate(field):
        return springs(field) + links(field)

    solution_field = jnp.zeros_like(rhs)
    residual = rhs
    image = operate(residual)
    norm_now, product = two_products(residual, image)
    alpha = norm_now / product
    direction, along = (residual, image)
    for step in range(ITERS):
        solution_field = solution_field + alpha * direction
        residual = residual - alpha * along
        if step + 1 < ITERS:
            image = operate(residual)
            norm_next, product = two_products(residual, image)
            ratio = norm_next / norm_now
            alpha = norm_next / (product - ratio * norm_next / alpha)
            direction = residual + ratio * direction
            along = image + ratio * along
            norm_now = norm_next
    return (solution_field[:, None], residual[:, None])


def solution(mesh):
    in_specs = (
        P(None, "gz", "xy", None),
        P("gz", "xy", None),
        P("gz", "xy", None),
        P("gz", "xy", None),
        P("gz", "xy", None),
        P("gz", "xy", None),
        P(None, "gz", "xy", None),
        P("gz", "xy"),
    )
    out_specs = (P(None, "gz", "xy", None), P(None, "gz", "xy", None))
    return jax.shard_map(body, mesh=mesh, in_specs=in_specs, out_specs=out_specs, check_vma=False)
```

profile of v0, /device:TPU:0, one launch (start us, length us, event | category | flops | bytes accessed | tf_op | source)
XLA Modules:
  0.0 478.1 jit_solution(10191054004728580233)
XLA Ops:
  11.7 5.4 %copy.23 = f32[2,1,8,2048]{0,3,2,1:T(8,128)} copy(f32[2,1,8,2048]{3,2,1,0:T(8,128)} %param.9) | data formatting | bytes 262144 | tf_op args[0]
  17.2 5.3 %copy.24 = f32[2,16384]{1,0:T(2,128)S(1)} copy(f32[2,16384]{0,1:T(8,128)} %bitcast.76) | data formatting | bytes 262144 | tf_op jit(solution)/shard_map/reshape;squeeze | solution.py:82
  25.5 7.4 %gather_fusion.1 = f32[1024,2]{1,0:T(8,128)} fusion(f32[2,16384]{0,1:T(8,128)} %bitcast.77, s32[1024]{0:T(1024)S(1)} %broadcast_clamp_fusion), kind=kCustom, calls=%fused_computation.1 | custom fusion | bytes 20480 | tf_op jit(solution)/shard_map/gather | solution.py:83
  33.0 5.0 %copy.25 = f32[2,16384]{0,1:T(8,128)} copy(f32[2,16384]{1,0:T(2,128)S(1)} %collective-permute-done.3) | data formatting | bytes 262144 | tf_op jit(solution)/shard_map/ppermute | solution.py:13
  38.0 14.1 %gather_fusion = f32[4096,2]{1,0:T(8,128)S(1)} fusion(f32[2,16384]{0,1:T(8,128)} %copy.25, s32[4096]{0:T(1024)S(1)} %bitcast_clamp_fusion), kind=kCustom, calls=%fused_computation | custom fusion | bytes 81920 | tf_op jit(solution)/shard_map/gather | solution.py:86
  54.7 26.1 %scatter_custom_fusion = f32[2,16384]{0,1:T(8,128)} fusion(s32[4096]{0:T(1024)S(1)} %bitcast.108, f32[]{:T(128)} %constant.8.clone.1, f32[2,4096]{0,1:T(8,128)S(1)} %bitcast_multiply_fusion.2), kind=kCustom, calls=%fused_computation.16 | custom fusion | flops 8192 | bytes 2228228 | tf_op jit(solution)/shard_map/scatter-add | solution.py:88
  80.8 5.3 %copy.26 = f32[2,16384]{1,0:T(2,128)S(1)} copy(f32[2,16384]{0,1:T(8,128)} %scatter_custom_fusion) | data formatting | bytes 262144 | tf_op jit(solution)/shard_map/scatter-add | solution.py:88
  86.2 4.9 %collective-permute-start.4 = (f32[2,16384]{1,0:T(2,128)S(1)}, f32[2,16384]{1,0:T(2,128)S(1)}, u32[]{:S(2)}, u32[]{:S(2)}) collective-permute-start(f32[2,16384]{1,0:T(2,128)S(1)} %copy.26), channel_id=1, source_target_pairs={{0,2},{2,4},{4,6},{6,8},{8,10},{10,12},{12,14},{14,16},{16,18},{18... | collective-permute-start | bytes 393224 | tf_op jit(solution)/shard_map/ppermute | solution.py:13
  93.5 4.9 %copy.27 = f32[2,16384]{0,1:T(8,128)} copy(f32[2,16384]{1,0:T(2,128)S(1)} %collective-permute-done.4) | data formatting | bytes 262144 | tf_op jit(solution)/shard_map/ppermute | solution.py:13
  98.4 12.2 %scatter_custom_fusion.1 = f32[2,16384]{0,1:T(8,128)} fusion(f32[2,16384]{0,1:T(8,128)} %copy.27, s32[1024]{0:T(1024)} %bitcast.112, f32[2,1024]{0,1:T(8,128)S(1)} %multiply_bitcast_fusion.2), kind=kCustom, calls=%fused_computation.31 | custom fusion | flops 4096 | bytes 139264 | tf_op jit(solution)/shard_map/scatter-add | solution.py:92
  110.7 5.2 %copy.28 = f32[2,8,2048]{2,1,0:T(8,128)S(1)} copy(f32[2,8,2048]{0,2,1:T(8,128)} %bitcast.83) | data formatting | bytes 262144 | tf_op jit(solution)/shard_map/reshape | solution.py:93
  117.4 44.8 %all-reduce.9 = (f32[]{:T(128)}, f32[]{:T(128)}) all-reduce(f32[]{:T(128)} %get-tuple-element.7, f32[]{:T(128)} %get-tuple-element.6), channel_id=1, replica_groups=mesh['gz'=16,'xy'=2] {'gz','xy'}, use_global_device_ids=true, to_apply=%region_1.0 | all-reduce | flops 2 | bytes 16 | tf_op jit(solution)/shard_map/psum | solution.py:34
  168.1 5.3 %copy.30 = f32[2,16384]{1,0:T(2,128)S(1)} copy(f32[2,16384]{0,1:T(8,128)} %bitcast.80) | data formatting | bytes 262144 | tf_op jit(solution)/shard_map/reshape | solution.py:82
  175.4 7.4 %gather_fusion.3 = f32[1024,2]{1,0:T(8,128)} fusion(f32[2,16384]{0,1:T(8,128)} %bitcast.81, s32[1024]{0:T(1024)S(1)} %copy-done.10), kind=kCustom, calls=%fused_computation.3 | custom fusion | bytes 20480 | tf_op jit(solution)/shard_map/gather | solution.py:83
  187.8 4.9 %copy.31 = f32[2,16384]{0,1:T(8,128)} copy(f32[2,16384]{1,0:T(2,128)S(1)} %collective-permute-done.7) | data formatting | bytes 262144 | tf_op jit(solution)/shard_map/ppermute | solution.py:13
  192.8 14.1 %gather_fusion.2 = f32[4096,2]{1,0:T(8,128)S(1)} fusion(f32[2,16384]{0,1:T(8,128)} %copy.31, s32[4096]{0:T(1024)S(1)} %bitcast_clamp_fusion), kind=kCustom, calls=%fused_computation.2 | custom fusion | bytes 81920 | tf_op jit(solution)/shard_map/gather | solution.py:86
  209.5 26.2 %scatter_custom_fusion.2 = f32[2,16384]{0,1:T(8,128)} fusion(s32[4096]{0:T(1024)} %bitcast.109, f32[]{:T(128)} %constant.8.clone.1, f32[2,4096]{0,1:T(8,128)S(1)} %bitcast_multiply_fusion.1), kind=kCustom, calls=%fused_computation.14 | custom fusion | flops 8192 | bytes 164352 | tf_op jit(solution)/shard_map/scatter-add | solution.py:88
  235.8 5.3 %copy.32 = f32[2,16384]{1,0:T(2,128)S(1)} copy(f32[2,16384]{0,1:T(8,128)} %scatter_custom_fusion.2) | data formatting | bytes 262144 | tf_op jit(solution)/shard_map/scatter-add | solution.py:88
  248.4 4.9 %copy.33 = f32[2,16384]{0,1:T(8,128)} copy(f32[2,16384]{1,0:T(2,128)S(1)} %collective-permute-done.8) | data formatting | bytes 262144 | tf_op jit(solution)/shard_map/ppermute | solution.py:13
  253.3 12.2 %scatter_custom_fusion.3 = f32[2,16384]{0,1:T(8,128)} fusion(f32[2,16384]{0,1:T(8,128)} %copy.33, s32[1024]{0:T(1024)} %bitcast.113, f32[2,1024]{0,1:T(8,128)S(1)} %multiply_bitcast_fusion.1), kind=kCustom, calls=%fused_computation.29 | custom fusion | flops 4096 | bytes 139264 | tf_op jit(solution)/shard_map/scatter-add | solution.py:92
  265.5 5.2 %copy.34 = f32[2,8,2048]{2,1,0:T(8,128)S(1)} copy(f32[2,8,2048]{0,2,1:T(8,128)} %bitcast.84) | data formatting | bytes 262144 | tf_op jit(solution)/shard_map/reshape | solution.py:93
  272.2 43.4 %all-reduce.8 = (f32[]{:T(128)}, f32[]{:T(128)}) all-reduce(f32[]{:T(128)} %get-tuple-element.5, f32[]{:T(128)} %get-tuple-element.4), channel_id=1, replica_groups=mesh['gz'=16,'xy'=2] {'gz','xy'}, use_global_device_ids=true, to_apply=%region_8.0 | all-reduce | flops 2 | bytes 16 | tf_op jit(solution)/shard_map/psum | solution.py:34
  324.6 5.3 %copy.36 = f32[2,16384]{1,0:T(2,128)S(1)} copy(f32[2,16384]{0,1:T(8,128)} %bitcast.78) | data formatting | bytes 262144 | tf_op jit(solution)/shard_map/reshape | solution.py:82
  331.9 7.4 %gather_fusion.5 = f32[1024,2]{1,0:T(8,128)} fusion(f32[2,16384]{0,1:T(8,128)} %bitcast.79, s32[1024]{0:T(1024)S(1)} %copy-done.10), kind=kCustom, calls=%fused_computation.5 | custom fusion | bytes 20480 | tf_op jit(solution)/shard_map/gather | solution.py:83
  344.8 4.9 %copy.37 = f32[2,16384]{0,1:T(8,128)} copy(f32[2,16384]{1,0:T(2,128)S(1)} %collective-permute-done.11) | data formatting | bytes 262144 | tf_op jit(solution)/shard_map/ppermute | solution.py:13
  349.7 14.1 %gather_fusion.4 = f32[4096,2]{1,0:T(8,128)S(1)} fusion(f32[2,16384]{0,1:T(8,128)} %copy.37, s32[4096]{0:T(1024)S(1)} %bitcast_clamp_fusion), kind=kCustom, calls=%fused_computation.4 | custom fusion | bytes 81920 | tf_op jit(solution)/shard_map/gather | solution.py:86
  366.5 26.2 %scatter_custom_fusion.4 = f32[2,16384]{0,1:T(8,128)} fusion(s32[4096]{0:T(1024)} %bitcast.110, f32[]{:T(128)} %constant.8.clone.1, f32[2,4096]{0,1:T(8,128)S(1)} %bitcast_multiply_fusion), kind=kCustom, calls=%fused_computation.12 | custom fusion | flops 8192 | bytes 164352 | tf_op jit(solution)/shard_map/scatter-add | solution.py:88
  392.7 5.3 %copy.38 = f32[2,16384]{1,0:T(2,128)S(1)} copy(f32[2,16384]{0,1:T(8,128)} %scatter_custom_fusion.4) | data formatting | bytes 262144 | tf_op jit(solution)/shard_map/scatter-add | solution.py:88
  405.3 4.9 %copy.39 = f32[2,16384]{0,1:T(8,128)} copy(f32[2,16384]{1,0:T(2,128)S(1)} %collective-permute-done.12) | data formatting | bytes 262144 | tf_op jit(solution)/shard_map/ppermute | solution.py:13
  410.3 12.2 %scatter_custom_fusion.5 = f32[2,16384]{0,1:T(8,128)} fusion(f32[2,16384]{0,1:T(8,128)} %copy.39, s32[1024]{0:T(1024)} %bitcast.114, f32[2,1024]{0,1:T(8,128)S(1)} %multiply_bitcast_fusion), kind=kCustom, calls=%fused_computation.27 | custom fusion | flops 4096 | bytes 139264 | tf_op jit(solution)/shard_map/scatter-add | solution.py:92
  422.5 5.2 %copy.40 = f32[2,8,2048]{2,1,0:T(8,128)S(1)} copy(f32[2,8,2048]{0,2,1:T(8,128)} %bitcast.82) | data formatting | bytes 262144 | tf_op jit(solution)/shard_map/reshape | solution.py:93
  429.2 44.2 %all-reduce.7 = (f32[]{:T(128)}, f32[]{:T(128)}) all-reduce(f32[]{:T(128)} %get-tuple-element.3, f32[]{:T(128)} %get-tuple-element.2), channel_id=1, replica_groups=mesh['gz'=16,'xy'=2] {'gz','xy'}, use_global_device_ids=true, to_apply=%region_15.0 | all-reduce | flops 2 | bytes 16 | tf_op jit(solution)/shard_map/psum | solution.py:34
  (93 shorter events, 67.1 us)
Async XLA Ops:
  1.5 89.6 %collective-permute-start.1 = (f32[1,2048]{1,0:T(1,128)S(1)}, f32[1,2048]{1,0:T(1,128)}, u32[]{:S(2)}, u32[]{:S(2)}) collective-permute-start(f32[1,2048]{1,0:T(1,128)S(1)} %slice_bitcast_fusion.1), channel_id=1, source_target_pairs={{0,1},{2,3},{4,5},{6,7},{8,9},{10,11},{12,13},{14,15},{16,17},{18,... | collective-permute-start | bytes 24584 | tf_op jit(solution)/shard_map/ppermute | solution.py:13
  6.1 109.8 %collective-permute-start = (f32[2,1,2048]{2,1,0:T(1,128)}, f32[2,1,2048]{2,1,0:T(1,128)}, u32[]{:S(2)}, u32[]{:S(2)}) collective-permute-start(f32[2,1,2048]{2,1,0:T(1,128)} %get-tuple-element.29), channel_id=1, source_target_pairs={{1,0},{3,2},{5,4},{7,6},{9,8},{11,10},{13,12},{15,14},{17,16},{19,... | collective-permute-start | bytes 49160 | tf_op jit(solution)/shard_map/ppermute | solution.py:26
  7.4 16.5 %copy-start.13 = (s32[1,1,1024]{2,1,0:T(1,128)S(1)}, s32[1,1,1024]{2,1,0:T(1,128)}, u32[]{:S(2)}) copy-start(s32[1,1,1024]{2,1,0:T(1,128)} %param.14) | copy-start | bytes 12292
  7.4 16.5 %copy-start.15 = (s32[4]{0:T(128)S(1)}, s32[4]{0:T(128)}, u32[]{:S(2)}) copy-start(s32[4]{0:T(128)} %constant.4.clone) | copy-start | bytes 52
  7.4 16.6 %copy-start.1 = (f32[1,8,2048]{2,1,0:T(8,128)S(1)}, f32[1,8,2048]{2,1,0:T(8,128)}, u32[]{:S(2)}) copy-start(f32[1,8,2048]{2,1,0:T(8,128)} %param.11) | copy-start | bytes 196612
  7.4 16.6 %copy-start = (f32[2,1,8,2048]{3,2,1,0:T(8,128)S(1)}, f32[2,1,8,2048]{3,2,1,0:T(8,128)}, u32[]{:S(2)}) copy-start(f32[2,1,8,2048]{3,2,1,0:T(8,128)} %param.9) | copy-start | bytes 393220
  7.4 17.3 %copy-start.14 = (s32[1,1,1024]{2,1,0:T(1,128)S(1)}, s32[1,1,1024]{2,1,0:T(1,128)}, u32[]{:S(2)}) copy-start(s32[1,1,1024]{2,1,0:T(1,128)} %param.13) | copy-start | bytes 12292
  7.4 18.1 %copy-start.6 = (f32[4,1,1,1024]{3,2,1,0:T(1,128)S(1)}, f32[4,1,1,1024]{3,2,1,0:T(1,128)}, u32[]{:S(2)}) copy-start(f32[4,1,1,1024]{3,2,1,0:T(1,128)} %param.15) | copy-start | bytes 49156
  7.4 25.5 %copy-start.2 = (f32[1,8,2048]{2,1,0:T(8,128)S(1)}, f32[1,8,2048]{2,1,0:T(8,128)}, u32[]{:S(2)}) copy-start(f32[1,8,2048]{2,1,0:T(8,128)} %param.10) | copy-start | bytes 196612
  7.4 108.5 %collective-permute-start.2 = (f32[2,1,2048]{2,1,0:T(1,128)}, f32[2,1,2048]{2,1,0:T(1,128)}, u32[]{:S(2)}, u32[]{:S(2)}) collective-permute-start(f32[2,1,2048]{2,1,0:T(1,128)} %get-tuple-element.30), channel_id=1, source_target_pairs={{0,1},{2,3},{4,5},{6,7},{8,9},{10,11},{12,13},{14,15},{16,17},{18,... | collective-permute-start | bytes 49160 | tf_op jit(solution)/shard_map/ppermute | solution.py:24
  22.5 10.5 %collective-permute-start.3 = (f32[2,16384]{1,0:T(2,128)S(1)}, f32[2,16384]{1,0:T(2,128)S(1)}, u32[]{:S(2)}, u32[]{:S(2)}) collective-permute-start(f32[2,16384]{1,0:T(2,128)S(1)} %copy.24), channel_id=1, source_target_pairs={{2,0},{4,2},{6,4},{8,6},{10,8},{12,10},{14,12},{16,14},{18,16},{20... | collective-permute-start | bytes 393224 | tf_op jit(solution)/shard_map/ppermute | solution.py:13
  24.7 8.2 %copy-start.12 = (s32[1024,1]{0,1:T(1,128)}, s32[1024,1]{0,1:T(1,128)S(1)}, u32[]{:S(2)}) copy-start(s32[1024,1]{0,1:T(1,128)S(1)} %compare_select_fusion.2) | copy-start | bytes 12292
  24.8 56.0 %copy-start.11 = (s32[4096,1]{0,1:T(1,128)}, s32[4096,1]{0,1:T(1,128)S(1)}, u32[]{:S(2)}) copy-start(s32[4096,1]{0,1:T(1,128)S(1)} %compare_select_fusion) | copy-start | bytes 49156
  24.8 8.1 %copy-start.9 = (s32[1024]{0:T(1024)}, s32[1024]{0:T(1024)S(1)}, u32[]{:S(2)}) copy-start(s32[1024]{0:T(1024)S(1)} %broadcast_clamp_fusion) | copy-start | bytes 12292
  33.0 47.8 %copy-start.7 = (f32[1024]{0:T(1024)}, f32[1024]{0:T(1024)S(1)}, u32[]{:S(2)}) copy-start(f32[1024]{0:T(1024)S(1)} %fusion.44) | copy-start | bytes 12292
  86.2 7.4 %collective-permute-start.4 = (f32[2,16384]{1,0:T(2,128)S(1)}, f32[2,16384]{1,0:T(2,128)S(1)}, u32[]{:S(2)}, u32[]{:S(2)}) collective-permute-start(f32[2,16384]{1,0:T(2,128)S(1)} %copy.26), channel_id=1, source_target_pairs={{0,2},{2,4},{4,6},{6,8},{8,10},{10,12},{12,14},{14,16},{16,18},{18... | collective-permute-start | bytes 393224 | tf_op jit(solution)/shard_map/ppermute | solution.py:13
  98.4 17.5 %copy-start.3 = (f32[1,8,2048]{2,1,0:T(8,128)S(1)}, f32[1,8,2048]{2,1,0:T(8,128)}, u32[]{:S(2)}) copy-start(f32[1,8,2048]{2,1,0:T(8,128)} %param.12) | copy-start | bytes 196612
  98.4 17.5 %copy-start.5 = (f32[2,8,2047]{2,1,0:T(8,128)S(1)}, f32[2,8,2047]{2,1,0:T(8,128)}, u32[]{:S(2)}) copy-start(f32[2,8,2047]{2,1,0:T(8,128)} %get-tuple-element.28) | copy-start | bytes 393028
  163.5 11.9 %copy-start.10 = (s32[1024]{0:T(1024)S(1)}, s32[1024]{0:T(1024)}, u32[]{:S(2)}) copy-start(s32[1024]{0:T(1024)} %copy-done.9) | copy-start | bytes 12292
  168.1 39.6 %copy-start.8 = (f32[1024]{0:T(1024)S(1)}, f32[1024]{0:T(1024)}, u32[]{:S(2)}) copy-start(f32[1024]{0:T(1024)} %copy-done.7) | copy-start | bytes 12292
  173.4 14.4 %collective-permute-start.7 = (f32[2,16384]{1,0:T(2,128)S(1)}, f32[2,16384]{1,0:T(2,128)S(1)}, u32[]{:S(2)}, u32[]{:S(2)}) collective-permute-start(f32[2,16384]{1,0:T(2,128)S(1)} %copy.30), channel_id=1, source_target_pairs={{2,0},{4,2},{6,4},{8,6},{10,8},{12,10},{14,12},{16,14},{18,16},{20... | collective-permute-start | bytes 393224 | tf_op jit(solution)/shard_map/ppermute | solution.py:13
  182.7 88.0 %collective-permute-start.5 = (f32[2,1,2048]{2,1,0:T(1,128)}, f32[2,1,2048]{2,1,0:T(1,128)S(1)}, u32[]{:S(2)}, u32[]{:S(2)}) collective-permute-start(f32[2,1,2048]{2,1,0:T(1,128)} %get-tuple-element.25), channel_id=1, source_target_pairs={{1,0},{3,2},{5,4},{7,6},{9,8},{11,10},{13,12},{15,14},{17,16},{19,... | collective-permute-start | bytes 49160 | tf_op jit(solution)/shard_map/ppermute | solution.py:26
  184.2 86.5 %collective-permute-start.6 = (f32[2,1,2048]{2,1,0:T(1,128)}, f32[2,1,2048]{2,1,0:T(1,128)}, u32[]{:S(2)}, u32[]{:S(2)}) collective-permute-start(f32[2,1,2048]{2,1,0:T(1,128)} %get-tuple-element.26), channel_id=1, source_target_pairs={{0,1},{2,3},{4,5},{6,7},{8,9},{10,11},{12,13},{14,15},{16,17},{18,... | collective-permute-start | bytes 49160 | tf_op jit(solution)/shard_map/ppermute | solution.py:24
  241.1 7.3 %collective-permute-start.8 = (f32[2,16384]{1,0:T(2,128)S(1)}, f32[2,16384]{1,0:T(2,128)S(1)}, u32[]{:S(2)}, u32[]{:S(2)}) collective-permute-start(f32[2,16384]{1,0:T(2,128)S(1)} %copy.32), channel_id=1, source_target_pairs={{0,2},{2,4},{4,6},{6,8},{8,10},{10,12},{12,14},{14,16},{16,18},{18... | collective-permute-start | bytes 393224 | tf_op jit(solution)/shard_map/ppermute | solution.py:13
  330.0 14.8 %collective-permute-start.11 = (f32[2,16384]{1,0:T(2,128)S(1)}, f32[2,16384]{1,0:T(2,128)S(1)}, u32[]{:S(2)}, u32[]{:S(2)}) collective-permute-start(f32[2,16384]{1,0:T(2,128)S(1)} %copy.36), channel_id=1, source_target_pairs={{2,0},{4,2},{6,4},{8,6},{10,8},{12,10},{14,12},{16,14},{18,16},{20... | collective-permute-start | bytes 393224 | tf_op jit(solution)/shard_map/ppermute | solution.py:13
  339.3 88.4 %collective-permute-start.9 = (f32[2,1,2048]{2,1,0:T(1,128)}, f32[2,1,2048]{2,1,0:T(1,128)}, u32[]{:S(2)}, u32[]{:S(2)}) collective-permute-start(f32[2,1,2048]{2,1,0:T(1,128)} %get-tuple-element.21), channel_id=1, source_target_pairs={{1,0},{3,2},{5,4},{7,6},{9,8},{11,10},{13,12},{15,14},{17,16},{19,... | collective-permute-start | bytes 49160 | tf_op jit(solution)/shard_map/ppermute | solution.py:26
  340.6 87.1 %collective-permute-start.10 = (f32[2,1,2048]{2,1,0:T(1,128)}, f32[2,1,2048]{2,1,0:T(1,128)}, u32[]{:S(2)}, u32[]{:S(2)}) collective-permute-start(f32[2,1,2048]{2,1,0:T(1,128)} %get-tuple-element.22), channel_id=1, source_target_pairs={{0,1},{2,3},{4,5},{6,7},{8,9},{10,11},{12,13},{14,15},{16,17},{18,... | collective-permute-start | bytes 49160 | tf_op jit(solution)/shard_map/ppermute | solution.py:24
  398.0 7.3 %collective-permute-start.12 = (f32[2,16384]{1,0:T(2,128)S(1)}, f32[2,16384]{1,0:T(2,128)S(1)}, u32[]{:S(2)}, u32[]{:S(2)}) collective-permute-start(f32[2,16384]{1,0:T(2,128)S(1)} %copy.38), channel_id=1, source_target_pairs={{0,2},{2,4},{4,6},{6,8},{8,10},{10,12},{12,14},{14,16},{16,18},{18... | collective-permute-start | bytes 393224 | tf_op jit(solution)/shard_map/ppermute | solution.py:13
  410.3 17.5 %copy-start.4 = (f32[1,8,2048]{2,1,0:T(8,128)S(1)}, f32[1,8,2048]{2,1,0:T(8,128)}, u32[]{:S(2)}) copy-start(f32[1,8,2048]{2,1,0:T(8,128)} %param.12) | copy-start | bytes 196612
where the time goes:
time: 480 us; the launch traced here: 478 us
  local copies, waits for them, and re-layouts  161 us (34%)
  blocking collectives  132 us (28%)
  other arithmetic  129 us (27%)
  starting transfers between devices  37.5 us (8%)
  between operations  11.4 us (2%)
  waiting for transfers between devices  6.59 us (1%)
    psum x3, blocking collectives, two_products(): lax.psum((jnp.sum(residual * residual), jnp.sum(residual * image)), ('gz'...  132 us
    scatter-add x3, other arithmetic, links(): empty.at[:, corners.reshape(-1)]  78.6 us
    gather x3, local copies, waits for them, and re-layouts, links(): interp = jnp.sum(weights[None] * following[:, corners], 1)  42.4 us
    scatter-add x3, other arithmetic, links(): own = empty.at[:, source].add(-error)  36.6 us
    ppermute x6, local copies, waits for them, and re-layouts, passed_along(): return lax.ppermute(block, axis, route)  29.5 us
    gather x3, local copies, waits for them, and re-layouts, links(): own_values = flat[:, source]  22.1 us
    ppermute x7, starting transfers between devices, passed_along(): return lax.ppermute(block, axis, route)  21.3 us
    scatter-add x3, local copies, waits for them, and re-layouts, links(): empty.at[:, corners.reshape(-1)]  16 us
  transfers between devices with their start and end apart: 13, of which 3 were waited for; matrix products, arithmetic and copies ran while one was open for 55% of the time, Pallas kernels for 0%

commit v1 on v0

v1 whole, which is shorter than its diff:
```python
import functools

import jax
import jax.numpy as jnp
from jax import lax
from jax.experimental import pallas as pl
from jax.experimental.pallas import tpu as pltpu
from jax.sharding import PartitionSpec as P

BLOCK = 128
ITERS = 3
LANES = 128
GAIN = 0.25
SHIFT = 1.25
F32 = jnp.float32
BF16 = jnp.bfloat16
CHUNK = 256


def swapped(block, axis, first):
    count = lax.axis_size(axis)
    route = []
    for i in range(first, count - 1, 2):
        route += [(i, i + 1), (i + 1, i)]
    return lax.ppermute(block, axis, route) if route else None


def split2(x):
    high = x.astype(BF16)
    return high, (x - high.astype(F32)).astype(BF16)


def div_mod(x, d):
    if d & (d - 1) == 0:
        return lax.shift_right_logical(x, jnp.int32(d.bit_length() - 1)), x & (d - 1)
    q = lax.div(x, jnp.int32(d))
    return q, x - q * d


def hi_lo(index, rows, cols):
    row, col = div_mod(index, cols)
    tile, lane = div_mod(col, LANES)
    return tile * rows + row, lane


def row_of(tile, k):
    return tile[k : k + 1, :]


def one_hot(lanes_of):
    nb = lanes_of.shape[0]
    at = lax.broadcasted_iota(jnp.int32, (LANES, LANES), 0)
    return jnp.concatenate(
        [jnp.where(at == row_of(lanes_of, k), 1.0, 0.0).astype(BF16) for k in range(nb)], axis=1
    )


def tall(field):
    n = field.shape[1] // LANES
    return jnp.concatenate([field[:, i * LANES : (i + 1) * LANES] for i in range(n)], axis=0)


def wide(stack, rows):
    n = stack.shape[0] // rows
    return jnp.concatenate([stack[i * rows : (i + 1) * rows, :] for i in range(n)], axis=1)


def operand(fields):
    out = []
    for f in fields:
        high, low = split2(tall(f))
        out.append(jnp.concatenate([high, low], axis=1))
    return jnp.concatenate(out, axis=0)


def right_of(field):
    return pltpu.roll(field, field.shape[1] - 1, 1)


def looked_up(field, slots_hi, hot2):
    high = tall(field[0]).shape[0]
    left = operand([field[0], field[1]])
    nb = slots_hi.shape[0]
    at = lax.broadcasted_iota(jnp.int32, (high, LANES), 0)
    found = ([], [])
    for k in range(nb):
        got = jnp.dot(left, hot2[:, k * LANES : (k + 1) * LANES], preferred_element_type=F32)
        mask = at == row_of(slots_hi, k)
        for c in range(2):
            found[c].append(
                jnp.sum(jnp.where(mask, got[c * high : (c + 1) * high], 0.0), axis=0, keepdims=True)
            )
    return jnp.stack([jnp.concatenate(f, axis=0) for f in found])


def interpolated(field, slots_hi, hot2, weights):
    high = tall(field[0]).shape[0]
    left = operand([field[0], field[1], right_of(field[0]), right_of(field[1])])
    nb = slots_hi.shape[0]
    at = lax.broadcasted_iota(jnp.int32, (high, LANES), 0)
    found = ([], [])
    for k in range(nb):
        got = jnp.dot(left, hot2[:, k * LANES : (k + 1) * LANES], preferred_element_type=F32)
        here = row_of(slots_hi, k)
        upper = at == here
        lower = at == here + 1
        w = [row_of(weights[q], k) for q in range(4)]
        wl = jnp.where(upper, w[0], jnp.where(lower, w[2], 0.0))
        wr = jnp.where(upper, w[1], jnp.where(lower, w[3], 0.0))
        for c in range(2):
            value = wl * got[c * high : (c + 1) * high] + wr * got[(2 + c) * high : (3 + c) * high]
            found[c].append(jnp.sum(value, axis=0, keepdims=True))
    return jnp.stack([jnp.concatenate(f, axis=0) for f in found])


NT = (((1,), (1,)), ((), ()))


def spread_own(values, slots_hi, hot, rows, high):
    nb = slots_hi.shape[0]
    at = lax.broadcasted_iota(jnp.int32, (high, LANES), 0)
    masks = [at == row_of(slots_hi, k) for k in range(nb)]
    parts = []
    for c in range(2):
        high_part = values[c].astype(BF16).astype(F32)
        for part in (high_part, values[c] - high_part):
            parts.append(
                jnp.concatenate(
                    [jnp.where(masks[k], row_of(part, k), 0.0).astype(BF16) for k in range(nb)], axis=1
                )
            )
    out = lax.dot_general(jnp.concatenate(parts, axis=0), hot, NT, preferred_element_type=F32)
    return [
        wide(out[2 * c * high : (2 * c + 1) * high] + out[(2 * c + 1) * high : (2 * c + 2) * high], rows)
        for c in range(2)
    ]


def spread_corners(values, weights, slots_hi, hot, rows, high):
    nb = slots_hi.shape[0]
    at = lax.broadcasted_iota(jnp.int32, (high, LANES), 0)
    upper = [at == row_of(slots_hi, k) for k in range(nb)]
    lower = [at == row_of(slots_hi, k) + 1 for k in range(nb)]
    parts = []
    for c in range(2):
        for side in range(2):
            up = values[c] * weights[side]
            down = values[c] * weights[2 + side]
            up_high = up.astype(BF16).astype(F32)
            down_high = down.astype(BF16).astype(F32)
            for a, b in ((up_high, down_high), (up - up_high, down - down_high)):
                parts.append(
                    jnp.concatenate(
                        [
                            jnp.where(
                                upper[k], row_of(a, k), jnp.where(lower[k], row_of(b, k), 0.0)
                            ).astype(BF16)
                            for k in range(nb)
                        ],
                        axis=1,
                    )
                )
    out = lax.dot_general(jnp.concatenate(parts, axis=0), hot, NT, preferred_element_type=F32)
    result = []
    for c in range(2):
        sides = []
        for side in range(2):
            p = (2 * c + side) * 2
            sides.append(wide(out[p * high : (p + 1) * high] + out[(p + 1) * high : (p + 2) * high], rows))
        result.append(sides[0] + pltpu.roll(sides[1], 1, 1))
    return result


def springs(field, across, down, hold, upper_row, lower_row, rim):
    rows, cols = field.shape
    col = lax.broadcasted_iota(jnp.int32, (rows, cols), 1)
    row = lax.broadcasted_iota(jnp.int32, (rows, cols), 0)
    right = jnp.where(col == cols - 1, 0.0, pltpu.roll(field, cols - 1, 1))
    pull = across * (field - right)
    out = pull - jnp.where(col == 0, 0.0, pltpu.roll(pull, 1, 1))
    lower = jnp.where(row == rows - 1, lower_row, pltpu.roll(field, rows - 1, 0))
    pull = down * (field - lower)
    above = rim * (upper_row - field[0:1, :])
    out = out + pull - jnp.where(row == 0, above, pltpu.roll(pull, 1, 0))
    return out + hold * field


def pick(flag, a, b):
    return jnp.where(flag, a, b)


def edges_of(get_row, rows, even_b, two):
    first = [get_row(c, 0) for c in range(2)]
    last = [get_row(c, rows - 1) for c in range(2)]
    out = [jnp.concatenate([pick(even_b, last[c], first[c]) for c in range(2)], axis=0)]
    if two:
        out.append(jnp.concatenate([pick(even_b, first[c], last[c]) for c in range(2)], axis=0))
    return out


def pack_kernel(two, flags, count, field, down, source, target, weights, pack, *edges):
    rows, cols = down.shape
    even_b = flags[1] == 0
    has_next = flags[2]
    nb = source.shape[0]
    block = lax.broadcasted_iota(jnp.int32, (nb, LANES), 0)
    live = jnp.where(block * LANES < count[0, 0] * BLOCK * has_next, 1.0, 0.0)
    for c in range(2):
        pack[:, c * cols : (c + 1) * cols] = field[c]
    parts = [source[...].astype(F32), target[...].astype(F32)] + [weights[q] * live for q in range(4)]
    for i, part in enumerate(parts):
        pack[:nb, 2 * cols + i * LANES : 2 * cols + (i + 1) * LANES] = part
    messages = edges_of(lambda c, r: field[c, r : r + 1, :], rows, even_b, two)
    for message, edge in zip(messages, edges):
        edge[0:2, :] = message
        edge[2:3, :] = down[rows - 1 : rows, :]


def halves(flags, edge_refs):
    even_b = flags[1] == 0
    zero = edge_refs[0][...]
    if len(edge_refs) == 2:
        other = edge_refs[1][...]
    else:
        other = jnp.zeros_like(zero)
    return pick(even_b, other, zero), pick(even_b, zero, other)


def advance(field, error, error_prev, own, prev, across, down, hold, above, below, rim):
    own_hi, own_hot = own
    prev_hi, prev_hot, prev_weights = prev
    rows, cols = field[0].shape
    high = rows * (cols // LANES)
    pulled = spread_own(error, own_hi, own_hot, rows, high)
    pushed = spread_corners(error_prev, prev_weights, prev_hi, prev_hot, rows, high)
    result = []
    for c in range(2):
        image = springs(field[c], across, down, hold, above[c : c + 1], below[c : c + 1], rim)
        image = image + (pushed[c] - pulled[c])
        result.append(GAIN * image - SHIFT * field[c])
    return result


def step_kernel(
    first, last, two, n_edges, flags, count, field_ref, across, down, hold, source, weights_or_prev, local, *rest
):
    rest = list(rest)
    take = lambda n: [rest.pop(0) for _ in range(n)]
    even = flags[0] == 0
    even_b = flags[1] == 0
    has_next = flags[2]
    nb = source.shape[0]
    rows, cols = across.shape
    block = lax.broadcasted_iota(jnp.int32, (nb, LANES), 0)
    live = jnp.where(block * LANES < count[0, 0] * BLOCK * has_next, 1.0, 0.0)
    field = [field_ref[0], field_ref[1]]
    own_hi, own_lo = hi_lo(source[...], rows, cols)
    own_hot = one_hot(own_lo)
    own_hot2 = jnp.concatenate([own_hot, own_hot], axis=0)
    got0, got1 = take(2)
    edge_refs = take(n_edges)
    above, below = halves(flags, edge_refs)
    if first:
        target = local
        rim = above[2:3, :]
        slot = lambda ref, i: ref[:nb, 2 * cols + i * LANES : 2 * cols + (i + 1) * LANES]
        prev_parts = [pick(even, slot(got1, i), slot(got0, i)) for i in range(6)]
        prev_target = prev_parts[1].astype(jnp.int32)
        prev_weights = prev_parts[2:]
        prev_hi, prev_lo = hi_lo(prev_target, rows, cols)
        prev_hot = one_hot(prev_lo)
        prev_hot2 = jnp.concatenate([prev_hot, prev_hot], axis=0)
        comp = lambda ref, c: ref[:, c * cols : (c + 1) * cols]
        next_field = [pick(even, comp(got0, c), comp(got1, c)) for c in range(2)]
        prev_field = [pick(even, comp(got1, c), comp(got0, c)) for c in range(2)]
        own = looked_up(field, own_hi, own_hot2)
        mid = interpolated(field, prev_hi, prev_hot2, prev_weights)
        t_hi, t_lo = hi_lo(target[...], rows, cols)
        t_hot = one_hot(t_lo)
        own_weights = [weights_or_prev[q] for q in range(4)]
        from_next = interpolated(next_field, t_hi, jnp.concatenate([t_hot, t_hot], axis=0), own_weights)
        p_hi, p_lo = hi_lo(prev_parts[0].astype(jnp.int32), rows, cols)
        p_hot = one_hot(p_lo)
        from_prev = looked_up(prev_field, p_hi, jnp.concatenate([p_hot, p_hot], axis=0))
    else:
        rim = rest.pop(0)[...]
        prev_ref = weights_or_prev
        prev_target = prev_ref[0].astype(jnp.int32)
        prev_weights = [prev_ref[1 + q] for q in range(4)]
        prev_hi, prev_lo = hi_lo(prev_target, rows, cols)
        prev_hot = one_hot(prev_lo)
        prev_hot2 = jnp.concatenate([prev_hot, prev_hot], axis=0)
        own, mid = local[0], local[1]
        from_next = pick(even, got0[...], got1[...])
        from_prev = pick(even, got1[...], got0[...])
    if last:
        earlier = take(2)
    error = [live * (from_next[c] - own[c]) for c in range(2)]
    error_prev = [mid[c] - from_prev[c] for c in range(2)]
    after = advance(
        field,
        error,
        error_prev,
        (own_hi, own_hot),
        (prev_hi, prev_hot, prev_weights),
        across[...],
        down[...],
        hold[...],
        above,
        below,
        rim,
    )
    out = rest.pop(0)
    for c in range(2):
        out[c] = after[c]
    if last:
        moments = rest.pop(0)
        basis = [[ref[0], ref[1]] for ref in earlier] + [field, after]
        lane = lax.broadcasted_iota(jnp.int32, (1, LANES), 1)
        total = jnp.zeros((1, LANES), F32)
        for i in range(2 * ITERS):
            u, w = basis[i // 2], basis[i - i // 2]
            s = u[0] * w[0] + u[1] * w[1]
            s = jnp.sum(jnp.sum(s, axis=0, keepdims=True), axis=1, keepdims=True)
            total = total + jnp.where(lane == i, s, 0.0)
        moments[...] = jnp.broadcast_to(total, moments.shape)
        return
    after_own = looked_up(after, own_hi, own_hot2)
    after_mid = interpolated(after, prev_hi, prev_hot2, prev_weights)
    local_out, send0, send1 = take(3)
    local_out[0] = after_own
    local_out[1] = after_mid
    send0[...] = pick(even, after_own, after_mid)
    send1[...] = pick(even, after_mid, after_own)
    messages = edges_of(lambda c, r: after[c][r : r + 1, :], rows, even_b, two)
    for message, edge in zip(messages, take(len(messages))):
        edge[...] = message
    if first:
        prev_out, rim_out = take(2)
        prev_out[0] = prev_parts[1]
        for q in range(4):
            prev_out[1 + q] = prev_weights[q]
        rim_out[...] = rim


def conjugate(moments):
    def apply(p):
        shifted = [None] + p
        return [
            (SHIFT * p[k] if k < len(p) else 0.0) * (1.0 / GAIN)
            + ((1.0 / GAIN) * shifted[k] if k else 0.0)
            for k in range(len(p) + 1)
        ]

    def product(p, q):
        return sum(p[i] * q[j] * moments[i + j] for i in range(len(p)) for j in range(len(q)))

    def plus(p, factor, q):
        size = max(len(p), len(q))
        pad = lambda a: a + [None] * (size - len(a))
        out = []
        for a, b in zip(pad(p), pad(q)):
            out.append(factor * b if a is None else a if b is None else a + factor * b)
        return out

    one = jnp.ones_like(moments[0])
    solution_field, residual, direction = [], [one], [one]
    norm_now = moments[0]
    for step in range(ITERS):
        image = apply(direction)
        alpha = norm_now / product(direction, image)
        solution_field = plus(solution_field, alpha, direction)
        residual = plus(residual, -alpha, image)
        if step + 1 < ITERS:
            norm_next = product(residual, residual)
            direction = plus(residual, norm_next / norm_now, direction)
            norm_now = norm_next
    return solution_field, residual


def finish_kernel(sums, *refs):
    basis, (solution_ref, residual_ref) = refs[: ITERS + 1], refs[ITERS + 1 :]
    total = jnp.sum(sums[...], axis=0, keepdims=True)
    lane = lax.broadcasted_iota(jnp.int32, (1, LANES), 1)
    moments = [
        jnp.sum(jnp.where(lane == i, total, 0.0), axis=1, keepdims=True) for i in range(2 * ITERS)
    ]
    solution_field, residual = conjugate(moments)
    for c in range(2):
        values = [ref[c] for ref in basis]
        solution_ref[c] = sum(a * v for a, v in zip(solution_field, values))
        residual_ref[c] = sum(a * v for a, v in zip(residual, values))


VMEM = pl.BlockSpec(memory_space=pltpu.VMEM)
SMEM = pl.BlockSpec(memory_space=pltpu.SMEM)


def call(kernel, in_specs, shapes, name):
    shapes = [jax.ShapeDtypeStruct(s, F32) for s in shapes]
    return pl.pallas_call(
        kernel,
        in_specs=in_specs,
        out_specs=[VMEM] * len(shapes),
        out_shape=shapes,
        name=name,
        compiler_params=pltpu.CompilerParams(vmem_limit_bytes=48 * 1024 * 1024),
    )


def body(
    right_side,
    stiff_across,
    stiff_down,
    anchor,
    source_node,
    target_cell,
    corner_weight,
    block_count,
):
    rows, cols = stiff_across.shape[1:]
    rhs = right_side[:, 0]
    across, down, hold = stiff_across[0], stiff_down[0], anchor[0]
    slots = source_node.shape[2]
    nb = slots // LANES
    source = source_node.reshape(nb, LANES)
    target = target_cell.reshape(nb, LANES)
    weights = corner_weight.reshape(4, nb, LANES)
    n_gz, n_xy = lax.axis_size("gz"), lax.axis_size("xy")
    at_gz, at_xy = lax.axis_index("gz"), lax.axis_index("xy")
    two = n_xy > 2
    flags = jnp.stack([at_gz % 2, at_xy % 2, (at_gz < n_gz - 1).astype(jnp.int32)]).astype(jnp.int32)
    n_edges = 2 if two else 1

    pack, *edges = call(
        functools.partial(pack_kernel, two),
        [SMEM, SMEM] + [VMEM] * 5,
        [(rows, 2 * cols + 6 * LANES)] + [(4, cols)] * n_edges,
        "pack",
    )(flags, block_count, rhs, down, source, target, weights)

    def exchange(to0, to1, edges):
        got1 = swapped(to1, "gz", 1)
        got0 = swapped(to0, "gz", 0)
        return got0, got1, [swapped(e, "xy", i) for i, e in enumerate(edges)]

    field_shape = (2, rows, cols)
    message = (2, nb, LANES)
    common = [field_shape, (2,) + message, message, message] + [(2, cols)] * n_edges
    basis = [rhs]

    got0, got1, got_edges = exchange(pack, pack, edges)
    field, local, to0, to1, *tail = call(
        functools.partial(step_kernel, True, False, two, n_edges),
        [SMEM, SMEM] + [VMEM] * (9 + n_edges),
        common + [(5, nb, LANES), (1, cols)],
        "first",
    )(flags, block_count, rhs, across, down, hold, source, weights, target, got0, got1, *got_edges)
    edges, (prev, rim) = tail[:n_edges], tail[n_edges:]

    for step in range(1, ITERS):
        last = step == ITERS - 1
        got0, got1, got_edges = exchange(to0, to1, edges)
        args = [flags, block_count, field, across, down, hold, source, prev, local, got0, got1, *got_edges, rim]
        shapes = common
        if last:
            args += basis
            shapes = [field_shape, (n_gz * n_xy, LANES)]
        basis.append(field)
        field, *tail = call(
            functools.partial(step_kernel, False, last, two, n_edges),
            [SMEM, SMEM] + [VMEM] * (len(args) - 2),
            shapes,
            "last" if last else "step",
        )(*args)
        if not last:
            local, to0, to1, *edges = tail
    basis.append(field)
    sums = tail[0].reshape(n_gz * n_xy, 1, LANES)
    sums = lax.all_to_all(sums, ("gz", "xy"), 0, 0).reshape(n_gz * n_xy, LANES)
    solution_field, residual = call(
        finish_kernel, [VMEM] * (1 + len(basis)), [field_shape] * 2, "finish"
    )(sums, *basis)
    return solution_field[:, None], residual[:, None]


def solution(mesh):
    in_specs = (
        P(None, "gz", "xy", None),
        P("gz", "xy", None),
        P("gz", "xy", None),
        P("gz", "xy", None),
        P("gz", "xy", None),
        P("gz", "xy", None),
        P(None, "gz", "xy", None),
        P("gz", "xy"),
    )
    out_specs = (P(None, "gz", "xy", None), P(None, "gz", "xy", None))
    return jax.shard_map(body, mesh=mesh, in_specs=in_specs, out_specs=out_specs, check_vma=False)
```

time: 480 us -> 56.8 us (0.12)
  local copies, waits for them, and re-layouts: 161 us -> 2.34 us
  other arithmetic: 129 us -> 0.08 us
  blocking collectives: 132 us -> 16.9 us
  starting transfers between devices: 37.5 us -> 14.6 us
  Pallas kernels: 0 us -> 12 us
  between operations: 11.4 us -> 1.41 us
    psum x3 -> x0, blocking collectives: 132 us -> none  [two_products(): lax.psum((jnp.sum(residual * residual), jnp.sum(residual * image)), ('gz'...]
    scatter-add x6 -> x0, other arithmetic: 115 us -> none  [the longest x3 78.6 us: links(): empty.at[:, corners.reshape(-1)]]
    gather x6 -> x0, local copies, waits for them, and re-layouts: 64.6 us -> none  [the longest x3 42.4 us: links(): interp = jnp.sum(weights[None] * following[:, corners], 1)]
    ppermute x6 -> x0, local copies, waits for them, and re-layouts: 29.5 us -> none  [passed_along(): return lax.ppermute(block, axis, route)]
    reshape x5 -> x0, local copies, waits for them, and re-layouts: 26.3 us -> none  [the longest x3 15.7 us: links(): return (own + onward).reshape(2, rows, cols)]
    ppermute x13 -> x9, starting transfers between devices: 37.5 us -> 14.6 us  [swapped(): return lax.ppermute(block, axis, route) if route else None]
    all_to_all x0 -> x1, blocking collectives: none -> 16.9 us  [body(): sums = lax.all_to_all(sums, ('gz', 'xy'), 0, 0).reshape(n_gz * n_xy, LANES)]
    scatter-add x3 -> x0, local copies, waits for them, and re-layouts: 16 us -> none  [links(): empty.at[:, corners.reshape(-1)]]
  transfers between devices with their start and end apart: 13 -> 9, of which waited for: 3 -> 4; matrix products, arithmetic and copies ran while one was open for 55% -> 0% of each run, Pallas kernels for 0% -> 0%
where the time goes in v1:
time: 56.8 us; the launch traced here: 56.4 us
  blocking collectives  16.9 us (30%)
  starting transfers between devices  14.6 us (26%)
  Pallas kernels  12 us (21%)
  waiting for transfers between devices  9.12 us (16%)
  local copies, waits for them, and re-layouts  2.34 us (4%)
  between operations  1.41 us (2%)
    all_to_all x1, blocking collectives, body(): sums = lax.all_to_all(sums, ('gz', 'xy'), 0, 0).reshape(n_gz * n_xy, LANES)  16.9 us
    ppermute x9, starting transfers between devices, swapped(): return lax.ppermute(block, axis, route) if route else None  14.6 us
    ppermute x9, waiting for transfers between devices, swapped(): return lax.ppermute(block, axis, route) if route else None  9.12 us
    pallas_call x1, Pallas kernels, body(): call(functools.partial(step_kernel, True, False, two, n_edges), [SMEM, SM...  5.28 us
    pallas_call x2, Pallas kernels, body(): call(functools.partial(step_kernel, False, last, two, n_edges), [SMEM, SM...  5.2 us
    unnamed x16, local copies, waits for them, and re-layouts  2.34 us
  transfers between devices with their start and end apart: 9, of which 4 were waited for; matrix products, arithmetic and copies ran while one was open for 0% of the time, Pallas kernels for 0%

profile of v1, /device:TPU:0, one launch (start us, length us, event | category | flops | bytes accessed | tf_op | source)
XLA Modules:
  0.0 56.4 jit_solution(3336654645223415929)
XLA Ops:
  0.6 0.0 copy-start.2
  1.3 0.1 pad_add_fusion.flags
  1.4 0.1 copy-done.2
  1.5 0.6 %copy-done.7 = s32[1,1,1024]{2,1,0:T(1,128)S(1)} copy-done((s32[1,1,1024]{2,1,0:T(1,128)S(1)}, s32[1,1,1024]{2,1,0:T(1,128)}, u32[]{:S(2)}) %copy-start.7) | copy-done | bytes 4120
  2.1 0.0 copy-done.5
  2.1 0.9 %copy-done = f32[2,1,8,2048]{3,2,1,0:T(8,128)S(1)} copy-done((f32[2,1,8,2048]{3,2,1,0:T(8,128)S(1)}, f32[2,1,8,2048]{3,2,1,0:T(8,128)}, u32[]{:S(2)}) %copy-start) | copy-done | bytes 131096
  3.0 0.7 %copy-done.6 = f32[4,1,1,1024]{3,2,1,0:T(1,128)S(1)} copy-done((f32[4,1,1,1024]{3,2,1,0:T(1,128)S(1)}, f32[4,1,1,1024]{3,2,1,0:T(1,128)}, u32[]{:S(2)}) %copy-start.6) | copy-done | bytes 16408
  3.8 0.6 %pack.1 = (f32[8,4864]{1,0:T(8,128)S(1)}, f32[4,2048]{1,0:T(4,128)S(1)}) custom-call(s32[3]{0:T(128)S(1)} %pad_add_fusion.flags, s32[1,1]{1,0:T(1,128)S(6)} %copy.15.count, f32[2,8,2048]{2,1,0:T(8,128)S(1)} %bitcast.20, f32[8,2048]{1,0:T(8,128)S(1)} %bitcast.24, s32[8,128]{1,0:T(8,128)S(1)} %bitcast.34, s32[8,128]{1,0:T(8,128)S(1)} %bitcast.41, ...), custom_call_target="tpu_custom_call" | custom-call | tf_op jit(solution)/shard_map/pack/pallas_call | solution.py:435
  4.3 0.7 %collective-permute-start.1 = (f32[8,4864]{1,0:T(8,128)S(1)}, f32[8,4864]{1,0:T(8,128)S(1)}, u32[]{:S(2)}, u32[]{:S(2)}) collective-permute-start(f32[8,4864]{1,0:T(8,128)S(1)} %get-tuple-element.20), channel_id=1, source_target_pairs={{2,4},{4,2},{6,8},{8,6},{10,12},{12,10},{14,16},{16,14},{18,20},{2... | collective-permute-start | bytes 466952 | tf_op jit(solution)/shard_map/ppermute | solution.py:25
  5.0 5.8 %collective-permute-start = (f32[8,4864]{1,0:T(8,128)S(1)}, f32[8,4864]{1,0:T(8,128)S(1)}, u32[]{:S(2)}, u32[]{:S(2)}) collective-permute-start(f32[8,4864]{1,0:T(8,128)S(1)} %get-tuple-element.20), channel_id=1, source_target_pairs={{0,2},{2,0},{4,6},{6,4},{8,10},{10,8},{12,14},{14,12},{16,18},{18,... | collective-permute-start | bytes 466952 | tf_op jit(solution)/shard_map/ppermute | solution.py:25
  10.8 0.0 collective-permute-start.2
  10.8 1.2 %collective-permute-done.2.rest_2_ = f32[4,2048]{1,0:T(4,128)S(1)} collective-permute-done((f32[4,2048]{1,0:T(4,128)S(1)}, f32[4,2048]{1,0:T(4,128)S(1)}, u32[]{:S(2)}, u32[]{:S(2)}) %collective-permute-start.2) | collective-permute-done | bytes 32800 | tf_op jit(solution)/shard_map/ppermute | solution.py:25
  12.0 0.0 collective-permute-done.1.rest_1_
  12.0 5.8 %collective-permute-done.rest_0_ = f32[8,4864]{1,0:T(8,128)S(1)} collective-permute-done((f32[8,4864]{1,0:T(8,128)S(1)}, f32[8,4864]{1,0:T(8,128)S(1)}, u32[]{:S(2)}, u32[]{:S(2)}) %collective-permute-start) | collective-permute-done | bytes 155680 | tf_op jit(solution)/shard_map/ppermute | solution.py:25
  17.7 0.0 copy-done.3
  17.8 5.3 %first.1 = (f32[2,8,2048]{2,1,0:T(8,128)S(1)}, f32[2,2,8,128]{3,2,1,0:T(8,128)S(1)}, f32[2,8,128]{2,1,0:T(8,128)S(1)}, f32[2,8,128]{2,1,0:T(8,128)S(1)}, f32[2,2...) custom-call(s32[3]{0:T(128)S(1)} %pad_add_fusion.flags, s32[1,1]{1,0:T(1,128)S(6)} %copy.15.count, ...), custom_call_target="tpu_custom_call" | custom-call | tf_op jit(solution)/shard_map/first/pallas_call | solution.py:453
  23.0 0.1 collective-permute-start.5
  23.1 1.9 %collective-permute-start.3 = (f32[2,8,128]{2,1,0:T(8,128)S(1)}, f32[2,8,128]{2,1,0:T(8,128)S(1)}, u32[]{:S(2)}, u32[]{:S(2)}) collective-permute-start(f32[2,8,128]{2,1,0:T(8,128)S(1)} %get-tuple-element.25), channel_id=1, source_target_pairs={{0,2},{2,0},{4,6},{6,4},{8,10},{10,8},{12,14},{14,12},{16,18},{18,... | collective-permute-start | bytes 24584 | tf_op jit(solution)/shard_map/ppermute | solution.py:25
  25.0 0.6 %collective-permute-start.4 = (f32[2,8,128]{2,1,0:T(8,128)S(1)}, f32[2,8,128]{2,1,0:T(8,128)S(1)}, u32[]{:S(2)}, u32[]{:S(2)}) collective-permute-start(f32[2,8,128]{2,1,0:T(8,128)S(1)} %get-tuple-element.26), channel_id=1, source_target_pairs={{2,4},{4,2},{6,8},{8,6},{10,12},{12,10},{14,16},{16,14},{18,20},{2... | collective-permute-start | bytes 24584 | tf_op jit(solution)/shard_map/ppermute | solution.py:25
  25.7 1.2 %collective-permute-done.3.rest_0_ = f32[2,8,128]{2,1,0:T(8,128)S(1)} collective-permute-done((f32[2,8,128]{2,1,0:T(8,128)S(1)}, f32[2,8,128]{2,1,0:T(8,128)S(1)}, u32[]{:S(2)}, u32[]{:S(2)}) %collective-permute-start.3) | collective-permute-done | bytes 8224 | tf_op jit(solution)/shard_map/ppermute | solution.py:25
  26.8 0.0 collective-permute-done.4.rest_1_
  26.8 0.0 collective-permute-done.5.rest_2_
  26.8 3.2 %step.1 = (f32[2,8,2048]{2,1,0:T(8,128)S(1)}, f32[2,2,8,128]{3,2,1,0:T(8,128)S(1)}, f32[2,8,128]{2,1,0:T(8,128)S(1)}, f32[2,8,128]{2,1,0:T(8,128)S(1)}, f32[2,2048]{1,0:T(2,128)S(1)}) custom-call(s32[3]{0:T(128)S(1)} %pad_add_fusion.flags, s32[1,1]{1,0:T(1,128)S(6)} %copy.15.count, f32[2,8,2048]{2,1,0:T(8,128)S(1)} %get-tuple-element.22.field_ref.rest_5_.refs_1_, ...), custom_call_target="tpu_custom_call" | custom-call | tf_op jit(solution)/shard_map/step/pallas_call | solution.py:470
  30.1 0.1 collective-permute-start.8
  30.1 4.9 %collective-permute-start.6 = (f32[2,8,128]{2,1,0:T(8,128)S(1)}, f32[2,8,128]{2,1,0:T(8,128)S(1)}, u32[]{:S(2)}, u32[]{:S(2)}) collective-permute-start(f32[2,8,128]{2,1,0:T(8,128)S(1)} %get-tuple-element.31), channel_id=1, source_target_pairs={{0,2},{2,0},{4,6},{6,4},{8,10},{10,8},{12,14},{14,12},{16,18},{18,... | collective-permute-start | bytes 24584 | tf_op jit(solution)/shard_map/ppermute | solution.py:25
  35.0 0.6 %collective-permute-start.7 = (f32[2,8,128]{2,1,0:T(8,128)S(1)}, f32[2,8,128]{2,1,0:T(8,128)S(1)}, u32[]{:S(2)}, u32[]{:S(2)}) collective-permute-start(f32[2,8,128]{2,1,0:T(8,128)S(1)} %get-tuple-element.32), channel_id=1, source_target_pairs={{2,4},{4,2},{6,8},{8,6},{10,12},{12,10},{14,16},{16,14},{18,20},{2... | collective-permute-start | bytes 24584 | tf_op jit(solution)/shard_map/ppermute | solution.py:25
  35.7 1.0 %collective-permute-done.6.rest_0_ = f32[2,8,128]{2,1,0:T(8,128)S(1)} collective-permute-done((f32[2,8,128]{2,1,0:T(8,128)S(1)}, f32[2,8,128]{2,1,0:T(8,128)S(1)}, u32[]{:S(2)}, u32[]{:S(2)}) %collective-permute-start.6) | collective-permute-done | bytes 8224 | tf_op jit(solution)/shard_map/ppermute | solution.py:25
  36.6 0.0 collective-permute-done.7.rest_1_
  36.6 0.0 collective-permute-done.8.rest_2_
  36.6 2.0 %last.1 = (f32[2,8,2048]{2,1,0:T(8,128)S(1)}, f32[32,128]{1,0:T(8,128)S(1)}) custom-call(s32[3]{0:T(128)S(1)} %pad_add_fusion.flags, s32[1,1]{1,0:T(1,128)S(6)} %copy.15.count, f32[2,8,2048]{2,1,0:T(8,128)S(1)} %get-tuple-element.29.field_ref.refs_2_, f32[8,2048]{1,0:T(8,128)S(1)} %bitcast.30, f32[8,2048]{1,0:T(8,128)S(1)} %bitcast.27, ...), custom_call_target="tpu_custom_call" | custom-call | tf_op jit(solution)/shard_map/last/pallas_call | solution.py:470
  38.6 16.9 %all_to_all.5 = f32[32,1,128]{2,1,0:T(1,128)S(1)} all-to-all(f32[32,1,128]{2,1,0:T(1,128)S(1)} %bitcast.43), channel_id=1, replica_groups=mesh['gz'=16,'xy'=2] {'gz','xy'}, dimensions={0} | all-to-all | bytes 32768 | tf_op jit(solution)/shard_map/all_to_all | solution.py:480
  55.5 0.9 %finish.1 = (f32[2,8,2048]{2,1,0:T(8,128)}, f32[2,8,2048]{2,1,0:T(8,128)}) custom-call(f32[32,128]{1,0:T(8,128)S(1)} %bitcast.40, f32[2,8,2048]{2,1,0:T(8,128)S(1)} %bitcast.23, f32[2,8,2048]{2,1,0:T(8,128)S(1)} %get-tuple-element.22.field_ref.rest_5_.refs_1_, f32[2,8,2048]{2,1,0:T(8,128)S(1)} %get-tuple-element.29.field_ref.refs_2_, ...), custom_call_target="tpu_custom_call" | custom-call | tf_op jit(solution)/shard_map/finish/pallas_call | solution.py:481
  (9 shorter events, 0.0 us)
Async XLA Ops:
  0.6 0.8 %copy-start.2 = (f32[1,8,2048]{2,1,0:T(8,128)S(1)}, f32[1,8,2048]{2,1,0:T(8,128)}, u32[]{:S(2)}) copy-start(f32[1,8,2048]{2,1,0:T(8,128)} %param.10) | copy-start | bytes 196612
  1.4 0.7 %copy-start.7 = (s32[1,1,1024]{2,1,0:T(1,128)S(1)}, s32[1,1,1024]{2,1,0:T(1,128)}, u32[]{:S(2)}) copy-start(s32[1,1,1024]{2,1,0:T(1,128)} %param.13) | copy-start | bytes 12292
  1.4 0.7 %copy-start.5 = (s32[1,1,1024]{2,1,0:T(1,128)S(1)}, s32[1,1,1024]{2,1,0:T(1,128)}, u32[]{:S(2)}) copy-start(s32[1,1,1024]{2,1,0:T(1,128)} %param.12) | copy-start | bytes 12292
  2.1 0.9 %copy-start = (f32[2,1,8,2048]{3,2,1,0:T(8,128)S(1)}, f32[2,1,8,2048]{3,2,1,0:T(8,128)}, u32[]{:S(2)}) copy-start(f32[2,1,8,2048]{3,2,1,0:T(8,128)} %param.8) | copy-start | bytes 393220
  3.0 0.7 %copy-start.6 = (f32[4,1,1,1024]{3,2,1,0:T(1,128)S(1)}, f32[4,1,1,1024]{3,2,1,0:T(1,128)}, u32[]{:S(2)}) copy-start(f32[4,1,1,1024]{3,2,1,0:T(1,128)} %param.14) | copy-start | bytes 49156
  3.7 14.0 %copy-start.3 = (f32[1,8,2048]{2,1,0:T(8,128)S(1)}, f32[1,8,2048]{2,1,0:T(8,128)}, u32[]{:S(2)}) copy-start(f32[1,8,2048]{2,1,0:T(8,128)} %param.9) | copy-start | bytes 196612
  3.7 14.0 %copy-start.4 = (f32[1,8,2048]{2,1,0:T(8,128)S(1)}, f32[1,8,2048]{2,1,0:T(8,128)}, u32[]{:S(2)}) copy-start(f32[1,8,2048]{2,1,0:T(8,128)} %param.11) | copy-start | bytes 196612
  4.3 7.7 %collective-permute-start.1 = (f32[8,4864]{1,0:T(8,128)S(1)}, f32[8,4864]{1,0:T(8,128)S(1)}, u32[]{:S(2)}, u32[]{:S(2)}) collective-permute-start(f32[8,4864]{1,0:T(8,128)S(1)} %get-tuple-element.20), channel_id=1, source_target_pairs={{2,4},{4,2},{6,8},{8,6},{10,12},{12,10},{14,16},{16,14},{18,20},{2... | collective-permute-start | bytes 466952 | tf_op jit(solution)/shard_map/ppermute | solution.py:25
  5.0 12.7 %collective-permute-start = (f32[8,4864]{1,0:T(8,128)S(1)}, f32[8,4864]{1,0:T(8,128)S(1)}, u32[]{:S(2)}, u32[]{:S(2)}) collective-permute-start(f32[8,4864]{1,0:T(8,128)S(1)} %get-tuple-element.20), channel_id=1, source_target_pairs={{0,2},{2,0},{4,6},{6,4},{8,10},{10,8},{12,14},{14,12},{16,18},{18,... | collective-permute-start | bytes 466952 | tf_op jit(solution)/shard_map/ppermute | solution.py:25
  10.8 1.2 %collective-permute-start.2 = (f32[4,2048]{1,0:T(4,128)S(1)}, f32[4,2048]{1,0:T(4,128)S(1)}, u32[]{:S(2)}, u32[]{:S(2)}) collective-permute-start(f32[4,2048]{1,0:T(4,128)S(1)} %get-tuple-element.21), channel_id=1, source_target_pairs={{0,1},{1,0},{2,3},{3,2},{4,5},{5,4},{6,7},{7,6},{8,9},{9,8},{10,11... | collective-permute-start | bytes 98312 | tf_op jit(solution)/shard_map/ppermute | solution.py:25
  23.0 3.8 %collective-permute-start.5 = (f32[2,2048]{1,0:T(2,128)S(1)}, f32[2,2048]{1,0:T(2,128)S(1)}, u32[]{:S(2)}, u32[]{:S(2)}) collective-permute-start(f32[2,2048]{1,0:T(2,128)S(1)} %get-tuple-element.27), channel_id=1, source_target_pairs={{0,1},{1,0},{2,3},{3,2},{4,5},{5,4},{6,7},{7,6},{8,9},{9,8},{10,11... | collective-permute-start | bytes 49160 | tf_op jit(solution)/shard_map/ppermute | solution.py:25
  23.1 3.7 %collective-permute-start.3 = (f32[2,8,128]{2,1,0:T(8,128)S(1)}, f32[2,8,128]{2,1,0:T(8,128)S(1)}, u32[]{:S(2)}, u32[]{:S(2)}) collective-permute-start(f32[2,8,128]{2,1,0:T(8,128)S(1)} %get-tuple-element.25), channel_id=1, source_target_pairs={{0,2},{2,0},{4,6},{6,4},{8,10},{10,8},{12,14},{14,12},{16,18},{18,... | collective-permute-start | bytes 24584 | tf_op jit(solution)/shard_map/ppermute | solution.py:25
  25.0 1.8 %collective-permute-start.4 = (f32[2,8,128]{2,1,0:T(8,128)S(1)}, f32[2,8,128]{2,1,0:T(8,128)S(1)}, u32[]{:S(2)}, u32[]{:S(2)}) collective-permute-start(f32[2,8,128]{2,1,0:T(8,128)S(1)} %get-tuple-element.26), channel_id=1, source_target_pairs={{2,4},{4,2},{6,8},{8,6},{10,12},{12,10},{14,16},{16,14},{18,20},{2... | collective-permute-start | bytes 24584 | tf_op jit(solution)/shard_map/ppermute | solution.py:25
  26.8 9.8 %copy-start.1 = (f32[2,1,8,2048]{3,2,1,0:T(8,128)S(1)}, f32[2,1,8,2048]{3,2,1,0:T(8,128)}, u32[]{:S(2)}) copy-start(f32[2,1,8,2048]{3,2,1,0:T(8,128)} %param.8) | copy-start | bytes 393220
  30.1 6.6 %collective-permute-start.8 = (f32[2,2048]{1,0:T(2,128)S(1)}, f32[2,2048]{1,0:T(2,128)S(1)}, u32[]{:S(2)}, u32[]{:S(2)}) collective-permute-start(f32[2,2048]{1,0:T(2,128)S(1)} %get-tuple-element.33), channel_id=1, source_target_pairs={{0,1},{1,0},{2,3},{3,2},{4,5},{5,4},{6,7},{7,6},{8,9},{9,8},{10,11... | collective-permute-start | bytes 49160 | tf_op jit(solution)/shard_map/ppermute | solution.py:25
  30.1 6.5 %collective-permute-start.6 = (f32[2,8,128]{2,1,0:T(8,128)S(1)}, f32[2,8,128]{2,1,0:T(8,128)S(1)}, u32[]{:S(2)}, u32[]{:S(2)}) collective-permute-start(f32[2,8,128]{2,1,0:T(8,128)S(1)} %get-tuple-element.31), channel_id=1, source_target_pairs={{0,2},{2,0},{4,6},{6,4},{8,10},{10,8},{12,14},{14,12},{16,18},{18,... | collective-permute-start | bytes 24584 | tf_op jit(solution)/shard_map/ppermute | solution.py:25
  35.0 1.6 %collective-permute-start.7 = (f32[2,8,128]{2,1,0:T(8,128)S(1)}, f32[2,8,128]{2,1,0:T(8,128)S(1)}, u32[]{:S(2)}, u32[]{:S(2)}) collective-permute-start(f32[2,8,128]{2,1,0:T(8,128)S(1)} %get-tuple-element.32), channel_id=1, source_target_pairs={{2,4},{4,2},{6,8},{8,6},{10,12},{12,10},{14,16},{16,14},{18,20},{2... | collective-permute-start | bytes 24584 | tf_op jit(solution)/shard_map/ppermute | solution.py:25

commit v2 on v1

--- a/solution.py
+++ b/solution.py
@@ -6,6 +6,7 @@
 from jax.experimental import pallas as pl
 from jax.experimental.pallas import tpu as pltpu
 from jax.sharding import PartitionSpec as P
+
 
 BLOCK = 128
 ITERS = 3
@@ -14,7 +15,6 @@
 SHIFT = 1.25
 F32 = jnp.float32
 BF16 = jnp.bfloat16
-CHUNK = 256
 
 
 def swapped(block, axis, first):
@@ -23,6 +23,20 @@
     for i in range(first, count - 1, 2):
         route += [(i, i + 1), (i + 1, i)]
     return lax.ppermute(block, axis, route) if route else None
+
+
+def swapped_sections(block, first):
+    count, width = lax.axis_size("gz"), lax.axis_size("xy")
+    route = []
+    for i in range(first, count - 1, 2):
+        for j in range(width):
+            a, b = i * width + j, (i + 1) * width + j
+            route += [(a, b), (b, a)]
+    paired = {a for a, _ in route}
+    for a in range(0, count * width - 1, 2):
+        if a not in paired and a + 1 not in paired and a // width == (a + 1) // width:
+            route += [(a, a + 1), (a + 1, a)]
+    return lax.ppermute(block, ("gz", "xy"), route)
 
 
 def split2(x):
@@ -198,22 +212,29 @@
     return out
 
 
-def pack_kernel(two, flags, count, field, down, source, target, weights, pack, *edges):
+def pack_kernel(two, flags, count, field, down, source, target, weights, *refs):
     rows, cols = down.shape
     even_b = flags[1] == 0
     has_next = flags[2]
     nb = source.shape[0]
+    n_edges = 2 if two else 1
+    pack, edges, (last_down, ids, held, sems) = refs[0], refs[1 : 1 + n_edges], refs[1 + n_edges :]
+    pairs = [(field.at[c], pack.at[:, c * cols : (c + 1) * cols]) for c in range(2)]
+    pairs += [(down, last_down), (source, ids.at[0]), (target, ids.at[1]), (weights, held)]
+    copies = [pltpu.make_async_copy(a, b, sems.at[i]) for i, (a, b) in enumerate(pairs)]
+    for copy in copies:
+        copy.start()
+    for copy in copies:
+        copy.wait()
     block = lax.broadcasted_iota(jnp.int32, (nb, LANES), 0)
     live = jnp.where(block * LANES < count[0, 0] * BLOCK * has_next, 1.0, 0.0)
-    for c in range(2):
-        pack[:, c * cols : (c + 1) * cols] = field[c]
-    parts = [source[...].astype(F32), target[...].astype(F32)] + [weights[q] * live for q in range(4)]
+    parts = [ids[0].astype(F32), ids[1].astype(F32)] + [held[q] * live for q in range(4)]
     for i, part in enumerate(parts):
         pack[:nb, 2 * cols + i * LANES : 2 * cols + (i + 1) * LANES] = part
-    messages = edges_of(lambda c, r: field[c, r : r + 1, :], rows, even_b, two)
+    messages = edges_of(lambda c, r: pack[r : r + 1, c * cols : (c + 1) * cols], rows, even_b, two)
     for message, edge in zip(messages, edges):
         edge[0:2, :] = message
-        edge[2:3, :] = down[rows - 1 : rows, :]
+        edge[2:3, :] = last_down[rows - 1 : rows, :]
 
 
 def halves(flags, edge_refs):
@@ -265,6 +286,7 @@
         rim = above[2:3, :]
         slot = lambda ref, i: ref[:nb, 2 * cols + i * LANES : 2 * cols + (i + 1) * LANES]
         prev_parts = [pick(even, slot(got1, i), slot(got0, i)) for i in range(6)]
+        prev_parts[2:] = [jnp.where(flags[3] > 0, w, 0.0) for w in prev_parts[2:]]
         prev_target = prev_parts[1].astype(jnp.int32)
         prev_weights = prev_parts[2:]
         prev_hi, prev_lo = hi_lo(prev_target, rows, cols)
@@ -394,16 +416,17 @@
 
 VMEM = pl.BlockSpec(memory_space=pltpu.VMEM)
 SMEM = pl.BlockSpec(memory_space=pltpu.SMEM)
-
-
-def call(kernel, in_specs, shapes, name):
+HBM = pl.BlockSpec(memory_space=pltpu.HBM)
+
+
+def call(kernel, in_specs, shapes, scratch=()):
     shapes = [jax.ShapeDtypeStruct(s, F32) for s in shapes]
     return pl.pallas_call(
         kernel,
         in_specs=in_specs,
         out_specs=[VMEM] * len(shapes),
         out_shape=shapes,
-        name=name,
+        scratch_shapes=list(scratch),
         compiler_params=pltpu.CompilerParams(vmem_limit_bytes=48 * 1024 * 1024),
     )
 
@@ -429,20 +452,28 @@
     n_gz, n_xy = lax.axis_size("gz"), lax.axis_size("xy")
     at_gz, at_xy = lax.axis_index("gz"), lax.axis_index("xy")
     two = n_xy > 2
-    flags = jnp.stack([at_gz % 2, at_xy % 2, (at_gz < n_gz - 1).astype(jnp.int32)]).astype(jnp.int32)
+    flags = jnp.stack([at_gz % 2, at_xy % 2, (at_gz < n_gz - 1).astype(jnp.int32), (at_gz > 0).astype(jnp.int32)]).astype(jnp.int32)
     n_edges = 2 if two else 1
 
     pack, *edges = call(
         functools.partial(pack_kernel, two),
-        [SMEM, SMEM] + [VMEM] * 5,
+        [SMEM, SMEM] + [HBM] * 5,
         [(rows, 2 * cols + 6 * LANES)] + [(4, cols)] * n_edges,
-        "pack",
-    )(flags, block_count, rhs, down, source, target, weights)
+        [
+            pltpu.VMEM((rows, cols), F32),
+            pltpu.VMEM((2, nb, LANES), jnp.int32),
+            pltpu.VMEM((4, nb, LANES), F32),
+            pltpu.SemaphoreType.DMA((6,)),
+        ],
+    )(flags, block_count, *(pltpu.with_memory_space_constraint(a, pltpu.HBM) for a in (rhs, down, source, target, weights)))
 
     def exchange(to0, to1, edges):
-        got1 = swapped(to1, "gz", 1)
-        got0 = swapped(to0, "gz", 0)
-        return got0, got1, [swapped(e, "xy", i) for i, e in enumerate(edges)]
+        got1 = swapped_sections(to1, 1)
+        got0 = swapped_sections(to0, 0)
+        got_edges = []
+        for i, edge in enumerate(edges):
+            got_edges.append(swapped(edge, "xy", i))
+        return got0, got1, got_edges
 
     field_shape = (2, rows, cols)
     message = (2, nb, LANES)
@@ -454,7 +485,6 @@
         functools.partial(step_kernel, True, False, two, n_edges),
         [SMEM, SMEM] + [VMEM] * (9 + n_edges),
         common + [(5, nb, LANES), (1, cols)],
-        "first",
     )(flags, block_count, rhs, across, down, hold, source, weights, target, got0, got1, *got_edges)
     edges, (prev, rim) = tail[:n_edges], tail[n_edges:]
 
@@ -471,7 +501,6 @@
             functools.partial(step_kernel, False, last, two, n_edges),
             [SMEM, SMEM] + [VMEM] * (len(args) - 2),
             shapes,
-            "last" if last else "step",
         )(*args)
         if not last:
             local, to0, to1, *edges = tail
@@ -479,7 +508,7 @@
     sums = tail[0].reshape(n_gz * n_xy, 1, LANES)
     sums = lax.all_to_all(sums, ("gz", "xy"), 0, 0).reshape(n_gz * n_xy, LANES)
     solution_field, residual = call(
-        finish_kernel, [VMEM] * (1 + len(basis)), [field_shape] * 2, "finish"
+        finish_kernel, [VMEM] * (1 + len(basis)), [field_shape] * 2
     )(sums, *basis)
     return solution_field[:, None], residual[:, None]
 

time: 56.8 us -> 50.6 us (0.89)
  starting transfers between devices: 14.6 us -> 9.78 us
  blocking collectives: 16.9 us -> 15 us
  local copies, waits for them, and re-layouts: 2.34 us -> 0.87 us
  waiting for transfers between devices: 9.12 us -> 10.3 us
  Pallas kernels: 12 us -> 12.9 us
    ppermute x9 -> x3, starting transfers between devices: 14.6 us -> 0.14 us  [swapped(): return lax.ppermute(block, axis, route) if route else None]
    ppermute x0 -> x6, starting transfers between devices: none -> 9.63 us  [swapped_sections(): return lax.ppermute(block, ('gz', 'xy'), route)]
    ppermute x0 -> x6, waiting for transfers between devices: none -> 9.09 us  [swapped_sections(): return lax.ppermute(block, ('gz', 'xy'), route)]
    ppermute x9 -> x3, waiting for transfers between devices: 9.12 us -> 1.21 us  [swapped(): return lax.ppermute(block, axis, route) if route else None]
    all_to_all x1, blocking collectives: 16.9 us -> 15 us  [body(): sums = lax.all_to_all(sums, ('gz', 'xy'), 0, 0).reshape(n_gz * n_xy, LANES)]
    unnamed x16 -> x14, local copies, waits for them, and re-layouts: 2.34 us -> 0.87 us
    pallas_call x2, Pallas kernels: 1.48 us -> 2.43 us  [the longest x1 1.52 us: body(): call(functools.partial(pack_kernel, two), [SMEM, SMEM] + [HBM] * 5, [(row...]
where the time goes in v2:
time: 50.6 us; the launch traced here: 50.4 us
  blocking collectives  15 us (30%)
  Pallas kernels  12.9 us (25%)
  waiting for transfers between devices  10.3 us (20%)
  starting transfers between devices  9.78 us (19%)
  between operations  1.45 us (3%)
  local copies, waits for them, and re-layouts  0.87 us (2%)
    all_to_all x1, blocking collectives, body(): sums = lax.all_to_all(sums, ('gz', 'xy'), 0, 0).reshape(n_gz * n_xy, LANES)  15 us
    ppermute x6, starting transfers between devices, swapped_sections(): return lax.ppermute(block, ('gz', 'xy'), route)  9.63 us
    ppermute x6, waiting for transfers between devices, swapped_sections(): return lax.ppermute(block, ('gz', 'xy'), route)  9.09 us
    pallas_call x1, Pallas kernels, body(): call(functools.partial(step_kernel, True, False, two, n_edges), [SMEM, SM...  5.27 us
    pallas_call x2, Pallas kernels, body(): call(functools.partial(step_kernel, False, last, two, n_edges), [SMEM, SM...  5.21 us
    pallas_call x1, Pallas kernels, body(): call(functools.partial(pack_kernel, two), [SMEM, SMEM] + [HBM] * 5, [(row...  1.52 us
    ppermute x3, waiting for transfers between devices, swapped(): return lax.ppermute(block, axis, route) if route else None  1.21 us
  transfers between devices with their start and end apart: 9, of which 4 were waited for; matrix products, arithmetic and copies ran while one was open for 0% of the time, Pallas kernels for 0%

profile of v2, /device:TPU:0, one launch (start us, length us, event | category | flops | bytes accessed | tf_op | source)
XLA Modules:
  0.0 50.4 jit_solution(8323956253073779119)
XLA Ops:
  0.6 0.0 copy-start.6
  0.7 0.0 copy-start.5
  0.7 0.0 copy-start.4
  0.7 0.0 copy-start
  1.4 0.1 pad_add_fusion.flags
  1.5 1.5 %shard_map.95 = (f32[8,4864]{1,0:T(8,128)S(1)}, f32[4,2048]{1,0:T(4,128)S(1)}) custom-call(s32[4]{0:T(128)S(1)} %pad_add_fusion.flags, s32[1,1]{1,0:T(1,128)S(6)} %copy.15.count, f32[2,8,2048]{2,1,0:T(8,128)} %bitcast.21, f32[8,2048]{1,0:T(8,128)} %bitcast.25, s32[8,128]{1,0:T(8,128)} %bitcast.35, s32[8,128]{1,0:T(8,128)} %bitcast.42, f32[4,8,128]{2,1,0:T(8,128)} %bitcast.39), custom_call_target="tpu_custom_call" | custom-call | tf_op jit(solution)/shard_map/pallas_call | solution.py:458
  3.0 0.6 %collective-permute-start.1 = (f32[8,4864]{1,0:T(8,128)S(1)}, f32[8,4864]{1,0:T(8,128)S(1)}, u32[]{:S(2)}, u32[]{:S(2)}) collective-permute-start(f32[8,4864]{1,0:T(8,128)S(1)} %get-tuple-element.20), channel_id=1, source_target_pairs={{2,4},{4,2},{3,5},{5,3},{6,8},{8,6},{7,9},{9,7},{10,12},{12,10},{1... | collective-permute-start | bytes 466952 | tf_op jit(solution)/shard_map/ppermute | solution.py:39
  3.6 4.0 %collective-permute-start = (f32[8,4864]{1,0:T(8,128)S(1)}, f32[8,4864]{1,0:T(8,128)S(1)}, u32[]{:S(2)}, u32[]{:S(2)}) collective-permute-start(f32[8,4864]{1,0:T(8,128)S(1)} %get-tuple-element.20), channel_id=1, source_target_pairs={{0,2},{2,0},{1,3},{3,1},{4,6},{6,4},{5,7},{7,5},{8,10},{10,8},{9,1... | collective-permute-start | bytes 466952 | tf_op jit(solution)/shard_map/ppermute | solution.py:39
  7.5 0.0 collective-permute-start.2
  7.5 1.2 %collective-permute-done.2.rest_2_ = f32[4,2048]{1,0:T(4,128)S(1)} collective-permute-done((f32[4,2048]{1,0:T(4,128)S(1)}, f32[4,2048]{1,0:T(4,128)S(1)}, u32[]{:S(2)}, u32[]{:S(2)}) %collective-permute-start.2) | collective-permute-done | bytes 32800 | tf_op jit(solution)/shard_map/ppermute | solution.py:25
  8.7 0.0 collective-permute-done.1.rest_1_
  8.7 5.9 %collective-permute-done.rest_0_ = f32[8,4864]{1,0:T(8,128)S(1)} collective-permute-done((f32[8,4864]{1,0:T(8,128)S(1)}, f32[8,4864]{1,0:T(8,128)S(1)}, u32[]{:S(2)}, u32[]{:S(2)}) %collective-permute-start) | collective-permute-done | bytes 155680 | tf_op jit(solution)/shard_map/ppermute | solution.py:39
  14.6 0.0 copy-done.4
  14.6 0.0 copy-start.3
  14.7 0.8 %copy-done.3 = f32[1,8,2048]{2,1,0:T(8,128)S(1)} copy-done((f32[1,8,2048]{2,1,0:T(8,128)S(1)}, f32[1,8,2048]{2,1,0:T(8,128)}, u32[]{:S(2)}) %copy-start.3) | copy-done | bytes 65560
  15.5 5.3 %shard_map.96 = (f32[2,8,2048]{2,1,0:T(8,128)S(1)}, f32[2,2,8,128]{3,2,1,0:T(8,128)S(1)}, f32[2,8,128]{2,1,0:T(8,128)S(1)}, f32[2,8,128]{2,1,0:T(8,128)S(1)}, f3...) custom-call(s32[4]{0:T(128)S(1)} %pad_add_fusion.flags, s32[1,1]{1,0:T(1,128)S(6)} %copy.15.count, ...), custom_call_target="tpu_custom_call" | custom-call | tf_op jit(solution)/shard_map/pallas_call | solution.py:484
  20.8 0.1 collective-permute-start.5
  20.8 1.8 %collective-permute-start.3 = (f32[2,8,128]{2,1,0:T(8,128)S(1)}, f32[2,8,128]{2,1,0:T(8,128)S(1)}, u32[]{:S(2)}, u32[]{:S(2)}) collective-permute-start(f32[2,8,128]{2,1,0:T(8,128)S(1)} %get-tuple-element.25), channel_id=1, source_target_pairs={{0,2},{2,0},{1,3},{3,1},{4,6},{6,4},{5,7},{7,5},{8,10},{10,8},{9,1... | collective-permute-start | bytes 24584 | tf_op jit(solution)/shard_map/ppermute | solution.py:39
  22.7 0.2 collective-permute-start.4
  22.8 1.7 %collective-permute-done.3.rest_0_ = f32[2,8,128]{2,1,0:T(8,128)S(1)} collective-permute-done((f32[2,8,128]{2,1,0:T(8,128)S(1)}, f32[2,8,128]{2,1,0:T(8,128)S(1)}, u32[]{:S(2)}, u32[]{:S(2)}) %collective-permute-start.3) | collective-permute-done | bytes 8224 | tf_op jit(solution)/shard_map/ppermute | solution.py:39
  24.5 0.0 collective-permute-done.4.rest_1_
  24.6 0.0 collective-permute-done.5.rest_2_
  24.6 3.2 %shard_map.97 = (f32[2,8,2048]{2,1,0:T(8,128)S(1)}, f32[2,2,8,128]{3,2,1,0:T(8,128)S(1)}, f32[2,8,128]{2,1,0:T(8,128)S(1)}, f32[2,8,128]{2,1,0:T(8,128)S(1)}, f32[2,2048]{1,0:T(2,128)S(1)}) custom-call(s32[4]{0:T(128)S(1)} %pad_add_fusion.flags, s32[1,1]{1,0:T(1,128)S(6)} %copy.15.count, f32[2,8,2048]{2,1,0:T(8,128)S(1)} %get-tuple-element.22.field_ref.rest_5_.refs_1_, ...), custom_call_target="tpu_custom_call" | custom-call | tf_op jit(solution)/shard_map/pallas_call | solution.py:500
  27.8 0.1 collective-permute-start.8
  27.9 3.0 %collective-permute-start.6 = (f32[2,8,128]{2,1,0:T(8,128)S(1)}, f32[2,8,128]{2,1,0:T(8,128)S(1)}, u32[]{:S(2)}, u32[]{:S(2)}) collective-permute-start(f32[2,8,128]{2,1,0:T(8,128)S(1)} %get-tuple-element.31), channel_id=1, source_target_pairs={{0,2},{2,0},{1,3},{3,1},{4,6},{6,4},{5,7},{7,5},{8,10},{10,8},{9,1... | collective-permute-start | bytes 24584 | tf_op jit(solution)/shard_map/ppermute | solution.py:39
  30.8 0.2 collective-permute-start.7
  31.0 1.5 %collective-permute-done.6.rest_0_ = f32[2,8,128]{2,1,0:T(8,128)S(1)} collective-permute-done((f32[2,8,128]{2,1,0:T(8,128)S(1)}, f32[2,8,128]{2,1,0:T(8,128)S(1)}, u32[]{:S(2)}, u32[]{:S(2)}) %collective-permute-start.6) | collective-permute-done | bytes 8224 | tf_op jit(solution)/shard_map/ppermute | solution.py:39
  32.5 0.0 collective-permute-done.7.rest_1_
  32.5 0.0 collective-permute-done.8.rest_2_
  32.5 2.0 %shard_map.98 = (f32[2,8,2048]{2,1,0:T(8,128)S(1)}, f32[32,128]{1,0:T(8,128)S(1)}) custom-call(s32[4]{0:T(128)S(1)} %pad_add_fusion.flags, s32[1,1]{1,0:T(1,128)S(6)} %copy.15.count, f32[2,8,2048]{2,1,0:T(8,128)S(1)} %get-tuple-element.29.field_ref.refs_2_, f32[8,2048]{1,0:T(8,128)S(1)} %bitcast.31, f32[8,2048]{1,0:T(8,128)S(1)} %bitcast.28, ...), custom_call_target="tpu_custom_call" | custom-call | tf_op jit(solution)/shard_map/pallas_call | solution.py:500
  34.5 15.0 %all_to_all.5 = f32[32,1,128]{2,1,0:T(1,128)S(1)} all-to-all(f32[32,1,128]{2,1,0:T(1,128)S(1)} %bitcast.44), channel_id=1, replica_groups=mesh['gz'=16,'xy'=2] {'gz','xy'}, dimensions={0} | all-to-all | bytes 32768 | tf_op jit(solution)/shard_map/all_to_all | solution.py:509
  49.5 0.9 %shard_map.99 = (f32[2,8,2048]{2,1,0:T(8,128)}, f32[2,8,2048]{2,1,0:T(8,128)}) custom-call(f32[32,128]{1,0:T(8,128)S(1)} %bitcast.41, f32[2,8,2048]{2,1,0:T(8,128)S(1)} %bitcast.24, f32[2,8,2048]{2,1,0:T(8,128)S(1)} %get-tuple-element.22.field_ref.rest_5_.refs_1_, f32[2,8,2048]{2,1,0:T(8,128)S(1)} %get-tuple-element.29.field_ref.refs_2_, ...), custom_call_target="tpu_custom_call" | custom-call | tf_op jit(solution)/shard_map/pallas_call | solution.py:510
  (7 shorter events, 0.0 us)
Async XLA Ops:
  0.6 14.0 %copy-start.6 = (s32[1,1,1024]{2,1,0:T(1,128)S(1)}, s32[1,1,1024]{2,1,0:T(1,128)}, u32[]{:S(2)}) copy-start(s32[1,1,1024]{2,1,0:T(1,128)} %param.13) | copy-start | bytes 12292
  0.7 14.0 %copy-start.5 = (f32[4,1,1,1024]{3,2,1,0:T(1,128)S(1)}, f32[4,1,1,1024]{3,2,1,0:T(1,128)}, u32[]{:S(2)}) copy-start(f32[4,1,1,1024]{3,2,1,0:T(1,128)} %param.14) | copy-start | bytes 49156
  0.7 13.9 %copy-start.4 = (s32[1,1,1024]{2,1,0:T(1,128)S(1)}, s32[1,1,1024]{2,1,0:T(1,128)}, u32[]{:S(2)}) copy-start(s32[1,1,1024]{2,1,0:T(1,128)} %param.12) | copy-start | bytes 12292
  0.7 13.9 %copy-start.2 = (f32[1,8,2048]{2,1,0:T(8,128)S(1)}, f32[1,8,2048]{2,1,0:T(8,128)}, u32[]{:S(2)}) copy-start(f32[1,8,2048]{2,1,0:T(8,128)} %param.9) | copy-start | bytes 196612
  0.7 13.9 %copy-start = (f32[2,1,8,2048]{3,2,1,0:T(8,128)S(1)}, f32[2,1,8,2048]{3,2,1,0:T(8,128)}, u32[]{:S(2)}) copy-start(f32[2,1,8,2048]{3,2,1,0:T(8,128)} %param.8) | copy-start | bytes 393220
  1.5 13.2 %copy-start.1 = (f32[1,8,2048]{2,1,0:T(8,128)S(1)}, f32[1,8,2048]{2,1,0:T(8,128)}, u32[]{:S(2)}) copy-start(f32[1,8,2048]{2,1,0:T(8,128)} %param.10) | copy-start | bytes 196612
  3.0 5.7 %collective-permute-start.1 = (f32[8,4864]{1,0:T(8,128)S(1)}, f32[8,4864]{1,0:T(8,128)S(1)}, u32[]{:S(2)}, u32[]{:S(2)}) collective-permute-start(f32[8,4864]{1,0:T(8,128)S(1)} %get-tuple-element.20), channel_id=1, source_target_pairs={{2,4},{4,2},{3,5},{5,3},{6,8},{8,6},{7,9},{9,7},{10,12},{12,10},{1... | collective-permute-start | bytes 466952 | tf_op jit(solution)/shard_map/ppermute | solution.py:39
  3.6 11.0 %collective-permute-start = (f32[8,4864]{1,0:T(8,128)S(1)}, f32[8,4864]{1,0:T(8,128)S(1)}, u32[]{:S(2)}, u32[]{:S(2)}) collective-permute-start(f32[8,4864]{1,0:T(8,128)S(1)} %get-tuple-element.20), channel_id=1, source_target_pairs={{0,2},{2,0},{1,3},{3,1},{4,6},{6,4},{5,7},{7,5},{8,10},{10,8},{9,1... | collective-permute-start | bytes 466952 | tf_op jit(solution)/shard_map/ppermute | solution.py:39
  7.5 1.2 %collective-permute-start.2 = (f32[4,2048]{1,0:T(4,128)S(1)}, f32[4,2048]{1,0:T(4,128)S(1)}, u32[]{:S(2)}, u32[]{:S(2)}) collective-permute-start(f32[4,2048]{1,0:T(4,128)S(1)} %get-tuple-element.21), channel_id=1, source_target_pairs={{0,1},{1,0},{2,3},{3,2},{4,5},{5,4},{6,7},{7,6},{8,9},{9,8},{10,11... | collective-permute-start | bytes 98312 | tf_op jit(solution)/shard_map/ppermute | solution.py:25
  14.6 0.8 %copy-start.3 = (f32[1,8,2048]{2,1,0:T(8,128)S(1)}, f32[1,8,2048]{2,1,0:T(8,128)}, u32[]{:S(2)}) copy-start(f32[1,8,2048]{2,1,0:T(8,128)} %param.11) | copy-start | bytes 196612
  20.8 3.8 %collective-permute-start.5 = (f32[2,2048]{1,0:T(2,128)S(1)}, f32[2,2048]{1,0:T(2,128)S(1)}, u32[]{:S(2)}, u32[]{:S(2)}) collective-permute-start(f32[2,2048]{1,0:T(2,128)S(1)} %get-tuple-element.27), channel_id=1, source_target_pairs={{0,1},{1,0},{2,3},{3,2},{4,5},{5,4},{6,7},{7,6},{8,9},{9,8},{10,11... | collective-permute-start | bytes 49160 | tf_op jit(solution)/shard_map/ppermute | solution.py:25
  20.8 3.7 %collective-permute-start.3 = (f32[2,8,128]{2,1,0:T(8,128)S(1)}, f32[2,8,128]{2,1,0:T(8,128)S(1)}, u32[]{:S(2)}, u32[]{:S(2)}) collective-permute-start(f32[2,8,128]{2,1,0:T(8,128)S(1)} %get-tuple-element.25), channel_id=1, source_target_pairs={{0,2},{2,0},{1,3},{3,1},{4,6},{6,4},{5,7},{7,5},{8,10},{10,8},{9,1... | collective-permute-start | bytes 24584 | tf_op jit(solution)/shard_map/ppermute | solution.py:39
  22.7 1.9 %collective-permute-start.4 = (f32[2,8,128]{2,1,0:T(8,128)S(1)}, f32[2,8,128]{2,1,0:T(8,128)S(1)}, u32[]{:S(2)}, u32[]{:S(2)}) collective-permute-start(f32[2,8,128]{2,1,0:T(8,128)S(1)} %get-tuple-element.26), channel_id=1, source_target_pairs={{2,4},{4,2},{3,5},{5,3},{6,8},{8,6},{7,9},{9,7},{10,12},{12,10},{1... | collective-permute-start | bytes 24584 | tf_op jit(solution)/shard_map/ppermute | solution.py:39
  27.8 4.7 %collective-permute-start.8 = (f32[2,2048]{1,0:T(2,128)S(1)}, f32[2,2048]{1,0:T(2,128)S(1)}, u32[]{:S(2)}, u32[]{:S(2)}) collective-permute-start(f32[2,2048]{1,0:T(2,128)S(1)} %get-tuple-element.33), channel_id=1, source_target_pairs={{0,1},{1,0},{2,3},{3,2},{4,5},{5,4},{6,7},{7,6},{8,9},{9,8},{10,11... | collective-permute-start | bytes 49160 | tf_op jit(solution)/shard_map/ppermute | solution.py:25
  27.9 4.6 %collective-permute-start.6 = (f32[2,8,128]{2,1,0:T(8,128)S(1)}, f32[2,8,128]{2,1,0:T(8,128)S(1)}, u32[]{:S(2)}, u32[]{:S(2)}) collective-permute-start(f32[2,8,128]{2,1,0:T(8,128)S(1)} %get-tuple-element.31), channel_id=1, source_target_pairs={{0,2},{2,0},{1,3},{3,1},{4,6},{6,4},{5,7},{7,5},{8,10},{10,8},{9,1... | collective-permute-start | bytes 24584 | tf_op jit(solution)/shard_map/ppermute | solution.py:39
  30.8 1.6 %collective-permute-start.7 = (f32[2,8,128]{2,1,0:T(8,128)S(1)}, f32[2,8,128]{2,1,0:T(8,128)S(1)}, u32[]{:S(2)}, u32[]{:S(2)}) collective-permute-start(f32[2,8,128]{2,1,0:T(8,128)S(1)} %get-tuple-element.32), channel_id=1, source_target_pairs={{2,4},{4,2},{3,5},{5,3},{6,8},{8,6},{7,9},{9,7},{10,12},{12,10},{1... | collective-permute-start | bytes 24584 | tf_op jit(solution)/shard_map/ppermute | solution.py:39

commit v3 on v2

v3 whole, which is shorter than its diff:
```python
import functools

import jax
import jax.numpy as jnp
from jax import lax
from jax.experimental import pallas as pl
from jax.experimental.pallas import tpu as pltpu
from jax.sharding import PartitionSpec as P


BLOCK = 128
ITERS = 3
LANES = 128
GAIN = 0.25
SHIFT = 1.25
F32 = jnp.float32
BF16 = jnp.bfloat16
CHUNK = 256


def swapped(block, axis, first):
    count = lax.axis_size(axis)
    route = []
    for i in range(first, count - 1, 2):
        route += [(i, i + 1), (i + 1, i)]
    return lax.ppermute(block, axis, route) if route else None


def swapped_sections(block, first):
    count, width = lax.axis_size("gz"), lax.axis_size("xy")
    route = []
    for i in range(first, count - 1, 2):
        for j in range(width):
            a, b = i * width + j, (i + 1) * width + j
            route += [(a, b), (b, a)]
    paired = {a for a, _ in route}
    for a in range(0, count * width - 1, 2):
        if a not in paired and a + 1 not in paired and a // width == (a + 1) // width:
            route += [(a, a + 1), (a + 1, a)]
    return lax.ppermute(block, ("gz", "xy"), route)


def split2(x):
    high = x.astype(BF16)
    return high, (x - high.astype(F32)).astype(BF16)


def div_mod(x, d):
    if d & (d - 1) == 0:
        return lax.shift_right_logical(x, jnp.int32(d.bit_length() - 1)), x & (d - 1)
    q = lax.div(x, jnp.int32(d))
    return q, x - q * d


def hi_lo(index, rows, cols):
    row, col = div_mod(index, cols)
    tile, lane = div_mod(col, LANES)
    return tile * rows + row, lane


def row_of(tile, k):
    return tile[k : k + 1, :]


def one_hot(index, size, shift=0):
    at = lax.broadcasted_iota(jnp.int32, (size, LANES), 0) - shift
    return jnp.concatenate(
        [jnp.where(at == row_of(index, k), 1.0, 0.0).astype(BF16) for k in range(index.shape[0])],
        axis=1,
    )


def blend(index, size, first, second):
    at = lax.broadcasted_iota(jnp.int32, (size, LANES), 0)
    out = []
    for k in range(index.shape[0]):
        here = row_of(index, k)
        out.append(
            jnp.where(at == here, row_of(first, k), jnp.where(at == here + 1, row_of(second, k), 0.0))
        )
    return jnp.concatenate(out, axis=1)


def store_lanes(lo, lanes_ref):
    hot = one_hot(lo, LANES)
    lanes_ref[0:LANES, :] = hot
    lanes_ref[LANES : 2 * LANES, :] = hot


def tall(field):
    n = field.shape[1] // LANES
    return jnp.concatenate([field[:, i * LANES : (i + 1) * LANES] for i in range(n)], axis=0)


def wide(stack, rows):
    n = stack.shape[0] // rows
    return jnp.concatenate([stack[i * rows : (i + 1) * rows, :] for i in range(n)], axis=1)


def right_of(field):
    return pltpu.roll(field, field.shape[1] - 1, 1)


def load_left(field, left_ref, sides):
    fields = []
    for c in range(2):
        fields += [field[c], right_of(field[c])] if sides == 2 else [field[c]]
    for i, f in enumerate(fields):
        stack = tall(f)
        high, low = split2(stack)
        n = stack.shape[0]
        left_ref[i * n : (i + 1) * n, 0:LANES] = high
        left_ref[i * n : (i + 1) * n, LANES : 2 * LANES] = low


def as_tiles(rows_of):
    return jnp.concatenate(
        [r[:, i * LANES : (i + 1) * LANES] for r in rows_of for i in range(CHUNK // LANES)], axis=0
    )


def looked_up(left_ref, lanes_ref, high_ref):
    high, slots = high_ref.shape
    stride = left_ref.shape[0] // 2
    found = ([], [])
    for k in range(0, slots, CHUNK):
        mask = high_ref[:, k : k + CHUNK].astype(F32)
        for c in range(2):
            got = jnp.dot(
                left_ref[c * stride : c * stride + high, :],
                lanes_ref[:, k : k + CHUNK],
                preferred_element_type=F32,
            )
            found[c].append(jnp.sum(mask * got, axis=0, keepdims=True))
    return jnp.stack([as_tiles(f) for f in found])


def interpolated(left_ref, lanes_ref, blend_ref):
    high, slots = blend_ref.shape[1:]
    found = ([], [])
    for k in range(0, slots, CHUNK):
        wl = blend_ref[0, :, k : k + CHUNK]
        wr = blend_ref[1, :, k : k + CHUNK]
        for c in range(2):
            got = jnp.dot(
                left_ref[2 * c * high : 2 * (c + 1) * high, :],
                lanes_ref[:, k : k + CHUNK],
                preferred_element_type=F32,
            )
            value = wl * got[:high] + wr * got[high:]
            found[c].append(jnp.sum(value, axis=0, keepdims=True))
    return jnp.stack([as_tiles(f) for f in found])


NT = (((1,), (1,)), ((), ()))


def scaled(mask_ref, tile):
    return jnp.concatenate(
        [mask_ref[:, k * LANES : (k + 1) * LANES] * row_of(tile, k) for k in range(tile.shape[0])],
        axis=1,
    )


def spread_own(values, lanes_ref, high_ref, rows):
    high = high_ref.shape[0]
    result = []
    for c in range(2):
        parts = [scaled(high_ref, part) for part in split2(values[c])]
        out = lax.dot_general(
            jnp.concatenate(parts, axis=0), lanes_ref[0:LANES, :], NT, preferred_element_type=F32
        )
        result.append(wide(out[:high] + out[high:], rows))
    return result


def spread_corners(values, weights, lanes_ref, high_ref, below_ref, rows):
    high = high_ref.shape[0]
    result = []
    for c in range(2):
        parts = []
        for side in range(2):
            for up, down in zip(split2(values[c] * weights[side]), split2(values[c] * weights[2 + side])):
                parts.append(scaled(high_ref, up) + scaled(below_ref, down))
        out = lax.dot_general(
            jnp.concatenate(parts, axis=0), lanes_ref[0:LANES, :], NT, preferred_element_type=F32
        )
        sides = [
            wide(out[p * high : (p + 1) * high] + out[(p + 1) * high : (p + 2) * high], rows)
            for p in (0, 2)
        ]
        result.append(sides[0] + pltpu.roll(sides[1], 1, 1))
    return result


def springs(field, across, down, hold, upper_row, lower_row, rim):
    rows, cols = field.shape
    col = lax.broadcasted_iota(jnp.int32, (rows, cols), 1)
    row = lax.broadcasted_iota(jnp.int32, (rows, cols), 0)
    right = jnp.where(col == cols - 1, 0.0, pltpu.roll(field, cols - 1, 1))
    pull = across * (field - right)
    out = pull - jnp.where(col == 0, 0.0, pltpu.roll(pull, 1, 1))
    lower = jnp.where(row == rows - 1, lower_row, pltpu.roll(field, rows - 1, 0))
    pull = down * (field - lower)
    above = rim * (upper_row - field[0:1, :])
    out = out + pull - jnp.where(row == 0, above, pltpu.roll(pull, 1, 0))
    return out + hold * field


def pick(flag, a, b):
    return jnp.where(flag, a, b)


def edges_of(get_row, rows, even_b, two):
    first = [get_row(c, 0) for c in range(2)]
    last = [get_row(c, rows - 1) for c in range(2)]
    out = [jnp.concatenate([pick(even_b, last[c], first[c]) for c in range(2)], axis=0)]
    if two:
        out.append(jnp.concatenate([pick(even_b, first[c], last[c]) for c in range(2)], axis=0))
    return out


def pack_kernel(two, flags, count, field, down, hold, source, target, weights, *refs):
    rows, cols = down.shape
    even_b = flags[1] == 0
    has_next = flags[2]
    nb = source.shape[0]
    n_edges = 2 if two else 1
    pack, edges = refs[0], refs[1 : 1 + n_edges]
    last_down, hold_out, ids, held, sems = refs[1 + n_edges :]
    pairs = [(field.at[c], pack.at[:, c * cols : (c + 1) * cols]) for c in range(2)]
    pairs += [(down, last_down), (source, ids.at[0]), (target, ids.at[1]), (weights, held)]
    pairs += [(hold, hold_out)]
    copies = [pltpu.make_async_copy(a, b, sems.at[i]) for i, (a, b) in enumerate(pairs)]
    for copy in copies:
        copy.start()
    for copy in copies:
        copy.wait()
    block = lax.broadcasted_iota(jnp.int32, (nb, LANES), 0)
    live = jnp.where(block * LANES < count[0, 0] * BLOCK * has_next, 1.0, 0.0)
    parts = [ids[0].astype(F32), ids[1].astype(F32)] + [held[q] * live for q in range(4)]
    for i, part in enumerate(parts):
        pack[:nb, 2 * cols + i * LANES : 2 * cols + (i + 1) * LANES] = part
    messages = edges_of(lambda c, r: pack[r : r + 1, c * cols : (c + 1) * cols], rows, even_b, two)
    for message, edge in zip(messages, edges):
        edge[0:2, :] = message
        edge[2:3, :] = last_down[rows - 1 : rows, :]


def halves(flags, edge_refs):
    even_b = flags[1] == 0
    zero = edge_refs[0][...]
    if len(edge_refs) == 2:
        other = edge_refs[1][...]
    else:
        other = jnp.zeros_like(zero)
    return pick(even_b, other, zero), pick(even_b, zero, other)


def live_slots(flags, count, nb):
    block = lax.broadcasted_iota(jnp.int32, (nb, LANES), 0)
    return jnp.where(block * LANES < count[0, 0] * BLOCK * flags[2], 1.0, 0.0)


def spring_image(field, across, down, hold, above, below, rim):
    return [
        springs(
            field[c], across[...], down[...], hold[...], above[c : c + 1], below[c : c + 1], rim
        )
        for c in range(2)
    ]


def early_kernel(flags, field_ref, across, down, hold, source, target, weights, *refs):
    edge_refs = refs[:-8]
    base, own_ref, rim_ref, own_lanes, own_high, next_lanes, next_blend, left = refs[-8:]
    rows, cols = across.shape
    size = own_high.shape[0]
    field = [field_ref[0], field_ref[1]]
    above, below = halves(flags, edge_refs)
    image = spring_image(field, across, down, hold, above, below, above[2:3, :])
    for c in range(2):
        base[c] = image[c]
    rim_ref[...] = above[2:3, :]
    hi, lo = hi_lo(source[...], rows, cols)
    store_lanes(lo, own_lanes)
    own_high[...] = one_hot(hi, size)
    hi, lo = hi_lo(target[...], rows, cols)
    store_lanes(lo, next_lanes)
    for side in range(2):
        next_blend[side] = blend(hi, size, weights[side], weights[2 + side])
    load_left(field, left, 1)
    own_ref[...] = looked_up(left, own_lanes, own_high)


def send_on(even, even_b, two, field, own_tables, prev_tables, left, local_ref, send0, send1, *edges):
    own_lanes, own_high = own_tables
    prev_lanes, prev_blend = prev_tables
    load_left(field, left, 2)
    own = looked_up(left, own_lanes, own_high)
    mid = interpolated(left, prev_lanes, prev_blend)
    local_ref[0] = own
    local_ref[1] = mid
    send0[...] = pick(even, own, mid)
    send1[...] = pick(even, mid, own)
    messages = edges_of(lambda c, r: field[c][r : r + 1, :], field[0].shape[0], even_b, two)
    for message, edge in zip(messages, edges):
        edge[...] = message


def stepped(field_ref, image):
    return [GAIN * image[c] - SHIFT * field_ref[c] for c in range(2)]


def first_kernel(
    two, flags, count, field_ref, base, own, own_lanes, own_high, next_lanes, next_blend, got0, got1, *refs
):
    refs, (left, next_left, prev_left, lanes, mask) = refs[:-5], refs[-5:]
    out, local_ref, send0, send1, *edges = refs[:-5]
    prev_weights, prev_lanes, prev_high, prev_below, prev_blend = refs[-5:]
    even, even_b = flags[0] == 0, flags[1] == 0
    nb = own.shape[1]
    rows, cols = field_ref.shape[1:]
    size = own_high.shape[0]
    slot = lambda ref, i: ref[:nb, 2 * cols + i * LANES : 2 * cols + (i + 1) * LANES]
    prev = [pick(even, slot(got1, i), slot(got0, i)) for i in range(6)]
    comp = lambda ref, c: ref[:, c * cols : (c + 1) * cols]
    weights = [jnp.where(flags[3] > 0, w, 0.0) for w in prev[2:]]
    for q in range(4):
        prev_weights[q] = weights[q]
    hi, lo = hi_lo(prev[1].astype(jnp.int32), rows, cols)
    store_lanes(lo, prev_lanes)
    prev_high[...] = one_hot(hi, size)
    prev_below[...] = one_hot(hi, size, 1)
    for side in range(2):
        prev_blend[side] = blend(hi, size, weights[side], weights[2 + side])
    load_left([field_ref[0], field_ref[1]], left, 2)
    mid = interpolated(left, prev_lanes, prev_blend)
    load_left([pick(even, comp(got0, c), comp(got1, c)) for c in range(2)], next_left, 2)
    got_next = interpolated(next_left, next_lanes, next_blend)
    hi, lo = hi_lo(prev[0].astype(jnp.int32), rows, cols)
    store_lanes(lo, lanes)
    mask[...] = one_hot(hi, size)
    load_left([pick(even, comp(got1, c), comp(got0, c)) for c in range(2)], prev_left, 1)
    got_prev = looked_up(prev_left, lanes, mask)
    live = live_slots(flags, count, nb)
    pulled = spread_own([live * (own[c] - got_next[c]) for c in range(2)], own_lanes, own_high, rows)
    error = [mid[c] - got_prev[c] for c in range(2)]
    pushed = spread_corners(error, weights, prev_lanes, prev_high, prev_below, rows)
    after = stepped(field_ref, [base[c] + pulled[c] + pushed[c] for c in range(2)])
    for c in range(2):
        out[c] = after[c]
    send_on(
        even,
        even_b,
        two,
        after,
        (own_lanes, own_high),
        (prev_lanes, prev_blend),
        left,
        local_ref,
        send0,
        send1,
        *edges,
    )


def moments_of(pairs):
    lane = lax.broadcasted_iota(jnp.int32, (1, LANES), 1)
    total = jnp.zeros((1, LANES), F32)
    for i, (u, w) in enumerate(pairs):
        s = u[0] * w[0] + u[1] * w[1]
        s = jnp.sum(jnp.sum(s, axis=0, keepdims=True), axis=1, keepdims=True)
        total = total + jnp.where(lane == i, s, 0.0)
    return total


def step_kernel(
    last,
    two,
    n_edges,
    flags,
    count,
    field_ref,
    across,
    down,
    hold,
    own_lanes,
    own_high,
    prev_weights,
    prev_lanes,
    prev_high,
    prev_below,
    prev_blend,
    local,
    rim,
    got0,
    got1,
    *refs,
):
    refs = list(refs)
    edge_refs = [refs.pop(0) for _ in range(n_edges)]
    earlier = [refs.pop(0) for _ in range(ITERS - 1)] if last else []
    out = refs.pop(0)
    even, even_b = flags[0] == 0, flags[1] == 0
    nb = local.shape[2]
    rows, _ = across.shape
    field = [field_ref[0], field_ref[1]]
    live = live_slots(flags, count, nb)
    got_next = pick(even, got0[...], got1[...])
    got_prev = pick(even, got1[...], got0[...])
    pulled = spread_own([live * (local[0, c] - got_next[c]) for c in range(2)], own_lanes, own_high, rows)
    error = [local[1, c] - got_prev[c] for c in range(2)]
    weights = [prev_weights[q] for q in range(4)]
    pushed = spread_corners(error, weights, prev_lanes, prev_high, prev_below, rows)
    above, below = halves(flags, edge_refs)
    image = spring_image(field, across, down, hold, above, below, rim[...])
    after = stepped(field_ref, [image[c] + pulled[c] + pushed[c] for c in range(2)])
    for c in range(2):
        out[c] = after[c]
    if last:
        basis = [(ref[0], ref[1]) for ref in earlier] + [field, after]
        total = moments_of([(basis[i // 2], basis[i - i // 2]) for i in range(2 * ITERS)])
        sums = refs.pop(0)
        sums[...] = jnp.broadcast_to(total, sums.shape)
    else:
        messages, left = refs[:-1], refs[-1]
        send_on(even, even_b, two, after, (own_lanes, own_high), (prev_lanes, prev_blend), left, *messages)


def conjugate(moments):
    def apply(p):
        shifted = [None] + p
        return [
            (SHIFT * p[k] if k < len(p) else 0.0) * (1.0 / GAIN)
            + ((1.0 / GAIN) * shifted[k] if k else 0.0)
            for k in range(len(p) + 1)
        ]

    def product(p, q):
        return sum(p[i] * q[j] * moments[i + j] for i in range(len(p)) for j in range(len(q)))

    def plus(p, factor, q):
        size = max(len(p), len(q))
        pad = lambda a: a + [None] * (size - len(a))
        out = []
        for a, b in zip(pad(p), pad(q)):
            out.append(factor * b if a is None else a if b is None else a + factor * b)
        return out

    one = jnp.ones_like(moments[0])
    solution_field, residual, direction = [], [one], [one]
    norm_now = moments[0]
    for step in range(ITERS):
        image = apply(direction)
        alpha = norm_now / product(direction, image)
        solution_field = plus(solution_field, alpha, direction)
        residual = plus(residual, -alpha, image)
        if step + 1 < ITERS:
            norm_next = product(residual, residual)
            direction = plus(residual, norm_next / norm_now, direction)
            norm_now = norm_next
    return solution_field, residual


def finish_kernel(sums, *refs):
    basis, (solution_ref, residual_ref) = refs[: ITERS + 1], refs[ITERS + 1 :]
    total = jnp.sum(sums[...], axis=0, keepdims=True)
    lane = lax.broadcasted_iota(jnp.int32, (1, LANES), 1)
    moments = [
        jnp.sum(jnp.where(lane == i, total, 0.0), axis=1, keepdims=True) for i in range(2 * ITERS)
    ]
    solution_field, residual = conjugate(moments)
    for c in range(2):
        values = [ref[c] for ref in basis]
        solution_ref[c] = sum(a * v for a, v in zip(solution_field, values))
        residual_ref[c] = sum(a * v for a, v in zip(residual, values))


VMEM = pl.BlockSpec(memory_space=pltpu.VMEM)
SMEM = pl.BlockSpec(memory_space=pltpu.SMEM)
HBM = pl.BlockSpec(memory_space=pltpu.HBM)


def call(kernel, in_specs, shapes, scratch=()):
    shapes = [s if isinstance(s, jax.ShapeDtypeStruct) else jax.ShapeDtypeStruct(s, F32) for s in shapes]
    return pl.pallas_call(
        kernel,
        in_specs=in_specs,
        out_specs=[VMEM] * len(shapes),
        out_shape=shapes,
        scratch_shapes=list(scratch),
        compiler_params=pltpu.CompilerParams(vmem_limit_bytes=48 * 1024 * 1024),
    )


def body(
    right_side,
    stiff_across,
    stiff_down,
    anchor,
    source_node,
    target_cell,
    corner_weight,
    block_count,
):
    rows, cols = stiff_across.shape[1:]
    rhs = right_side[:, 0]
    across, down, hold = stiff_across[0], stiff_down[0], anchor[0]
    slots = source_node.shape[2]
    nb = slots // LANES
    source = source_node.reshape(nb, LANES)
    target = target_cell.reshape(nb, LANES)
    weights = corner_weight.reshape(4, nb, LANES)
    n_gz, n_xy = lax.axis_size("gz"), lax.axis_size("xy")
    at_gz, at_xy = lax.axis_index("gz"), lax.axis_index("xy")
    two = n_xy > 2
    flags = jnp.stack([at_gz % 2, at_xy % 2, (at_gz < n_gz - 1).astype(jnp.int32), (at_gz > 0).astype(jnp.int32)]).astype(jnp.int32)
    n_edges = 2 if two else 1

    in_hbm = lambda *arrays: [pltpu.with_memory_space_constraint(a, pltpu.HBM) for a in arrays]
    pack, *rest = call(
        functools.partial(pack_kernel, two),
        [SMEM, SMEM] + [HBM] * 6,
        [(rows, 2 * cols + 6 * LANES)] + [(4, cols)] * n_edges + [(rows, cols)] * 2,
        [
            pltpu.VMEM((2, nb, LANES), jnp.int32),
            pltpu.VMEM((4, nb, LANES), F32),
            pltpu.SemaphoreType.DMA((7,)),
        ],
    )(flags, block_count, *in_hbm(rhs, down, hold, source, target, weights))
    edges, (down, hold) = rest[:n_edges], rest[n_edges:]

    def exchange(to0, to1, edges):
        got1 = swapped_sections(to1, 1)
        got0 = swapped_sections(to0, 0)
        got_edges = []
        for i, edge in enumerate(edges):
            got_edges.append(swapped(edge, "xy", i))
        return got0, got1, got_edges

    field_shape = (2, rows, cols)
    message = (2, nb, LANES)
    size = rows * cols // LANES
    common = [field_shape, (2,) + message, message, message] + [(2, cols)] * n_edges
    table = lambda *shape: jax.ShapeDtypeStruct(shape, BF16)
    left = lambda sides: pltpu.VMEM((2 * sides * size, 2 * LANES), BF16)
    lanes, mask, blends = (2 * LANES, slots), (size, slots), (2, size, slots)
    run = lambda kernel, shapes, scratch, *args: call(
        kernel, [SMEM, SMEM] + [VMEM] * (len(args) - 2), shapes, scratch
    )(*args)
    stiff = (across, down, hold)
    basis = [rhs]

    got0, got1, got_edges = exchange(pack, pack, edges)
    base, own, rim, own_lanes, own_high, next_lanes, next_blend = call(
        early_kernel,
        [SMEM] + [VMEM] * (7 + n_edges),
        [field_shape, message, (1, cols), table(*lanes), table(*mask), table(*lanes), blends],
        [left(1)],
    )(flags, rhs, *stiff, source, target, weights, *got_edges)
    field, local, to0, to1, *rest = run(
        functools.partial(first_kernel, two),
        common + [(4, nb, LANES), table(*lanes), table(*mask), table(*mask), blends],
        [left(2), left(2), left(1), pltpu.VMEM(lanes, BF16), pltpu.VMEM(mask, BF16)],
        *(flags, block_count, rhs, base, own, own_lanes, own_high, next_lanes, next_blend, got0, got1),
    )
    edges, prev = rest[:n_edges], rest[n_edges:]

    for step in range(1, ITERS):
        last = step == ITERS - 1
        got0, got1, got_edges = exchange(to0, to1, edges)
        field_next, *rest = run(
            functools.partial(step_kernel, last, two, n_edges),
            [field_shape, (n_gz * n_xy, LANES)] if last else common,
            [] if last else [left(2)],
            *(flags, block_count, field, *stiff, own_lanes, own_high, *prev, local, rim),
            *(got0, got1, *got_edges),
            *(basis if last else []),
        )
        basis.append(field)
        field = field_next
        if not last:
            local, to0, to1, *edges = rest
    basis.append(field)
    sums = lax.all_to_all(rest[0].reshape(n_gz * n_xy, 1, LANES), ("gz", "xy"), 0, 0)
    sums = sums.reshape(n_gz * n_xy, LANES)
    solution_field, residual = call(finish_kernel, [VMEM] * (1 + len(basis)), [field_shape] * 2)(sums, *basis)
    return solution_field[:, None], residual[:, None]


def solution(mesh):
    in_specs = (
        P(None, "gz", "xy", None),
        P("gz", "xy", None),
        P("gz", "xy", None),
        P("gz", "xy", None),
        P("gz", "xy", None),
        P("gz", "xy", None),
        P(None, "gz", "xy", None),
        P("gz", "xy"),
    )
    out_specs = (P(None, "gz", "xy", None), P(None, "gz", "xy", None))
    return jax.shard_map(body, mesh=mesh, in_specs=in_specs, out_specs=out_specs, check_vma=False)
```

time: 50.6 us -> 46.9 us (0.927)
  Pallas kernels: 12.9 us -> 11.4 us
  waiting for transfers between devices: 10.3 us -> 9.05 us
  local copies, waits for them, and re-layouts: 0.87 us -> 0.02 us
    pallas_call x4 -> x5, Pallas kernels: 12 us -> 10.5 us  [the longest x3 7.64 us: body(): call(kernel, [SMEM, SMEM] + [VMEM] * (len(args) - 2), shapes, scratch)]
    ppermute x6, waiting for transfers between devices: 9.09 us -> 7.84 us  [swapped_sections(): return lax.ppermute(block, ('gz', 'xy'), route)]
    unnamed x14 -> x10, local copies, waits for them, and re-layouts: 0.87 us -> 0.02 us
  transfers between devices with their start and end apart: 9 -> 9, of which waited for: 4 -> 4; matrix products, arithmetic and copies ran while one was open for 0% -> 0% of each run, Pallas kernels for 0% -> 3%
where the time goes in v3:
time: 46.9 us; the launch traced here: 46.7 us
  blocking collectives  15 us (32%)
  Pallas kernels  11.4 us (24%)
  starting transfers between devices  9.77 us (21%)
  waiting for transfers between devices  9.05 us (19%)
  between operations  1.4 us (3%)
    all_to_all x1, blocking collectives, body(): lax.all_to_all(rest[0].reshape(n_gz * n_xy, 1, LANES), ('gz', 'xy'), 0, 0)  15 us
    ppermute x6, starting transfers between devices, swapped_sections(): return lax.ppermute(block, ('gz', 'xy'), route)  9.62 us
    ppermute x6, waiting for transfers between devices, swapped_sections(): return lax.ppermute(block, ('gz', 'xy'), route)  7.84 us
    pallas_call x3, Pallas kernels, body(): call(kernel, [SMEM, SMEM] + [VMEM] * (len(args) - 2), shapes, scratch)  7.64 us
    pallas_call x1, Pallas kernels, body(): call(functools.partial(pack_kernel, two), [SMEM, SMEM] + [HBM] * 6, [(row...  1.6 us
    pallas_call x1, Pallas kernels, body(): call(early_kernel, [SMEM] + [VMEM] * (7 + n_edges), [field_shape, message...  1.21 us
    ppermute x3, waiting for transfers between devices, swapped(): return lax.ppermute(block, axis, route) if route else None  1.21 us
  transfers between devices with their start and end apart: 9, of which 4 were waited for; matrix products, arithmetic and copies ran while one was open for 0% of the time, Pallas kernels for 3%

profile of v3, /device:TPU:0, one launch (start us, length us, event | category | flops | bytes accessed | tf_op | source)
XLA Modules:
  0.0 46.7 jit_solution(4291045779269269666)
XLA Ops:
  1.3 0.1 pad_add_fusion.flags
  1.4 1.6 %shard_map.95 = (f32[8,4864]{1,0:T(8,128)S(1)}, f32[4,2048]{1,0:T(4,128)S(1)}, f32[8,2048]{1,0:T(8,128)S(1)}, f32[8,2048]{1,0:T(8,128)S(1)}) custom-call(s32[4]{0:T(128)S(1)} %pad_add_fusion.flags, s32[1,1]{1,0:T(1,128)S(6)} %copy.15.count, f32[2,8,2048]{2,1,0:T(8,128)} %bitcast.21, f32[8,2048]{1,0:T(8,128)} %bitcast.37, f32[8,2048]{1,0:T(8,128)} %bitcast.38, ...), custom_call_target="tpu_custom_call" | custom-call | tf_op jit(solution)/shard_map/pallas_call | solution.py:522
  3.0 0.0 copy-start.4
  3.0 0.0 copy-start.3
  3.0 0.6 %collective-permute-start.2 = (f32[8,4864]{1,0:T(8,128)S(1)}, f32[8,4864]{1,0:T(8,128)S(1)}, u32[]{:S(2)}, u32[]{:S(2)}) collective-permute-start(f32[8,4864]{1,0:T(8,128)S(1)} %get-tuple-element.41), channel_id=1, source_target_pairs={{2,4},{4,2},{3,5},{5,3},{6,8},{8,6},{7,9},{9,7},{10,12},{12,10},{1... | collective-permute-start | bytes 466952 | tf_op jit(solution)/shard_map/ppermute | solution.py:40
  3.6 4.0 %collective-permute-start.1 = (f32[8,4864]{1,0:T(8,128)S(1)}, f32[8,4864]{1,0:T(8,128)S(1)}, u32[]{:S(2)}, u32[]{:S(2)}) collective-permute-start(f32[8,4864]{1,0:T(8,128)S(1)} %get-tuple-element.41), channel_id=1, source_target_pairs={{0,2},{2,0},{1,3},{3,1},{4,6},{6,4},{5,7},{7,5},{8,10},{10,8},{9,1... | collective-permute-start | bytes 466952 | tf_op jit(solution)/shard_map/ppermute | solution.py:40
  7.5 0.0 collective-permute-start
  7.5 1.2 %collective-permute-done.refs_0_ = f32[4,2048]{1,0:T(4,128)S(1)} collective-permute-done((f32[4,2048]{1,0:T(4,128)S(1)}, f32[4,2048]{1,0:T(4,128)S(1)}, u32[]{:S(2)}, u32[]{:S(2)}) %collective-permute-start) | collective-permute-done | bytes 32800 | tf_op jit(solution)/shard_map/ppermute | solution.py:26
  8.7 0.0 copy-done
  8.8 0.0 copy-done.1
  8.8 0.0 copy-done.2
  8.8 0.0 copy-done.4
  8.8 1.2 %shard_map.96 = (f32[2,8,2048]{2,1,0:T(8,128)S(1)}, f32[2,8,128]{2,1,0:T(8,128)S(1)}, f32[1,2048]{1,0:T(1,128)S(1)}, bf16[256,1024]{1,0:T(8,128)(2,1)S(1)}, bf16...) custom-call(s32[4]{0:T(128)S(1)} %pad_add_fusion.flags, ...), custom_call_target="tpu_custom_call" | custom-call | tf_op jit(solution)/shard_map/pallas_call | solution.py:556
  10.0 0.0 collective-permute-done.2.got1
  10.0 4.6 %collective-permute-done.1.got0 = f32[8,4864]{1,0:T(8,128)S(1)} collective-permute-done((f32[8,4864]{1,0:T(8,128)S(1)}, f32[8,4864]{1,0:T(8,128)S(1)}, u32[]{:S(2)}, u32[]{:S(2)}) %collective-permute-start.1) | collective-permute-done | bytes 155680 | tf_op jit(solution)/shard_map/ppermute | solution.py:40
  14.6 3.5 %shard_map.97 = (f32[2,8,2048]{2,1,0:T(8,128)S(1)}, f32[2,2,8,128]{3,2,1,0:T(8,128)S(1)}, f32[2,8,128]{2,1,0:T(8,128)S(1)}, f32[2,8,128]{2,1,0:T(8,128)S(1)}, f3...) custom-call(s32[4]{0:T(128)S(1)} %pad_add_fusion.flags, ...), custom_call_target="tpu_custom_call" | custom-call | tf_op jit(solution)/shard_map/pallas_call | solution.py:549
  18.1 0.1 collective-permute-start.5
  18.2 1.8 %collective-permute-start.3 = (f32[2,8,128]{2,1,0:T(8,128)S(1)}, f32[2,8,128]{2,1,0:T(8,128)S(1)}, u32[]{:S(2)}, u32[]{:S(2)}) collective-permute-start(f32[2,8,128]{2,1,0:T(8,128)S(1)} %get-tuple-element.50), channel_id=1, source_target_pairs={{0,2},{2,0},{1,3},{3,1},{4,6},{6,4},{5,7},{7,5},{8,10},{10,8},{9,1... | collective-permute-start | bytes 24584 | tf_op jit(solution)/shard_map/ppermute | solution.py:40
  20.0 0.2 collective-permute-start.4
  20.2 1.8 %collective-permute-done.3.got0 = f32[2,8,128]{2,1,0:T(8,128)S(1)} collective-permute-done((f32[2,8,128]{2,1,0:T(8,128)S(1)}, f32[2,8,128]{2,1,0:T(8,128)S(1)}, u32[]{:S(2)}, u32[]{:S(2)}) %collective-permute-start.3) | collective-permute-done | bytes 8224 | tf_op jit(solution)/shard_map/ppermute | solution.py:40
  21.9 0.0 collective-permute-done.4.got1
  21.9 0.0 collective-permute-done.5.refs_0_
  21.9 2.3 %shard_map.98 = (f32[2,8,2048]{2,1,0:T(8,128)S(1)}, f32[2,2,8,128]{3,2,1,0:T(8,128)S(1)}, f32[2,8,128]{2,1,0:T(8,128)S(1)}, f32[2,8,128]{2,1,0:T(8,128)S(1)}, f32[2,2048]{1,0:T(2,128)S(1)}) custom-call(s32[4]{0:T(128)S(1)} %pad_add_fusion.flags, s32[1,1]{1,0:T(1,128)S(6)} %copy.15.count, f32[2,8,2048]{2,1,0:T(8,128)S(1)} %get-tuple-element.42.field_ref.refs_2_.refs_1_, ...), custom_call_target="tpu_custom_call" | custom-call | tf_op jit(solution)/shard_map/pallas_call | solution.py:549
  24.2 0.1 collective-permute-start.8
  24.3 3.0 %collective-permute-start.6 = (f32[2,8,128]{2,1,0:T(8,128)S(1)}, f32[2,8,128]{2,1,0:T(8,128)S(1)}, u32[]{:S(2)}, u32[]{:S(2)}) collective-permute-start(f32[2,8,128]{2,1,0:T(8,128)S(1)} %get-tuple-element.55), channel_id=1, source_target_pairs={{0,2},{2,0},{1,3},{3,1},{4,6},{6,4},{5,7},{7,5},{8,10},{10,8},{9,1... | collective-permute-start | bytes 24584 | tf_op jit(solution)/shard_map/ppermute | solution.py:40
  27.3 0.2 collective-permute-start.7
  27.4 1.5 %collective-permute-done.6.got0 = f32[2,8,128]{2,1,0:T(8,128)S(1)} collective-permute-done((f32[2,8,128]{2,1,0:T(8,128)S(1)}, f32[2,8,128]{2,1,0:T(8,128)S(1)}, u32[]{:S(2)}, u32[]{:S(2)}) %collective-permute-start.6) | collective-permute-done | bytes 8224 | tf_op jit(solution)/shard_map/ppermute | solution.py:40
  28.9 0.0 collective-permute-done.7.got1
  28.9 0.0 collective-permute-done.8.refs_0_
  28.9 1.9 %shard_map.99 = (f32[2,8,2048]{2,1,0:T(8,128)S(1)}, f32[32,128]{1,0:T(8,128)S(1)}) custom-call(s32[4]{0:T(128)S(1)} %pad_add_fusion.flags, s32[1,1]{1,0:T(1,128)S(6)} %copy.15.count, f32[2,8,2048]{2,1,0:T(8,128)S(1)} %get-tuple-element.53.field_ref.refs_2_, f32[8,2048]{1,0:T(8,128)S(1)} %bitcast.28, f32[8,2048]{1,0:T(8,128)S(1)} %get-tuple-element.32.down, ...), custom_call_target="tpu_custom_call" | custom-call | tf_op jit(solution)/shard_map/pallas_call | solution.py:549
  30.8 15.0 %all_to_all.5 = f32[32,1,128]{2,1,0:T(1,128)S(1)} all-to-all(f32[32,1,128]{2,1,0:T(1,128)S(1)} %bitcast.36), channel_id=1, replica_groups=mesh['gz'=16,'xy'=2] {'gz','xy'}, dimensions={0} | all-to-all | bytes 32768 | tf_op jit(solution)/shard_map/all_to_all | solution.py:586
  45.8 0.9 %shard_map.100 = (f32[2,8,2048]{2,1,0:T(8,128)}, f32[2,8,2048]{2,1,0:T(8,128)}) custom-call(f32[32,128]{1,0:T(8,128)S(1)} %bitcast.31, f32[2,8,2048]{2,1,0:T(8,128)S(1)} %bitcast.25, f32[2,8,2048]{2,1,0:T(8,128)S(1)} %get-tuple-element.42.field_ref.refs_2_.refs_1_, f32[2,8,2048]{2,1,0:T(8,128)S(1)} %get-tuple-element.53.field_ref.refs_2_, ...), custom_call_target="tpu_custom_call" | custom-call | tf_op jit(solution)/shard_map/pallas_call | solution.py:588
  (4 shorter events, 0.0 us)
Async XLA Ops:
  1.4 7.4 %copy-start = (f32[2,1,8,2048]{3,2,1,0:T(8,128)S(1)}, f32[2,1,8,2048]{3,2,1,0:T(8,128)}, u32[]{:S(2)}) copy-start(f32[2,1,8,2048]{3,2,1,0:T(8,128)} %param.8) | copy-start | bytes 393220
  1.4 7.4 %copy-start.1 = (f32[1,8,2048]{2,1,0:T(8,128)S(1)}, f32[1,8,2048]{2,1,0:T(8,128)}, u32[]{:S(2)}) copy-start(f32[1,8,2048]{2,1,0:T(8,128)} %param.9) | copy-start | bytes 196612
  1.4 7.4 %copy-start.2 = (f32[4,1,1,1024]{3,2,1,0:T(1,128)S(1)}, f32[4,1,1,1024]{3,2,1,0:T(1,128)}, u32[]{:S(2)}) copy-start(f32[4,1,1,1024]{3,2,1,0:T(1,128)} %param.14) | copy-start | bytes 49156
  3.0 5.8 %copy-start.4 = (s32[1,1,1024]{2,1,0:T(1,128)S(1)}, s32[1,1,1024]{2,1,0:T(1,128)}, u32[]{:S(2)}) copy-start(s32[1,1,1024]{2,1,0:T(1,128)} %param.13) | copy-start | bytes 12292
  3.0 5.8 %copy-start.3 = (s32[1,1,1024]{2,1,0:T(1,128)S(1)}, s32[1,1,1024]{2,1,0:T(1,128)}, u32[]{:S(2)}) copy-start(s32[1,1,1024]{2,1,0:T(1,128)} %param.12) | copy-start | bytes 12292
  3.0 7.0 %collective-permute-start.2 = (f32[8,4864]{1,0:T(8,128)S(1)}, f32[8,4864]{1,0:T(8,128)S(1)}, u32[]{:S(2)}, u32[]{:S(2)}) collective-permute-start(f32[8,4864]{1,0:T(8,128)S(1)} %get-tuple-element.41), channel_id=1, source_target_pairs={{2,4},{4,2},{3,5},{5,3},{6,8},{8,6},{7,9},{9,7},{10,12},{12,10},{1... | collective-permute-start | bytes 466952 | tf_op jit(solution)/shard_map/ppermute | solution.py:40
  3.6 11.0 %collective-permute-start.1 = (f32[8,4864]{1,0:T(8,128)S(1)}, f32[8,4864]{1,0:T(8,128)S(1)}, u32[]{:S(2)}, u32[]{:S(2)}) collective-permute-start(f32[8,4864]{1,0:T(8,128)S(1)} %get-tuple-element.41), channel_id=1, source_target_pairs={{0,2},{2,0},{1,3},{3,1},{4,6},{6,4},{5,7},{7,5},{8,10},{10,8},{9,1... | collective-permute-start | bytes 466952 | tf_op jit(solution)/shard_map/ppermute | solution.py:40
  7.5 1.2 %collective-permute-start = (f32[4,2048]{1,0:T(4,128)S(1)}, f32[4,2048]{1,0:T(4,128)S(1)}, u32[]{:S(2)}, u32[]{:S(2)}) collective-permute-start(f32[4,2048]{1,0:T(4,128)S(1)} %get-tuple-element.34), channel_id=1, source_target_pairs={{0,1},{1,0},{2,3},{3,2},{4,5},{5,4},{6,7},{7,6},{8,9},{9,8},{10,11... | collective-permute-start | bytes 98312 | tf_op jit(solution)/shard_map/ppermute | solution.py:26
  18.1 3.8 %collective-permute-start.5 = (f32[2,2048]{1,0:T(2,128)S(1)}, f32[2,2048]{1,0:T(2,128)S(1)}, u32[]{:S(2)}, u32[]{:S(2)}) collective-permute-start(f32[2,2048]{1,0:T(2,128)S(1)} %get-tuple-element.52), channel_id=1, source_target_pairs={{0,1},{1,0},{2,3},{3,2},{4,5},{5,4},{6,7},{7,6},{8,9},{9,8},{10,11... | collective-permute-start | bytes 49160 | tf_op jit(solution)/shard_map/ppermute | solution.py:26
  18.2 3.7 %collective-permute-start.3 = (f32[2,8,128]{2,1,0:T(8,128)S(1)}, f32[2,8,128]{2,1,0:T(8,128)S(1)}, u32[]{:S(2)}, u32[]{:S(2)}) collective-permute-start(f32[2,8,128]{2,1,0:T(8,128)S(1)} %get-tuple-element.50), channel_id=1, source_target_pairs={{0,2},{2,0},{1,3},{3,1},{4,6},{6,4},{5,7},{7,5},{8,10},{10,8},{9,1... | collective-permute-start | bytes 24584 | tf_op jit(solution)/shard_map/ppermute | solution.py:40
  20.0 1.9 %collective-permute-start.4 = (f32[2,8,128]{2,1,0:T(8,128)S(1)}, f32[2,8,128]{2,1,0:T(8,128)S(1)}, u32[]{:S(2)}, u32[]{:S(2)}) collective-permute-start(f32[2,8,128]{2,1,0:T(8,128)S(1)} %get-tuple-element.51), channel_id=1, source_target_pairs={{2,4},{4,2},{3,5},{5,3},{6,8},{8,6},{7,9},{9,7},{10,12},{12,10},{1... | collective-permute-start | bytes 24584 | tf_op jit(solution)/shard_map/ppermute | solution.py:40
  24.2 4.7 %collective-permute-start.8 = (f32[2,2048]{1,0:T(2,128)S(1)}, f32[2,2048]{1,0:T(2,128)S(1)}, u32[]{:S(2)}, u32[]{:S(2)}) collective-permute-start(f32[2,2048]{1,0:T(2,128)S(1)} %get-tuple-element.57), channel_id=1, source_target_pairs={{0,1},{1,0},{2,3},{3,2},{4,5},{5,4},{6,7},{7,6},{8,9},{9,8},{10,11... | collective-permute-start | bytes 49160 | tf_op jit(solution)/shard_map/ppermute | solution.py:26
  24.3 4.6 %collective-permute-start.6 = (f32[2,8,128]{2,1,0:T(8,128)S(1)}, f32[2,8,128]{2,1,0:T(8,128)S(1)}, u32[]{:S(2)}, u32[]{:S(2)}) collective-permute-start(f32[2,8,128]{2,1,0:T(8,128)S(1)} %get-tuple-element.55), channel_id=1, source_target_pairs={{0,2},{2,0},{1,3},{3,1},{4,6},{6,4},{5,7},{7,5},{8,10},{10,8},{9,1... | collective-permute-start | bytes 24584 | tf_op jit(solution)/shard_map/ppermute | solution.py:40
  27.3 1.6 %collective-permute-start.7 = (f32[2,8,128]{2,1,0:T(8,128)S(1)}, f32[2,8,128]{2,1,0:T(8,128)S(1)}, u32[]{:S(2)}, u32[]{:S(2)}) collective-permute-start(f32[2,8,128]{2,1,0:T(8,128)S(1)} %get-tuple-element.56), channel_id=1, source_target_pairs={{2,4},{4,2},{3,5},{5,3},{6,8},{8,6},{7,9},{9,7},{10,12},{12,10},{1... | collective-permute-start | bytes 24584 | tf_op jit(solution)/shard_map/ppermute | solution.py:40

commit v4 on v3

--- a/solution.py
+++ b/solution.py
@@ -207,8 +207,12 @@
     return out + hold * field
 
 
+def mark(marks, i):
+    return marks[i, 0:1, 0:1]
+
+
 def pick(flag, a, b):
-    return jnp.where(flag, a, b)
+    return jnp.where(jnp.broadcast_to(flag, a.shape) > 0.5, a, b)
 
 
 def edges_of(get_row, rows, even_b, two):
@@ -222,12 +226,12 @@
 
 def pack_kernel(two, flags, count, field, down, hold, source, target, weights, *refs):
     rows, cols = down.shape
-    even_b = flags[1] == 0
+    even_b = jnp.full((1, 1), 1 - flags[1]).astype(F32)
     has_next = flags[2]
     nb = source.shape[0]
     n_edges = 2 if two else 1
     pack, edges = refs[0], refs[1 : 1 + n_edges]
-    last_down, hold_out, ids, held, sems = refs[1 + n_edges :]
+    last_down, hold_out, marks, ids, held, sems = refs[1 + n_edges :]
     pairs = [(field.at[c], pack.at[:, c * cols : (c + 1) * cols]) for c in range(2)]
     pairs += [(down, last_down), (source, ids.at[0]), (target, ids.at[1]), (weights, held)]
     pairs += [(hold, hold_out)]
@@ -239,6 +243,10 @@
     block = lax.broadcasted_iota(jnp.int32, (nb, LANES), 0)
     live = jnp.where(block * LANES < count[0, 0] * BLOCK * has_next, 1.0, 0.0)
     parts = [ids[0].astype(F32), ids[1].astype(F32)] + [held[q] * live for q in range(4)]
+    for i in range(2):
+        marks[i] = jnp.full((nb, LANES), 1 - flags[i]).astype(F32)
+    marks[2] = jnp.full((nb, LANES), flags[3]).astype(F32)
+    marks[3] = live
     for i, part in enumerate(parts):
         pack[:nb, 2 * cols + i * LANES : 2 * cols + (i + 1) * LANES] = part
     messages = edges_of(lambda c, r: pack[r : r + 1, c * cols : (c + 1) * cols], rows, even_b, two)
@@ -248,18 +256,13 @@
 
 
 def halves(flags, edge_refs):
-    even_b = flags[1] == 0
+    even_b = mark(flags, 1)
     zero = edge_refs[0][...]
     if len(edge_refs) == 2:
         other = edge_refs[1][...]
     else:
         other = jnp.zeros_like(zero)
     return pick(even_b, other, zero), pick(even_b, zero, other)
-
-
-def live_slots(flags, count, nb):
-    block = lax.broadcasted_iota(jnp.int32, (nb, LANES), 0)
-    return jnp.where(block * LANES < count[0, 0] * BLOCK * flags[2], 1.0, 0.0)
 
 
 def spring_image(field, across, down, hold, above, below, rim):
@@ -313,19 +316,19 @@
 
 
 def first_kernel(
-    two, flags, count, field_ref, base, own, own_lanes, own_high, next_lanes, next_blend, got0, got1, *refs
+    two, flags, field_ref, base, own, own_lanes, own_high, next_lanes, next_blend, got0, got1, *refs
 ):
     refs, (left, next_left, prev_left, lanes, mask) = refs[:-5], refs[-5:]
     out, local_ref, send0, send1, *edges = refs[:-5]
     prev_weights, prev_lanes, prev_high, prev_below, prev_blend = refs[-5:]
-    even, even_b = flags[0] == 0, flags[1] == 0
+    even, even_b = mark(flags, 0), mark(flags, 1)
     nb = own.shape[1]
     rows, cols = field_ref.shape[1:]
     size = own_high.shape[0]
     slot = lambda ref, i: ref[:nb, 2 * cols + i * LANES : 2 * cols + (i + 1) * LANES]
     prev = [pick(even, slot(got1, i), slot(got0, i)) for i in range(6)]
     comp = lambda ref, c: ref[:, c * cols : (c + 1) * cols]
-    weights = [jnp.where(flags[3] > 0, w, 0.0) for w in prev[2:]]
+    weights = [w * flags[2] for w in prev[2:]]
     for q in range(4):
         prev_weights[q] = weights[q]
     hi, lo = hi_lo(prev[1].astype(jnp.int32), rows, cols)
@@ -343,7 +346,7 @@
     mask[...] = one_hot(hi, size)
     load_left([pick(even, comp(got1, c), comp(got0, c)) for c in range(2)], prev_left, 1)
     got_prev = looked_up(prev_left, lanes, mask)
-    live = live_slots(flags, count, nb)
+    live = flags[3]
     pulled = spread_own([live * (own[c] - got_next[c]) for c in range(2)], own_lanes, own_high, rows)
     error = [mid[c] - got_prev[c] for c in range(2)]
     pushed = spread_corners(error, weights, prev_lanes, prev_high, prev_below, rows)
@@ -380,7 +383,6 @@
     two,
     n_edges,
     flags,
-    count,
     field_ref,
     across,
     down,
@@ -402,11 +404,10 @@
     edge_refs = [refs.pop(0) for _ in range(n_edges)]
     earlier = [refs.pop(0) for _ in range(ITERS - 1)] if last else []
     out = refs.pop(0)
-    even, even_b = flags[0] == 0, flags[1] == 0
-    nb = local.shape[2]
+    even, even_b = mark(flags, 0), mark(flags, 1)
     rows, _ = across.shape
     field = [field_ref[0], field_ref[1]]
-    live = live_slots(flags, count, nb)
+    live = flags[3]
     got_next = pick(even, got0[...], got1[...])
     got_prev = pick(even, got1[...], got0[...])
     pulled = spread_own([live * (local[0, c] - got_next[c]) for c in range(2)], own_lanes, own_high, rows)
@@ -522,14 +523,14 @@
     pack, *rest = call(
         functools.partial(pack_kernel, two),
         [SMEM, SMEM] + [HBM] * 6,
-        [(rows, 2 * cols + 6 * LANES)] + [(4, cols)] * n_edges + [(rows, cols)] * 2,
+        [(rows, 2 * cols + 6 * LANES)] + [(4, cols)] * n_edges + [(rows, cols)] * 2 + [(4, nb, LANES)],
         [
             pltpu.VMEM((2, nb, LANES), jnp.int32),
             pltpu.VMEM((4, nb, LANES), F32),
             pltpu.SemaphoreType.DMA((7,)),
         ],
     )(flags, block_count, *in_hbm(rhs, down, hold, source, target, weights))
-    edges, (down, hold) = rest[:n_edges], rest[n_edges:]
+    edges, (down, hold, marks) = rest[:n_edges], rest[n_edges:]
 
     def exchange(to0, to1, edges):
         got1 = swapped_sections(to1, 1)
@@ -546,24 +547,22 @@
     table = lambda *shape: jax.ShapeDtypeStruct(shape, BF16)
     left = lambda sides: pltpu.VMEM((2 * sides * size, 2 * LANES), BF16)
     lanes, mask, blends = (2 * LANES, slots), (size, slots), (2, size, slots)
-    run = lambda kernel, shapes, scratch, *args: call(
-        kernel, [SMEM, SMEM] + [VMEM] * (len(args) - 2), shapes, scratch
-    )(*args)
+    run = lambda kernel, shapes, scratch, *args: call(kernel, [VMEM] * len(args), shapes, scratch)(*args)
     stiff = (across, down, hold)
     basis = [rhs]
 
     got0, got1, got_edges = exchange(pack, pack, edges)
     base, own, rim, own_lanes, own_high, next_lanes, next_blend = call(
         early_kernel,
-        [SMEM] + [VMEM] * (7 + n_edges),
+        [VMEM] * (8 + n_edges),
         [field_shape, message, (1, cols), table(*lanes), table(*mask), table(*lanes), blends],
         [left(1)],
-    )(flags, rhs, *stiff, source, target, weights, *got_edges)
+    )(marks, rhs, *stiff, source, target, weights, *got_edges)
     field, local, to0, to1, *rest = run(
         functools.partial(first_kernel, two),
         common + [(4, nb, LANES), table(*lanes), table(*mask), table(*mask), blends],
         [left(2), left(2), left(1), pltpu.VMEM(lanes, BF16), pltpu.VMEM(mask, BF16)],
-        *(flags, block_count, rhs, base, own, own_lanes, own_high, next_lanes, next_blend, got0, got1),
+        *(marks, rhs, base, own, own_lanes, own_high, next_lanes, next_blend, got0, got1),
     )
     edges, prev = rest[:n_edges], rest[n_edges:]
 
@@ -574,7 +573,7 @@
             functools.partial(step_kernel, last, two, n_edges),
             [field_shape, (n_gz * n_xy, LANES)] if last else common,
             [] if last else [left(2)],
-            *(flags, block_count, field, *stiff, own_lanes, own_high, *prev, local, rim),
+            *(marks, field, *stiff, own_lanes, own_high, *prev, local, rim),
             *(got0, got1, *got_edges),
             *(basis if last else []),
         )

time: 46.9 us -> 45.5 us (0.970)
  Pallas kernels: 11.4 us -> 9.46 us
  waiting for transfers between devices: 9.05 us -> 9.57 us
    pallas_call x4, Pallas kernels: 8.86 us -> 6.94 us  [the longest x3 6.26 us: body(): call(kernel, [VMEM] * len(args), shapes, scratch)(*args)]
    ppermute x6, waiting for transfers between devices: 7.84 us -> 8.36 us  [swapped_sections(): return lax.ppermute(block, ('gz', 'xy'), route)]
  transfers between devices with their start and end apart: 9 -> 9, of which waited for: 4 -> 4; matrix products, arithmetic and copies ran while one was open for 0% -> 0% of each run, Pallas kernels for 3% -> 2%
where the time goes in v4:
time: 45.5 us; the launch traced here: 45.3 us
  blocking collectives  15 us (33%)
  starting transfers between devices  9.78 us (21%)
  waiting for transfers between devices  9.57 us (21%)
  Pallas kernels  9.46 us (21%)
  between operations  1.38 us (3%)
    all_to_all x1, blocking collectives, body(): lax.all_to_all(rest[0].reshape(n_gz * n_xy, 1, LANES), ('gz', 'xy'), 0, 0)  15 us
    ppermute x6, starting transfers between devices, swapped_sections(): return lax.ppermute(block, ('gz', 'xy'), route)  9.64 us
    ppermute x6, waiting for transfers between devices, swapped_sections(): return lax.ppermute(block, ('gz', 'xy'), route)  8.36 us
    pallas_call x3, Pallas kernels, body(): call(kernel, [VMEM] * len(args), shapes, scratch)(*args)  6.26 us
    pallas_call x1, Pallas kernels, body(): call(functools.partial(pack_kernel, two), [SMEM, SMEM] + [HBM] * 6, [(row...  1.6 us
    ppermute x3, waiting for transfers between devices, swapped(): return lax.ppermute(block, axis, route) if route else None  1.21 us
    pallas_call x1, Pallas kernels, body(): call(finish_kernel, [VMEM] * (1 + len(basis)), [field_shape] * 2)  0.91 us
  transfers between devices with their start and end apart: 9, of which 4 were waited for; matrix products, arithmetic and copies ran while one was open for 0% of the time, Pallas kernels for 2%

profile of v4, /device:TPU:0, one launch (start us, length us, event | category | flops | bytes accessed | tf_op | source)
XLA Modules:
  0.0 45.3 jit_solution(14877755429067967224)
XLA Ops:
  1.3 0.1 pad_add_fusion.flags
  1.4 0.0 copy-start
  1.4 1.6 %shard_map.95 = (f32[8,4864]{1,0:T(8,128)S(1)}, f32[4,2048]{1,0:T(4,128)S(1)}, f32[8,2048]{1,0:T(8,128)S(1)}, f32[8,2048]{1,0:T(8,128)S(1)}, f32[4,8,128]{2,1,0:T(8,128)S(1)}) custom-call(s32[4]{0:T(128)S(1)} %pad_add_fusion.flags, s32[1,1]{1,0:T(1,128)S(6)} %copy.15.count, f32[2,8,2048]{2,1,0:T(8,128)} %bitcast.21, f32[8,2048]{1,0:T(8,128)} %bitcast.37, ...), custom_call_target="tpu_custom_call" | custom-call | tf_op jit(solution)/shard_map/pallas_call | solution.py:523
  3.0 0.6 %collective-permute-start.2 = (f32[8,4864]{1,0:T(8,128)S(1)}, f32[8,4864]{1,0:T(8,128)S(1)}, u32[]{:S(2)}, u32[]{:S(2)}) collective-permute-start(f32[8,4864]{1,0:T(8,128)S(1)} %get-tuple-element.43), channel_id=1, source_target_pairs={{2,4},{4,2},{3,5},{5,3},{6,8},{8,6},{7,9},{9,7},{10,12},{12,10},{1... | collective-permute-start | bytes 466952 | tf_op jit(solution)/shard_map/ppermute | solution.py:40
  3.6 4.0 %collective-permute-start.1 = (f32[8,4864]{1,0:T(8,128)S(1)}, f32[8,4864]{1,0:T(8,128)S(1)}, u32[]{:S(2)}, u32[]{:S(2)}) collective-permute-start(f32[8,4864]{1,0:T(8,128)S(1)} %get-tuple-element.43), channel_id=1, source_target_pairs={{0,2},{2,0},{1,3},{3,1},{4,6},{6,4},{5,7},{7,5},{8,10},{10,8},{9,1... | collective-permute-start | bytes 466952 | tf_op jit(solution)/shard_map/ppermute | solution.py:40
  7.5 0.0 collective-permute-start
  7.5 1.2 %collective-permute-done.refs_0_ = f32[4,2048]{1,0:T(4,128)S(1)} collective-permute-done((f32[4,2048]{1,0:T(4,128)S(1)}, f32[4,2048]{1,0:T(4,128)S(1)}, u32[]{:S(2)}, u32[]{:S(2)}) %collective-permute-start) | collective-permute-done | bytes 32800 | tf_op jit(solution)/shard_map/ppermute | solution.py:26
  8.7 0.0 copy-done
  8.7 0.0 copy-done.1
  8.7 0.0 copy-done.2
  8.7 0.0 copy-done.4
  8.8 0.0 copy-done.3
  8.8 0.7 %shard_map.96 = (f32[2,8,2048]{2,1,0:T(8,128)S(1)}, f32[2,8,128]{2,1,0:T(8,128)S(1)}, f32[1,2048]{1,0:T(1,128)S(1)}, bf16[256,1024]{1,0:T(8,128)(2,1)S(1)}, bf16...) custom-call(f32[4,8,128]{2,1,0:T(8,128)S(1)} %get-tuple-element.33.flags, ...), custom_call_target="tpu_custom_call" | custom-call | tf_op jit(solution)/shard_map/pallas_call | solution.py:555
  9.4 0.0 collective-permute-done.2.got1
  9.5 5.1 %collective-permute-done.1.got0 = f32[8,4864]{1,0:T(8,128)S(1)} collective-permute-done((f32[8,4864]{1,0:T(8,128)S(1)}, f32[8,4864]{1,0:T(8,128)S(1)}, u32[]{:S(2)}, u32[]{:S(2)}) %collective-permute-start.1) | collective-permute-done | bytes 155680 | tf_op jit(solution)/shard_map/ppermute | solution.py:40
  14.6 2.9 %shard_map.97 = (f32[2,8,2048]{2,1,0:T(8,128)S(1)}, f32[2,2,8,128]{3,2,1,0:T(8,128)S(1)}, f32[2,8,128]{2,1,0:T(8,128)S(1)}, f32[2,8,128]{2,1,0:T(8,128)S(1)}, f3...) custom-call(f32[4,8,128]{2,1,0:T(8,128)S(1)} %get-tuple-element.33.f, ...), custom_call_target="tpu_custom_call" | custom-call | tf_op jit(solution)/shard_map/pallas_call | solution.py:550
  17.5 0.1 collective-permute-start.5
  17.6 1.8 %collective-permute-start.3 = (f32[2,8,128]{2,1,0:T(8,128)S(1)}, f32[2,8,128]{2,1,0:T(8,128)S(1)}, u32[]{:S(2)}, u32[]{:S(2)}) collective-permute-start(f32[2,8,128]{2,1,0:T(8,128)S(1)} %get-tuple-element.52), channel_id=1, source_target_pairs={{0,2},{2,0},{1,3},{3,1},{4,6},{6,4},{5,7},{7,5},{8,10},{10,8},{9,1... | collective-permute-start | bytes 24584 | tf_op jit(solution)/shard_map/ppermute | solution.py:40
  19.4 0.2 collective-permute-start.4
  19.6 1.7 %collective-permute-done.3.got0 = f32[2,8,128]{2,1,0:T(8,128)S(1)} collective-permute-done((f32[2,8,128]{2,1,0:T(8,128)S(1)}, f32[2,8,128]{2,1,0:T(8,128)S(1)}, u32[]{:S(2)}, u32[]{:S(2)}) %collective-permute-start.3) | collective-permute-done | bytes 8224 | tf_op jit(solution)/shard_map/ppermute | solution.py:40
  21.3 0.0 collective-permute-done.4.got1
  21.3 0.0 collective-permute-done.5.refs_0_
  21.3 1.9 %shard_map.98 = (f32[2,8,2048]{2,1,0:T(8,128)S(1)}, f32[2,2,8,128]{3,2,1,0:T(8,128)S(1)}, f32[2,8,128]{2,1,0:T(8,128)S(1)}, f32[2,8,128]{2,1,0:T(8,128)S(1)}, f32[2,2048]{1,0:T(2,128)S(1)}) custom-call(f32[4,8,128]{2,1,0:T(8,128)S(1)} %get-tuple-element.33.flags, f32[2,8,2048]{2,1,0:T(8,128)S(1)} %get-tuple-element.44.field_ref.refs_2_.refs_1_, ...), custom_call_target="tpu_custom_call" | custom-call | tf_op jit(solution)/shard_map/pallas_call | solution.py:550
  23.2 0.1 collective-permute-start.8
  23.3 3.0 %collective-permute-start.6 = (f32[2,8,128]{2,1,0:T(8,128)S(1)}, f32[2,8,128]{2,1,0:T(8,128)S(1)}, u32[]{:S(2)}, u32[]{:S(2)}) collective-permute-start(f32[2,8,128]{2,1,0:T(8,128)S(1)} %get-tuple-element.57), channel_id=1, source_target_pairs={{0,2},{2,0},{1,3},{3,1},{4,6},{6,4},{5,7},{7,5},{8,10},{10,8},{9,1... | collective-permute-start | bytes 24584 | tf_op jit(solution)/shard_map/ppermute | solution.py:40
  26.3 0.2 collective-permute-start.7
  26.4 1.5 %collective-permute-done.6.got0 = f32[2,8,128]{2,1,0:T(8,128)S(1)} collective-permute-done((f32[2,8,128]{2,1,0:T(8,128)S(1)}, f32[2,8,128]{2,1,0:T(8,128)S(1)}, u32[]{:S(2)}, u32[]{:S(2)}) %collective-permute-start.6) | collective-permute-done | bytes 8224 | tf_op jit(solution)/shard_map/ppermute | solution.py:40
  27.9 0.0 collective-permute-done.7.got1
  27.9 0.0 collective-permute-done.8.refs_0_
  27.9 1.5 %shard_map.99 = (f32[2,8,2048]{2,1,0:T(8,128)S(1)}, f32[32,128]{1,0:T(8,128)S(1)}) custom-call(f32[4,8,128]{2,1,0:T(8,128)S(1)} %get-tuple-element.33.flags, f32[2,8,2048]{2,1,0:T(8,128)S(1)} %get-tuple-element.55.field_ref.refs_2_, f32[8,2048]{1,0:T(8,128)S(1)} %bitcast.28, f32[8,2048]{1,0:T(8,128)S(1)} %get-tuple-element.34.down, ...), custom_call_target="tpu_custom_call" | custom-call | tf_op jit(solution)/shard_map/pallas_call | solution.py:550
  29.4 15.0 %all_to_all.5 = f32[32,1,128]{2,1,0:T(1,128)S(1)} all-to-all(f32[32,1,128]{2,1,0:T(1,128)S(1)} %bitcast.36), channel_id=1, replica_groups=mesh['gz'=16,'xy'=2] {'gz','xy'}, dimensions={0} | all-to-all | bytes 32768 | tf_op jit(solution)/shard_map/all_to_all | solution.py:585
  44.4 0.9 %shard_map.100 = (f32[2,8,2048]{2,1,0:T(8,128)}, f32[2,8,2048]{2,1,0:T(8,128)}) custom-call(f32[32,128]{1,0:T(8,128)S(1)} %bitcast.31, f32[2,8,2048]{2,1,0:T(8,128)S(1)} %bitcast.25, f32[2,8,2048]{2,1,0:T(8,128)S(1)} %get-tuple-element.44.field_ref.refs_2_.refs_1_, f32[2,8,2048]{2,1,0:T(8,128)S(1)} %get-tuple-element.55.field_ref.refs_2_, ...), custom_call_target="tpu_custom_call" | custom-call | tf_op jit(solution)/shard_map/pallas_call | solution.py:587
  (4 shorter events, 0.0 us)
Async XLA Ops:
  1.4 7.4 %copy-start = (f32[2,1,8,2048]{3,2,1,0:T(8,128)S(1)}, f32[2,1,8,2048]{3,2,1,0:T(8,128)}, u32[]{:S(2)}) copy-start(f32[2,1,8,2048]{3,2,1,0:T(8,128)} %param.8) | copy-start | bytes 393220
  1.4 7.4 %copy-start.1 = (f32[1,8,2048]{2,1,0:T(8,128)S(1)}, f32[1,8,2048]{2,1,0:T(8,128)}, u32[]{:S(2)}) copy-start(f32[1,8,2048]{2,1,0:T(8,128)} %param.9) | copy-start | bytes 196612
  1.4 7.4 %copy-start.2 = (f32[4,1,1,1024]{3,2,1,0:T(1,128)S(1)}, f32[4,1,1,1024]{3,2,1,0:T(1,128)}, u32[]{:S(2)}) copy-start(f32[4,1,1,1024]{3,2,1,0:T(1,128)} %param.14) | copy-start | bytes 49156
  3.0 6.5 %collective-permute-start.2 = (f32[8,4864]{1,0:T(8,128)S(1)}, f32[8,4864]{1,0:T(8,128)S(1)}, u32[]{:S(2)}, u32[]{:S(2)}) collective-permute-start(f32[8,4864]{1,0:T(8,128)S(1)} %get-tuple-element.43), channel_id=1, source_target_pairs={{2,4},{4,2},{3,5},{5,3},{6,8},{8,6},{7,9},{9,7},{10,12},{12,10},{1... | collective-permute-start | bytes 466952 | tf_op jit(solution)/shard_map/ppermute | solution.py:40
  3.6 11.0 %collective-permute-start.1 = (f32[8,4864]{1,0:T(8,128)S(1)}, f32[8,4864]{1,0:T(8,128)S(1)}, u32[]{:S(2)}, u32[]{:S(2)}) collective-permute-start(f32[8,4864]{1,0:T(8,128)S(1)} %get-tuple-element.43), channel_id=1, source_target_pairs={{0,2},{2,0},{1,3},{3,1},{4,6},{6,4},{5,7},{7,5},{8,10},{10,8},{9,1... | collective-permute-start | bytes 466952 | tf_op jit(solution)/shard_map/ppermute | solution.py:40
  7.5 1.2 %copy-start.4 = (s32[1,1,1024]{2,1,0:T(1,128)S(1)}, s32[1,1,1024]{2,1,0:T(1,128)}, u32[]{:S(2)}) copy-start(s32[1,1,1024]{2,1,0:T(1,128)} %param.13) | copy-start | bytes 12292
  7.5 1.2 %copy-start.3 = (s32[1,1,1024]{2,1,0:T(1,128)S(1)}, s32[1,1,1024]{2,1,0:T(1,128)}, u32[]{:S(2)}) copy-start(s32[1,1,1024]{2,1,0:T(1,128)} %param.12) | copy-start | bytes 12292
  7.5 1.2 %collective-permute-start = (f32[4,2048]{1,0:T(4,128)S(1)}, f32[4,2048]{1,0:T(4,128)S(1)}, u32[]{:S(2)}, u32[]{:S(2)}) collective-permute-start(f32[4,2048]{1,0:T(4,128)S(1)} %get-tuple-element.36), channel_id=1, source_target_pairs={{0,1},{1,0},{2,3},{3,2},{4,5},{5,4},{6,7},{7,6},{8,9},{9,8},{10,11... | collective-permute-start | bytes 98312 | tf_op jit(solution)/shard_map/ppermute | solution.py:26
  17.5 3.8 %collective-permute-start.5 = (f32[2,2048]{1,0:T(2,128)S(1)}, f32[2,2048]{1,0:T(2,128)S(1)}, u32[]{:S(2)}, u32[]{:S(2)}) collective-permute-start(f32[2,2048]{1,0:T(2,128)S(1)} %get-tuple-element.54), channel_id=1, source_target_pairs={{0,1},{1,0},{2,3},{3,2},{4,5},{5,4},{6,7},{7,6},{8,9},{9,8},{10,11... | collective-permute-start | bytes 49160 | tf_op jit(solution)/shard_map/ppermute | solution.py:26
  17.6 3.7 %collective-permute-start.3 = (f32[2,8,128]{2,1,0:T(8,128)S(1)}, f32[2,8,128]{2,1,0:T(8,128)S(1)}, u32[]{:S(2)}, u32[]{:S(2)}) collective-permute-start(f32[2,8,128]{2,1,0:T(8,128)S(1)} %get-tuple-element.52), channel_id=1, source_target_pairs={{0,2},{2,0},{1,3},{3,1},{4,6},{6,4},{5,7},{7,5},{8,10},{10,8},{9,1... | collective-permute-start | bytes 24584 | tf_op jit(solution)/shard_map/ppermute | solution.py:40
  19.4 1.9 %collective-permute-start.4 = (f32[2,8,128]{2,1,0:T(8,128)S(1)}, f32[2,8,128]{2,1,0:T(8,128)S(1)}, u32[]{:S(2)}, u32[]{:S(2)}) collective-permute-start(f32[2,8,128]{2,1,0:T(8,128)S(1)} %get-tuple-element.53), channel_id=1, source_target_pairs={{2,4},{4,2},{3,5},{5,3},{6,8},{8,6},{7,9},{9,7},{10,12},{12,10},{1... | collective-permute-start | bytes 24584 | tf_op jit(solution)/shard_map/ppermute | solution.py:40
  23.2 4.7 %collective-permute-start.8 = (f32[2,2048]{1,0:T(2,128)S(1)}, f32[2,2048]{1,0:T(2,128)S(1)}, u32[]{:S(2)}, u32[]{:S(2)}) collective-permute-start(f32[2,2048]{1,0:T(2,128)S(1)} %get-tuple-element.59), channel_id=1, source_target_pairs={{0,1},{1,0},{2,3},{3,2},{4,5},{5,4},{6,7},{7,6},{8,9},{9,8},{10,11... | collective-permute-start | bytes 49160 | tf_op jit(solution)/shard_map/ppermute | solution.py:26
  23.3 4.6 %collective-permute-start.6 = (f32[2,8,128]{2,1,0:T(8,128)S(1)}, f32[2,8,128]{2,1,0:T(8,128)S(1)}, u32[]{:S(2)}, u32[]{:S(2)}) collective-permute-start(f32[2,8,128]{2,1,0:T(8,128)S(1)} %get-tuple-element.57), channel_id=1, source_target_pairs={{0,2},{2,0},{1,3},{3,1},{4,6},{6,4},{5,7},{7,5},{8,10},{10,8},{9,1... | collective-permute-start | bytes 24584 | tf_op jit(solution)/shard_map/ppermute | solution.py:40
  26.3 1.6 %collective-permute-start.7 = (f32[2,8,128]{2,1,0:T(8,128)S(1)}, f32[2,8,128]{2,1,0:T(8,128)S(1)}, u32[]{:S(2)}, u32[]{:S(2)}) collective-permute-start(f32[2,8,128]{2,1,0:T(8,128)S(1)} %get-tuple-element.58), channel_id=1, source_target_pairs={{2,4},{4,2},{3,5},{5,3},{6,8},{8,6},{7,9},{9,7},{10,12},{12,10},{1... | collective-permute-start | bytes 24584 | tf_op jit(solution)/shard_map/ppermute | solution.py:40

commit v5 on v4

--- a/solution.py
+++ b/solution.py
@@ -224,35 +224,46 @@
     return out
 
 
-def pack_kernel(two, flags, count, field, down, hold, source, target, weights, *refs):
-    rows, cols = down.shape
-    even_b = jnp.full((1, 1), 1 - flags[1]).astype(F32)
-    has_next = flags[2]
-    nb = source.shape[0]
-    n_edges = 2 if two else 1
-    pack, edges = refs[0], refs[1 : 1 + n_edges]
-    last_down, hold_out, marks, ids, held, sems = refs[1 + n_edges :]
-    pairs = [(field.at[c], pack.at[:, c * cols : (c + 1) * cols]) for c in range(2)]
-    pairs += [(down, last_down), (source, ids.at[0]), (target, ids.at[1]), (weights, held)]
-    pairs += [(hold, hold_out)]
+def prepare_kernel(two, count, field, across, down, hold, source, target, weights, *refs):
+    outs, (left, ids, held, sems) = refs[:-4], refs[-4:]
+    field_out, across_out, down_out, hold_out, up, marks, own_lanes, own_high, *edges = outs
+    pairs = [(source, ids.at[0]), (field, field_out), (down, down_out)]
+    pairs += [(target, ids.at[1]), (weights, held), (across, across_out), (hold, hold_out)]
     copies = [pltpu.make_async_copy(a, b, sems.at[i]) for i, (a, b) in enumerate(pairs)]
     for copy in copies:
         copy.start()
-    for copy in copies:
+    rows, cols = across_out.shape
+    nb, size = ids.shape[1], own_high.shape[0]
+    at_gz, at_xy = lax.axis_index("gz"), lax.axis_index("xy")
+    as_mark = lambda flag: jnp.full((nb, LANES), flag.astype(jnp.int32)).astype(F32)
+    copies[0].wait()
+    hi, lo = hi_lo(ids[0], rows, cols)
+    store_lanes(lo, own_lanes)
+    own_high[...] = one_hot(hi, size)
+    copies[1].wait()
+    load_left([field_out[0], field_out[1]], left, 1)
+    own = looked_up(left, own_lanes, own_high)
+    for copy in copies[2:]:
         copy.wait()
+    has_next = (at_gz < lax.axis_size("gz") - 1).astype(jnp.int32)
     block = lax.broadcasted_iota(jnp.int32, (nb, LANES), 0)
     live = jnp.where(block * LANES < count[0, 0] * BLOCK * has_next, 1.0, 0.0)
-    parts = [ids[0].astype(F32), ids[1].astype(F32)] + [held[q] * live for q in range(4)]
-    for i in range(2):
-        marks[i] = jnp.full((nb, LANES), 1 - flags[i]).astype(F32)
-    marks[2] = jnp.full((nb, LANES), flags[3]).astype(F32)
+    marks[0] = as_mark(1 - lax.rem(at_gz, 2))
+    marks[1] = as_mark(1 - lax.rem(at_xy, 2))
+    marks[2] = as_mark(at_gz > 0)
     marks[3] = live
+    parts = [own[0], own[1], ids[1].astype(F32)] + [held[q] * live for q in range(4)]
     for i, part in enumerate(parts):
-        pack[:nb, 2 * cols + i * LANES : 2 * cols + (i + 1) * LANES] = part
-    messages = edges_of(lambda c, r: pack[r : r + 1, c * cols : (c + 1) * cols], rows, even_b, two)
+        up[:, i * LANES : (i + 1) * LANES] = part
+    even_b = mark(marks, 1)
+    messages = edges_of(lambda c, r: field_out[c, r : r + 1, :], rows, even_b, two)
     for message, edge in zip(messages, edges):
         edge[0:2, :] = message
-        edge[2:3, :] = last_down[rows - 1 : rows, :]
+        edge[2:3, :] = down_out[rows - 1 : rows, :]
+
+
+def tile_of(up, i):
+    return up[:, i * LANES : (i + 1) * LANES]
 
 
 def halves(flags, edge_refs):
@@ -274,26 +285,19 @@
     ]
 
 
-def early_kernel(flags, field_ref, across, down, hold, source, target, weights, *refs):
-    edge_refs = refs[:-8]
-    base, own_ref, rim_ref, own_lanes, own_high, next_lanes, next_blend, left = refs[-8:]
+def early_kernel(flags, field_ref, across, down, hold, up, *refs):
+    edge_refs, (base, rim_ref, next_lanes, next_blend) = refs[:-4], refs[-4:]
     rows, cols = across.shape
-    size = own_high.shape[0]
     field = [field_ref[0], field_ref[1]]
     above, below = halves(flags, edge_refs)
     image = spring_image(field, across, down, hold, above, below, above[2:3, :])
     for c in range(2):
         base[c] = image[c]
     rim_ref[...] = above[2:3, :]
-    hi, lo = hi_lo(source[...], rows, cols)
-    store_lanes(lo, own_lanes)
-    own_high[...] = one_hot(hi, size)
-    hi, lo = hi_lo(target[...], rows, cols)
+    hi, lo = hi_lo(tile_of(up, 2).astype(jnp.int32), rows, cols)
     store_lanes(lo, next_lanes)
     for side in range(2):
-        next_blend[side] = blend(hi, size, weights[side], weights[2 + side])
-    load_left(field, left, 1)
-    own_ref[...] = looked_up(left, own_lanes, own_high)
+        next_blend[side] = blend(hi, next_blend.shape[1], tile_of(up, 3 + side), tile_of(up, 5 + side))
 
 
 def send_on(even, even_b, two, field, own_tables, prev_tables, left, local_ref, send0, send1, *edges):
@@ -316,22 +320,19 @@
 
 
 def first_kernel(
-    two, flags, field_ref, base, own, own_lanes, own_high, next_lanes, next_blend, got0, got1, *refs
+    two, flags, field_ref, base, up, own_lanes, own_high, next_lanes, next_blend, next_field, up0, up1, *refs
 ):
-    refs, (left, next_left, prev_left, lanes, mask) = refs[:-5], refs[-5:]
+    refs, (left, next_left) = refs[:-2], refs[-2:]
     out, local_ref, send0, send1, *edges = refs[:-5]
     prev_weights, prev_lanes, prev_high, prev_below, prev_blend = refs[-5:]
     even, even_b = mark(flags, 0), mark(flags, 1)
-    nb = own.shape[1]
     rows, cols = field_ref.shape[1:]
     size = own_high.shape[0]
-    slot = lambda ref, i: ref[:nb, 2 * cols + i * LANES : 2 * cols + (i + 1) * LANES]
-    prev = [pick(even, slot(got1, i), slot(got0, i)) for i in range(6)]
-    comp = lambda ref, c: ref[:, c * cols : (c + 1) * cols]
-    weights = [w * flags[2] for w in prev[2:]]
+    got_up = pick(even, up1[...], up0[...])
+    weights = [tile_of(got_up, 3 + q) * flags[2] for q in range(4)]
     for q in range(4):
         prev_weights[q] = weights[q]
-    hi, lo = hi_lo(prev[1].astype(jnp.int32), rows, cols)
+    hi, lo = hi_lo(tile_of(got_up, 2).astype(jnp.int32), rows, cols)
     store_lanes(lo, prev_lanes)
     prev_high[...] = one_hot(hi, size)
     prev_below[...] = one_hot(hi, size, 1)
@@ -339,13 +340,10 @@
         prev_blend[side] = blend(hi, size, weights[side], weights[2 + side])
     load_left([field_ref[0], field_ref[1]], left, 2)
     mid = interpolated(left, prev_lanes, prev_blend)
-    load_left([pick(even, comp(got0, c), comp(got1, c)) for c in range(2)], next_left, 2)
+    load_left([next_field[0], next_field[1]], next_left, 2)
     got_next = interpolated(next_left, next_lanes, next_blend)
-    hi, lo = hi_lo(prev[0].astype(jnp.int32), rows, cols)
-    store_lanes(lo, lanes)
-    mask[...] = one_hot(hi, size)
-    load_left([pick(even, comp(got1, c), comp(got0, c)) for c in range(2)], prev_left, 1)
-    got_prev = looked_up(prev_left, lanes, mask)
+    own = [tile_of(up, c) for c in range(2)]
+    got_prev = [tile_of(got_up, c) for c in range(2)]
     live = flags[3]
     pulled = spread_own([live * (own[c] - got_next[c]) for c in range(2)], own_lanes, own_high, rows)
     error = [mid[c] - got_prev[c] for c in range(2)]
@@ -368,25 +366,37 @@
     )
 
 
-def moments_of(pairs):
+def moments_of(pairs, start=0):
     lane = lax.broadcasted_iota(jnp.int32, (1, LANES), 1)
     total = jnp.zeros((1, LANES), F32)
     for i, (u, w) in enumerate(pairs):
         s = u[0] * w[0] + u[1] * w[1]
         s = jnp.sum(jnp.sum(s, axis=0, keepdims=True), axis=1, keepdims=True)
-        total = total + jnp.where(lane == i, s, 0.0)
+        total = total + jnp.where(lane == start + i, s, 0.0)
     return total
+
+
+def between_kernel(last, n_edges, flags, field_ref, across, down, hold, rim, *refs):
+    refs = list(refs)
+    edge_refs = [refs.pop(0) for _ in range(n_edges)]
+    earlier = [refs.pop(0) for _ in range(ITERS - 1)] if last else []
+    field = [field_ref[0], field_ref[1]]
+    above, below = halves(flags, edge_refs)
+    image = spring_image(field, across, down, hold, above, below, rim[...])
+    base = refs.pop(0)
+    for c in range(2):
+        base[c] = image[c]
+    if last:
+        basis = [(ref[0], ref[1]) for ref in earlier] + [field]
+        refs.pop(0)[...] = moments_of([(basis[i // 2], basis[i - i // 2]) for i in range(2 * ITERS - 1)])
 
 
 def step_kernel(
     last,
     two,
-    n_edges,
     flags,
     field_ref,
-    across,
-    down,
-    hold,
+    base,
     own_lanes,
     own_high,
     prev_weights,
@@ -395,18 +405,15 @@
     prev_below,
     prev_blend,
     local,
-    rim,
     got0,
     got1,
     *refs,
 ):
     refs = list(refs)
-    edge_refs = [refs.pop(0) for _ in range(n_edges)]
-    earlier = [refs.pop(0) for _ in range(ITERS - 1)] if last else []
+    partial = refs.pop(0) if last else None
     out = refs.pop(0)
     even, even_b = mark(flags, 0), mark(flags, 1)
-    rows, _ = across.shape
-    field = [field_ref[0], field_ref[1]]
+    rows = field_ref.shape[1]
     live = flags[3]
     got_next = pick(even, got0[...], got1[...])
     got_prev = pick(even, got1[...], got0[...])
@@ -414,16 +421,15 @@
     error = [local[1, c] - got_prev[c] for c in range(2)]
     weights = [prev_weights[q] for q in range(4)]
     pushed = spread_corners(error, weights, prev_lanes, prev_high, prev_below, rows)
-    above, below = halves(flags, edge_refs)
-    image = spring_image(field, across, down, hold, above, below, rim[...])
-    after = stepped(field_ref, [image[c] + pulled[c] + pushed[c] for c in range(2)])
+    after = stepped(field_ref, [base[c] + pulled[c] + pushed[c] for c in range(2)])
     for c in range(2):
         out[c] = after[c]
     if last:
-        basis = [(ref[0], ref[1]) for ref in earlier] + [field, after]
-        total = moments_of([(basis[i // 2], basis[i - i // 2]) for i in range(2 * ITERS)])
+        lane = lax.broadcasted_iota(jnp.int32, (1, LANES), 1)
+        end = 2 * ITERS - 1
+        newest = moments_of([((field_ref[0], field_ref[1]), after)], end)
         sums = refs.pop(0)
-        sums[...] = jnp.broadcast_to(total, sums.shape)
+        sums[...] = jnp.broadcast_to(jnp.where(lane == end, newest, partial[...]), sums.shape)
     else:
         messages, left = refs[:-1], refs[-1]
         send_on(even, even_b, two, after, (own_lanes, own_high), (prev_lanes, prev_blend), left, *messages)
@@ -514,23 +520,8 @@
     target = target_cell.reshape(nb, LANES)
     weights = corner_weight.reshape(4, nb, LANES)
     n_gz, n_xy = lax.axis_size("gz"), lax.axis_size("xy")
-    at_gz, at_xy = lax.axis_index("gz"), lax.axis_index("xy")
     two = n_xy > 2
-    flags = jnp.stack([at_gz % 2, at_xy % 2, (at_gz < n_gz - 1).astype(jnp.int32), (at_gz > 0).astype(jnp.int32)]).astype(jnp.int32)
     n_edges = 2 if two else 1
-
-    in_hbm = lambda *arrays: [pltpu.with_memory_space_constraint(a, pltpu.HBM) for a in arrays]
-    pack, *rest = call(
-        functools.partial(pack_kernel, two),
-        [SMEM, SMEM] + [HBM] * 6,
-        [(rows, 2 * cols + 6 * LANES)] + [(4, cols)] * n_edges + [(rows, cols)] * 2 + [(4, nb, LANES)],
-        [
-            pltpu.VMEM((2, nb, LANES), jnp.int32),
-            pltpu.VMEM((4, nb, LANES), F32),
-            pltpu.SemaphoreType.DMA((7,)),
-        ],
-    )(flags, block_count, *in_hbm(rhs, down, hold, source, target, weights))
-    edges, (down, hold, marks) = rest[:n_edges], rest[n_edges:]
 
     def exchange(to0, to1, edges):
         got1 = swapped_sections(to1, 1)
@@ -548,34 +539,53 @@
     left = lambda sides: pltpu.VMEM((2 * sides * size, 2 * LANES), BF16)
     lanes, mask, blends = (2 * LANES, slots), (size, slots), (2, size, slots)
     run = lambda kernel, shapes, scratch, *args: call(kernel, [VMEM] * len(args), shapes, scratch)(*args)
+    next_field = lax.ppermute(rhs, "gz", [(i, (i - 1) % n_gz) for i in range(n_gz)])
+    in_hbm = lambda *arrays: [pltpu.with_memory_space_constraint(a, pltpu.HBM) for a in arrays]
+    grid = (rows, cols)
+    rhs, across, down, hold, up, marks, own_lanes, own_high, *edges = call(
+        functools.partial(prepare_kernel, two),
+        [SMEM] + [HBM] * 7,
+        [field_shape, grid, grid, grid, (nb, 7 * LANES), (4, nb, LANES), table(*lanes), table(*mask)]
+        + [(4, cols)] * n_edges,
+        [
+            left(1),
+            pltpu.VMEM((2, nb, LANES), jnp.int32),
+            pltpu.VMEM((4, nb, LANES), F32),
+            pltpu.SemaphoreType.DMA((7,)),
+        ],
+    )(block_count, *in_hbm(rhs, across, down, hold, source, target, weights))
     stiff = (across, down, hold)
     basis = [rhs]
-
-    got0, got1, got_edges = exchange(pack, pack, edges)
-    base, own, rim, own_lanes, own_high, next_lanes, next_blend = call(
-        early_kernel,
-        [VMEM] * (8 + n_edges),
-        [field_shape, message, (1, cols), table(*lanes), table(*mask), table(*lanes), blends],
-        [left(1)],
-    )(marks, rhs, *stiff, source, target, weights, *got_edges)
+    up1 = swapped_sections(up, 1)
+    up0 = swapped_sections(up, 0)
+    got_edges = []
+    for i, edge in enumerate(edges):
+        got_edges.append(swapped(edge, "xy", i))
+    base, rim, next_lanes, next_blend = run(
+        early_kernel, [field_shape, (1, cols), table(*lanes), blends], [], *(marks, rhs, *stiff, up, *got_edges)
+    )
     field, local, to0, to1, *rest = run(
         functools.partial(first_kernel, two),
         common + [(4, nb, LANES), table(*lanes), table(*mask), table(*mask), blends],
-        [left(2), left(2), left(1), pltpu.VMEM(lanes, BF16), pltpu.VMEM(mask, BF16)],
-        *(marks, rhs, base, own, own_lanes, own_high, next_lanes, next_blend, got0, got1),
+        [left(2), left(2)],
+        *(marks, rhs, base, up, own_lanes, own_high, next_lanes, next_blend, next_field, up0, up1),
     )
     edges, prev = rest[:n_edges], rest[n_edges:]
 
     for step in range(1, ITERS):
         last = step == ITERS - 1
         got0, got1, got_edges = exchange(to0, to1, edges)
+        base, *partial = run(
+            functools.partial(between_kernel, last, n_edges),
+            [field_shape] + ([(1, LANES)] if last else []),
+            [],
+            *(marks, field, *stiff, rim, *got_edges, *(basis if last else [])),
+        )
         field_next, *rest = run(
-            functools.partial(step_kernel, last, two, n_edges),
+            functools.partial(step_kernel, last, two),
             [field_shape, (n_gz * n_xy, LANES)] if last else common,
             [] if last else [left(2)],
-            *(marks, field, *stiff, own_lanes, own_high, *prev, local, rim),
-            *(got0, got1, *got_edges),
-            *(basis if last else []),
+            *(marks, field, base, own_lanes, own_high, *prev, local, got0, got1, *partial),
         )
         basis.append(field)
         field = field_next

time: 45.5 us -> 43.3 us (0.952)
  waiting for transfers between devices: 9.57 us -> 7.65 us
  starting transfers between devices: 9.78 us -> 11.4 us
  blocking collectives: 15 us -> 13.5 us
    ppermute x0 -> x1, starting transfers between devices: none -> 7.01 us  [body(): lax.ppermute(rhs, 'gz', [(i, (i - 1) % n_gz) for i in range(n_gz)])]
    ppermute x6, starting transfers between devices: 9.64 us -> 4.13 us  [swapped_sections(): return lax.ppermute(block, ('gz', 'xy'), route)]
    ppermute x6, waiting for transfers between devices: 8.36 us -> 6.29 us  [swapped_sections(): return lax.ppermute(block, ('gz', 'xy'), route)]
    all_to_all x1, blocking collectives: 15 us -> 13.5 us  [body(): lax.all_to_all(rest[0].reshape(n_gz * n_xy, 1, LANES), ('gz', 'xy'), 0, 0)]
    pallas_call x2 -> x1, Pallas kernels: 2.29 us -> 1.42 us  [body(): call(functools.partial(prepare_kernel, two), [SMEM] + [HBM] * 7, [field_s...]
    pallas_call x3 -> x6, Pallas kernels: 6.26 us -> 6.81 us  [body(): call(kernel, [VMEM] * len(args), shapes, scratch)(*args)]
  transfers between devices with their start and end apart: 9 -> 10, of which waited for: 4 -> 5; matrix products, arithmetic and copies ran while one was open for 0% -> 0% of each run, Pallas kernels for 2% -> 5%
where the time goes in v5:
time: 43.3 us; the launch traced here: 43.1 us
  blocking collectives  13.5 us (31%)
  starting transfers between devices  11.4 us (26%)
  Pallas kernels  9.14 us (21%)
  waiting for transfers between devices  7.65 us (18%)
  between operations  1.37 us (3%)
    all_to_all x1, blocking collectives, body(): lax.all_to_all(rest[0].reshape(n_gz * n_xy, 1, LANES), ('gz', 'xy'), 0, 0)  13.5 us
    ppermute x1, starting transfers between devices, body(): lax.ppermute(rhs, 'gz', [(i, (i - 1) % n_gz) for i in range(n_gz)])  7.01 us
    pallas_call x6, Pallas kernels, body(): call(kernel, [VMEM] * len(args), shapes, scratch)(*args)  6.81 us
    ppermute x6, waiting for transfers between devices, swapped_sections(): return lax.ppermute(block, ('gz', 'xy'), route)  6.29 us
    ppermute x6, starting transfers between devices, swapped_sections(): return lax.ppermute(block, ('gz', 'xy'), route)  4.13 us
    pallas_call x1, Pallas kernels, body(): call(functools.partial(prepare_kernel, two), [SMEM] + [HBM] * 7, [field_s...  1.42 us
    ppermute x3, waiting for transfers between devices, swapped(): return lax.ppermute(block, axis, route) if route else None  1.37 us
    pallas_call x1, Pallas kernels, body(): call(finish_kernel, [VMEM] * (1 + len(basis)), [field_shape] * 2)  0.91 us
  transfers between devices with their start and end apart: 10, of which 5 were waited for; matrix products, arithmetic and copies ran while one was open for 0% of the time, Pallas kernels for 5%

profile of v5, /device:TPU:0, one launch (start us, length us, event | category | flops | bytes accessed | tf_op | source)
XLA Modules:
  0.0 43.1 jit_solution(4543177315591046688)
XLA Ops:
  0.6 7.0 %collective-permute-start.1 = (f32[2,8,2048]{2,1,0:T(8,128)}, f32[2,8,2048]{2,1,0:T(8,128)S(1)}, u32[]{:S(2)}, u32[]{:S(2)}) collective-permute-start(f32[2,8,2048]{2,1,0:T(8,128)} %bitcast.19), channel_id=1, source_target_pairs={{0,30},{2,0},{4,2},{6,4},{8,6},{10,8},{12,10},{14,12},{16,14},{18,... | collective-permute-start | bytes 393224 | tf_op jit(solution)/shard_map/ppermute | solution.py:542
  8.3 1.4 %shard_map.95 = (f32[2,8,2048]{2,1,0:T(8,128)S(1)}, f32[8,2048]{1,0:T(8,128)S(1)}, f32[8,2048]{1,0:T(8,128)S(1)}, f32[8,2048]{1,0:T(8,128)S(1)}, f32[8,896]{1,0:...) custom-call(s32[1,1]{1,0:T(1,128)S(6)} %copy.15.count, ...), custom_call_target="tpu_custom_call" | custom-call | tf_op jit(solution)/shard_map/pallas_call | solution.py:545
  9.7 0.1 collective-permute-start
  9.8 0.5 %collective-permute-start.3 = (f32[8,896]{1,0:T(8,128)S(1)}, f32[8,896]{1,0:T(8,128)S(1)}, u32[]{:S(2)}, u32[]{:S(2)}) collective-permute-start(f32[8,896]{1,0:T(8,128)S(1)} %get-tuple-element.41.up), channel_id=1, source_target_pairs={{2,4},{4,2},{3,5},{5,3},{6,8},{8,6},{7,9},{9,7},{10,12},{12,10},{1... | collective-permute-start | bytes 86024 | tf_op jit(solution)/shard_map/ppermute | solution.py:40
  10.3 0.0 collective-permute-start.2
  10.3 0.7 %collective-permute-done.refs_0_ = f32[4,2048]{1,0:T(4,128)S(1)} collective-permute-done((f32[4,2048]{1,0:T(4,128)S(1)}, f32[4,2048]{1,0:T(4,128)S(1)}, u32[]{:S(2)}, u32[]{:S(2)}) %collective-permute-start) | collective-permute-done | bytes 32800 | tf_op jit(solution)/shard_map/ppermute | solution.py:26
  11.0 0.5 %shard_map.96 = (f32[2,8,2048]{2,1,0:T(8,128)S(1)}, f32[1,2048]{1,0:T(1,128)S(1)}, bf16[256,1024]{1,0:T(8,128)(2,1)S(1)}, f32[2,128,1024]{2,1,0:T(8,128)S(1)}) custom-call(f32[4,8,128]{2,1,0:T(8,128)S(1)} %get-tuple-element.36.flags, f32[2,8,2048]{2,1,0:T(8,128)S(1)} %get-tuple-element.37.field_ref.refs_1_.refs_0_, f32[8,2048]{1,0:T(8,128)S(1)} %get-tuple-element.38.across, ...), custom_call_target="tpu_custom_call" | custom-call | tf_op jit(solution)/shard_map/pallas_call | solution.py:541
  11.5 0.0 collective-permute-done.3.up1
  11.5 2.7 %collective-permute-done.2.up0 = f32[8,896]{1,0:T(8,128)S(1)} collective-permute-done((f32[8,896]{1,0:T(8,128)S(1)}, f32[8,896]{1,0:T(8,128)S(1)}, u32[]{:S(2)}, u32[]{:S(2)}) %collective-permute-start.2) | collective-permute-done | bytes 28704 | tf_op jit(solution)/shard_map/ppermute | solution.py:40
  14.2 0.0 collective-permute-done.1.next_field
  14.2 2.8 %shard_map.97 = (f32[2,8,2048]{2,1,0:T(8,128)S(1)}, f32[2,2,8,128]{3,2,1,0:T(8,128)S(1)}, f32[2,8,128]{2,1,0:T(8,128)S(1)}, f32[2,8,128]{2,1,0:T(8,128)S(1)}, f3...) custom-call(f32[4,8,128]{2,1,0:T(8,128)S(1)} %get-tuple-element.36.f, ...), custom_call_target="tpu_custom_call" | custom-call | tf_op jit(solution)/shard_map/pallas_call | solution.py:541
  17.0 0.1 collective-permute-start.4
  17.1 0.1 collective-permute-start.5
  17.1 0.4 collective-permute-start.6
  17.6 0.7 %collective-permute-done.4.refs_0_ = f32[2,2048]{1,0:T(2,128)S(1)} collective-permute-done((f32[2,2048]{1,0:T(2,128)S(1)}, f32[2,2048]{1,0:T(2,128)S(1)}, u32[]{:S(2)}, u32[]{:S(2)}) %collective-permute-start.4) | collective-permute-done | bytes 16416 | tf_op jit(solution)/shard_map/ppermute | solution.py:26
  18.2 0.2 shard_map.98.base
  18.4 2.4 %collective-permute-done.5.got0 = f32[2,8,128]{2,1,0:T(8,128)S(1)} collective-permute-done((f32[2,8,128]{2,1,0:T(8,128)S(1)}, f32[2,8,128]{2,1,0:T(8,128)S(1)}, u32[]{:S(2)}, u32[]{:S(2)}) %collective-permute-start.5) | collective-permute-done | bytes 8224 | tf_op jit(solution)/shard_map/ppermute | solution.py:40
  20.8 0.0 collective-permute-done.6.got1
  20.8 1.8 %shard_map.99 = (f32[2,8,2048]{2,1,0:T(8,128)S(1)}, f32[2,2,8,128]{3,2,1,0:T(8,128)S(1)}, f32[2,8,128]{2,1,0:T(8,128)S(1)}, f32[2,8,128]{2,1,0:T(8,128)S(1)}, f32[2,2048]{1,0:T(2,128)S(1)}) custom-call(f32[4,8,128]{2,1,0:T(8,128)S(1)} %get-tuple-element.36.flags, f32[2,8,2048]{2,1,0:T(8,128)S(1)} %get-tuple-element.48.field_ref.refs_2_.refs_1_, ...), custom_call_target="tpu_custom_call" | custom-call | tf_op jit(solution)/shard_map/pallas_call | solution.py:541
  22.6 0.1 collective-permute-start.7
  22.7 3.0 %collective-permute-start.8 = (f32[2,8,128]{2,1,0:T(8,128)S(1)}, f32[2,8,128]{2,1,0:T(8,128)S(1)}, u32[]{:S(2)}, u32[]{:S(2)}) collective-permute-start(f32[2,8,128]{2,1,0:T(8,128)S(1)} %get-tuple-element.63), channel_id=1, source_target_pairs={{0,2},{2,0},{1,3},{3,1},{4,6},{6,4},{5,7},{7,5},{8,10},{10,8},{9,1... | collective-permute-start | bytes 24584 | tf_op jit(solution)/shard_map/ppermute | solution.py:40
  25.7 0.2 collective-permute-start.9
  25.8 0.0 collective-permute-done.7.refs_0_
  25.8 0.2 shard_map.100
  26.1 1.2 %collective-permute-done.8.got0 = f32[2,8,128]{2,1,0:T(8,128)S(1)} collective-permute-done((f32[2,8,128]{2,1,0:T(8,128)S(1)}, f32[2,8,128]{2,1,0:T(8,128)S(1)}, u32[]{:S(2)}, u32[]{:S(2)}) %collective-permute-start.8) | collective-permute-done | bytes 8224 | tf_op jit(solution)/shard_map/ppermute | solution.py:40
  27.3 0.0 collective-permute-done.9.got1
  27.3 1.3 %shard_map.101 = (f32[2,8,2048]{2,1,0:T(8,128)S(1)}, f32[32,128]{1,0:T(8,128)S(1)}) custom-call(f32[4,8,128]{2,1,0:T(8,128)S(1)} %get-tuple-element.36.flags, f32[2,8,2048]{2,1,0:T(8,128)S(1)} %get-tuple-element.59.field_ref.refs_2_, f32[2,8,2048]{2,1,0:T(8,128)S(1)} %get-tuple-element.61.base, bf16[256,1024]{1,0:T(8,128)(2,1)S(1)} %get-tuple-element.44.own_lanes, ...), custom_call_target="tpu_custom_call" | custom-call | tf_op jit(solution)/shard_map/pallas_call | solution.py:541
  28.6 13.5 %all_to_all.5 = f32[32,1,128]{2,1,0:T(1,128)S(1)} all-to-all(f32[32,1,128]{2,1,0:T(1,128)S(1)} %bitcast.18), channel_id=1, replica_groups=mesh['gz'=16,'xy'=2] {'gz','xy'}, dimensions={0} | all-to-all | bytes 32768 | tf_op jit(solution)/shard_map/all_to_all | solution.py:595
  42.2 0.9 %shard_map.102 = (f32[2,8,2048]{2,1,0:T(8,128)}, f32[2,8,2048]{2,1,0:T(8,128)}) custom-call(f32[32,128]{1,0:T(8,128)S(1)} %bitcast.17, f32[2,8,2048]{2,1,0:T(8,128)S(1)} %get-tuple-element.37.field_ref.refs_1_.refs_0_, f32[2,8,2048]{2,1,0:T(8,128)S(1)} %get-tuple-element.48.field_ref.refs_2_.refs_1_, f32[2,8,2048]{2,1,0:T(8,128)S(1)} %get-tuple-element.59.field_ref.refs_2_, ...), custom_call_target="tpu_custom_call" | custom-call | tf_op jit(solution)/shard_map/pallas_call | solution.py:597
Async XLA Ops:
  0.6 13.5 %collective-permute-start.1 = (f32[2,8,2048]{2,1,0:T(8,128)}, f32[2,8,2048]{2,1,0:T(8,128)S(1)}, u32[]{:S(2)}, u32[]{:S(2)}) collective-permute-start(f32[2,8,2048]{2,1,0:T(8,128)} %bitcast.19), channel_id=1, source_target_pairs={{0,30},{2,0},{4,2},{6,4},{8,6},{10,8},{12,10},{14,12},{16,14},{18,... | collective-permute-start | bytes 393224 | tf_op jit(solution)/shard_map/ppermute | solution.py:542
  9.7 1.3 %collective-permute-start = (f32[4,2048]{1,0:T(4,128)S(1)}, f32[4,2048]{1,0:T(4,128)S(1)}, u32[]{:S(2)}, u32[]{:S(2)}) collective-permute-start(f32[4,2048]{1,0:T(4,128)S(1)} %get-tuple-element.42), channel_id=1, source_target_pairs={{0,1},{1,0},{2,3},{3,2},{4,5},{5,4},{6,7},{7,6},{8,9},{9,8},{10,11... | collective-permute-start | bytes 98312 | tf_op jit(solution)/shard_map/ppermute | solution.py:26
  9.8 1.7 %collective-permute-start.3 = (f32[8,896]{1,0:T(8,128)S(1)}, f32[8,896]{1,0:T(8,128)S(1)}, u32[]{:S(2)}, u32[]{:S(2)}) collective-permute-start(f32[8,896]{1,0:T(8,128)S(1)} %get-tuple-element.41.up), channel_id=1, source_target_pairs={{2,4},{4,2},{3,5},{5,3},{6,8},{8,6},{7,9},{9,7},{10,12},{12,10},{1... | collective-permute-start | bytes 86024 | tf_op jit(solution)/shard_map/ppermute | solution.py:40
  10.3 3.9 %collective-permute-start.2 = (f32[8,896]{1,0:T(8,128)S(1)}, f32[8,896]{1,0:T(8,128)S(1)}, u32[]{:S(2)}, u32[]{:S(2)}) collective-permute-start(f32[8,896]{1,0:T(8,128)S(1)} %get-tuple-element.41.up), channel_id=1, source_target_pairs={{0,2},{2,0},{1,3},{3,1},{4,6},{6,4},{5,7},{7,5},{8,10},{10,8},{9,1... | collective-permute-start | bytes 86024 | tf_op jit(solution)/shard_map/ppermute | solution.py:40
  17.0 1.2 %collective-permute-start.4 = (f32[2,2048]{1,0:T(2,128)S(1)}, f32[2,2048]{1,0:T(2,128)S(1)}, u32[]{:S(2)}, u32[]{:S(2)}) collective-permute-start(f32[2,2048]{1,0:T(2,128)S(1)} %get-tuple-element.50), channel_id=1, source_target_pairs={{0,1},{1,0},{2,3},{3,2},{4,5},{5,4},{6,7},{7,6},{8,9},{9,8},{10,11... | collective-permute-start | bytes 49160 | tf_op jit(solution)/shard_map/ppermute | solution.py:26
  17.1 3.7 %collective-permute-start.5 = (f32[2,8,128]{2,1,0:T(8,128)S(1)}, f32[2,8,128]{2,1,0:T(8,128)S(1)}, u32[]{:S(2)}, u32[]{:S(2)}) collective-permute-start(f32[2,8,128]{2,1,0:T(8,128)S(1)} %get-tuple-element.57), channel_id=1, source_target_pairs={{0,2},{2,0},{1,3},{3,1},{4,6},{6,4},{5,7},{7,5},{8,10},{10,8},{9,1... | collective-permute-start | bytes 24584 | tf_op jit(solution)/shard_map/ppermute | solution.py:40
  17.1 3.6 %collective-permute-start.6 = (f32[2,8,128]{2,1,0:T(8,128)S(1)}, f32[2,8,128]{2,1,0:T(8,128)S(1)}, u32[]{:S(2)}, u32[]{:S(2)}) collective-permute-start(f32[2,8,128]{2,1,0:T(8,128)S(1)} %get-tuple-element.58), channel_id=1, source_target_pairs={{2,4},{4,2},{3,5},{5,3},{6,8},{8,6},{7,9},{9,7},{10,12},{12,10},{1... | collective-permute-start | bytes 24584 | tf_op jit(solution)/shard_map/ppermute | solution.py:40
  22.6 3.2 %collective-permute-start.7 = (f32[2,2048]{1,0:T(2,128)S(1)}, f32[2,2048]{1,0:T(2,128)S(1)}, u32[]{:S(2)}, u32[]{:S(2)}) collective-permute-start(f32[2,2048]{1,0:T(2,128)S(1)} %get-tuple-element.60), channel_id=1, source_target_pairs={{0,1},{1,0},{2,3},{3,2},{4,5},{5,4},{6,7},{7,6},{8,9},{9,8},{10,11... | collective-permute-start | bytes 49160 | tf_op jit(solution)/shard_map/ppermute | solution.py:26
  22.7 4.6 %collective-permute-start.8 = (f32[2,8,128]{2,1,0:T(8,128)S(1)}, f32[2,8,128]{2,1,0:T(8,128)S(1)}, u32[]{:S(2)}, u32[]{:S(2)}) collective-permute-start(f32[2,8,128]{2,1,0:T(8,128)S(1)} %get-tuple-element.63), channel_id=1, source_target_pairs={{0,2},{2,0},{1,3},{3,1},{4,6},{6,4},{5,7},{7,5},{8,10},{10,8},{9,1... | collective-permute-start | bytes 24584 | tf_op jit(solution)/shard_map/ppermute | solution.py:40
  25.7 1.6 %collective-permute-start.9 = (f32[2,8,128]{2,1,0:T(8,128)S(1)}, f32[2,8,128]{2,1,0:T(8,128)S(1)}, u32[]{:S(2)}, u32[]{:S(2)}) collective-permute-start(f32[2,8,128]{2,1,0:T(8,128)S(1)} %get-tuple-element.64), channel_id=1, source_target_pairs={{2,4},{4,2},{3,5},{5,3},{6,8},{8,6},{7,9},{9,7},{10,12},{12,10},{1... | collective-permute-start | bytes 24584 | tf_op jit(solution)/shard_map/ppermute | solution.py:40

commit v6 on v5

--- a/solution.py
+++ b/solution.py
@@ -11,6 +11,7 @@
 BLOCK = 128
 ITERS = 3
 LANES = 128
+WIDE = 256
 GAIN = 0.25
 SHIFT = 1.25
 F32 = jnp.float32
@@ -54,7 +55,7 @@
 
 def hi_lo(index, rows, cols):
     row, col = div_mod(index, cols)
-    tile, lane = div_mod(col, LANES)
+    tile, lane = div_mod(col, WIDE)
     return tile * rows + row, lane
 
 
@@ -82,14 +83,12 @@
 
 
 def store_lanes(lo, lanes_ref):
-    hot = one_hot(lo, LANES)
-    lanes_ref[0:LANES, :] = hot
-    lanes_ref[LANES : 2 * LANES, :] = hot
+    lanes_ref[...] = one_hot(lo, WIDE)
 
 
 def tall(field):
-    n = field.shape[1] // LANES
-    return jnp.concatenate([field[:, i * LANES : (i + 1) * LANES] for i in range(n)], axis=0)
+    n = field.shape[1] // WIDE
+    return jnp.concatenate([field[:, i * WIDE : (i + 1) * WIDE] for i in range(n)], axis=0)
 
 
 def wide(stack, rows):
@@ -109,8 +108,8 @@
         stack = tall(f)
         high, low = split2(stack)
         n = stack.shape[0]
-        left_ref[i * n : (i + 1) * n, 0:LANES] = high
-        left_ref[i * n : (i + 1) * n, LANES : 2 * LANES] = low
+        left_ref[2 * i * n : (2 * i + 1) * n, :] = high
+        left_ref[(2 * i + 1) * n : (2 * i + 2) * n, :] = low
 
 
 def as_tiles(rows_of):
@@ -124,14 +123,16 @@
     stride = left_ref.shape[0] // 2
     found = ([], [])
     for k in range(0, slots, CHUNK):
-        mask = high_ref[:, k : k + CHUNK].astype(F32)
+        hot = lanes_ref[:, k : k + CHUNK]
+        mask = high_ref[:, k : k + CHUNK]
         for c in range(2):
             got = jnp.dot(
-                left_ref[c * stride : c * stride + high, :],
-                lanes_ref[:, k : k + CHUNK],
+                left_ref[c * stride : c * stride + 2 * high, :],
+                hot,
                 preferred_element_type=F32,
             )
-            found[c].append(jnp.sum(mask * got, axis=0, keepdims=True))
+            value = mask * (got[:high] + got[high:])
+            found[c].append(jnp.sum(value, axis=0, keepdims=True))
     return jnp.stack([as_tiles(f) for f in found])
 
 
@@ -139,15 +140,16 @@
     high, slots = blend_ref.shape[1:]
     found = ([], [])
     for k in range(0, slots, CHUNK):
+        hot = lanes_ref[:, k : k + CHUNK]
         wl = blend_ref[0, :, k : k + CHUNK]
         wr = blend_ref[1, :, k : k + CHUNK]
         for c in range(2):
             got = jnp.dot(
-                left_ref[2 * c * high : 2 * (c + 1) * high, :],
-                lanes_ref[:, k : k + CHUNK],
+                left_ref[4 * c * high : 4 * (c + 1) * high, :],
+                hot,
                 preferred_element_type=F32,
             )
-            value = wl * got[:high] + wr * got[high:]
+            value = wl * (got[:high] + got[high : 2 * high]) + wr * (got[2 * high : 3 * high] + got[3 * high :])
             found[c].append(jnp.sum(value, axis=0, keepdims=True))
     return jnp.stack([as_tiles(f) for f in found])
 
@@ -166,9 +168,9 @@
     high = high_ref.shape[0]
     result = []
     for c in range(2):
-        parts = [scaled(high_ref, part) for part in split2(values[c])]
+        parts = [scaled(high_ref, part.astype(F32)).astype(BF16) for part in split2(values[c])]
         out = lax.dot_general(
-            jnp.concatenate(parts, axis=0), lanes_ref[0:LANES, :], NT, preferred_element_type=F32
+            jnp.concatenate(parts, axis=0), lanes_ref[...], NT, preferred_element_type=F32
         )
         result.append(wide(out[:high] + out[high:], rows))
     return result
@@ -181,9 +183,10 @@
         parts = []
         for side in range(2):
             for up, down in zip(split2(values[c] * weights[side]), split2(values[c] * weights[2 + side])):
-                parts.append(scaled(high_ref, up) + scaled(below_ref, down))
+                part = scaled(high_ref, up.astype(F32)) + scaled(below_ref, down.astype(F32))
+                parts.append(part.astype(BF16))
         out = lax.dot_general(
-            jnp.concatenate(parts, axis=0), lanes_ref[0:LANES, :], NT, preferred_element_type=F32
+            jnp.concatenate(parts, axis=0), lanes_ref[...], NT, preferred_element_type=F32
         )
         sides = [
             wide(out[p * high : (p + 1) * high] + out[(p + 1) * high : (p + 2) * high], rows)
@@ -239,7 +242,7 @@
     copies[0].wait()
     hi, lo = hi_lo(ids[0], rows, cols)
     store_lanes(lo, own_lanes)
-    own_high[...] = one_hot(hi, size)
+    own_high[...] = one_hot(hi, size).astype(F32)
     copies[1].wait()
     load_left([field_out[0], field_out[1]], left, 1)
     own = looked_up(left, own_lanes, own_high)
@@ -300,6 +303,11 @@
         next_blend[side] = blend(hi, next_blend.shape[1], tile_of(up, 3 + side), tile_of(up, 5 + side))
 
 
+def ahead_kernel(next_lanes, next_blend, next_field, out, left):
+    load_left([next_field[0], next_field[1]], left, 2)
+    out[...] = interpolated(left, next_lanes, next_blend)
+
+
 def send_on(even, even_b, two, field, own_tables, prev_tables, left, local_ref, send0, send1, *edges):
     own_lanes, own_high = own_tables
     prev_lanes, prev_blend = prev_tables
@@ -320,9 +328,9 @@
 
 
 def first_kernel(
-    two, flags, field_ref, base, up, own_lanes, own_high, next_lanes, next_blend, next_field, up0, up1, *refs
+    two, flags, field_ref, base, up, own_lanes, own_high, got_next, up0, up1, *refs
 ):
-    refs, (left, next_left) = refs[:-2], refs[-2:]
+    refs, left = refs[:-1], refs[-1]
     out, local_ref, send0, send1, *edges = refs[:-5]
     prev_weights, prev_lanes, prev_high, prev_below, prev_blend = refs[-5:]
     even, even_b = mark(flags, 0), mark(flags, 1)
@@ -334,14 +342,12 @@
         prev_weights[q] = weights[q]
     hi, lo = hi_lo(tile_of(got_up, 2).astype(jnp.int32), rows, cols)
     store_lanes(lo, prev_lanes)
-    prev_high[...] = one_hot(hi, size)
-    prev_below[...] = one_hot(hi, size, 1)
+    prev_high[...] = one_hot(hi, size).astype(F32)
+    prev_below[...] = one_hot(hi, size, 1).astype(F32)
     for side in range(2):
         prev_blend[side] = blend(hi, size, weights[side], weights[2 + side])
     load_left([field_ref[0], field_ref[1]], left, 2)
     mid = interpolated(left, prev_lanes, prev_blend)
-    load_left([next_field[0], next_field[1]], next_left, 2)
-    got_next = interpolated(next_left, next_lanes, next_blend)
     own = [tile_of(up, c) for c in range(2)]
     got_prev = [tile_of(got_up, c) for c in range(2)]
     live = flags[3]
@@ -387,8 +393,29 @@
     for c in range(2):
         base[c] = image[c]
     if last:
-        basis = [(ref[0], ref[1]) for ref in earlier] + [field]
-        refs.pop(0)[...] = moments_of([(basis[i // 2], basis[i - i // 2]) for i in range(2 * ITERS - 1)])
+        basis = [(ref[0], ref[1]) for ref in earlier] + [field, image]
+        refs.pop(0)[...] = moments_of([(basis[i // 2], basis[i - i // 2]) for i in range(2 * ITERS)])
+
+
+def errors_of(flags, local, got0, got1):
+    even, live = mark(flags, 0), flags[3]
+    got_next = pick(even, got0[...], got1[...])
+    got_prev = pick(even, got1[...], got0[...])
+    return (
+        [live * (local[0, c] - got_next[c]) for c in range(2)],
+        [local[1, c] - got_prev[c] for c in range(2)],
+    )
+
+
+def sum_kernel(flags, partial, local, got0, got1, sums):
+    own, prev = errors_of(flags, local, got0, got1)
+    s = own[0] * local[0, 0] + own[1] * local[0, 1] + prev[0] * local[1, 0] + prev[1] * local[1, 1]
+    s = jnp.sum(jnp.sum(s, axis=0, keepdims=True), axis=1, keepdims=True)
+    lane = lax.broadcasted_iota(jnp.int32, (1, LANES), 1)
+    at = 2 * ITERS - 1
+    before = jnp.sum(jnp.where(lane == at - 1, partial[...], 0.0), axis=1, keepdims=True)
+    total = jnp.where(lane == at, GAIN * (partial[...] + s) - SHIFT * before, partial[...])
+    sums[...] = jnp.broadcast_to(total, sums.shape)
 
 
 def step_kernel(
@@ -407,30 +434,19 @@
     local,
     got0,
     got1,
+    out,
     *refs,
 ):
-    refs = list(refs)
-    partial = refs.pop(0) if last else None
-    out = refs.pop(0)
-    even, even_b = mark(flags, 0), mark(flags, 1)
     rows = field_ref.shape[1]
-    live = flags[3]
-    got_next = pick(even, got0[...], got1[...])
-    got_prev = pick(even, got1[...], got0[...])
-    pulled = spread_own([live * (local[0, c] - got_next[c]) for c in range(2)], own_lanes, own_high, rows)
-    error = [local[1, c] - got_prev[c] for c in range(2)]
+    error, error_prev = errors_of(flags, local, got0, got1)
+    pulled = spread_own(error, own_lanes, own_high, rows)
     weights = [prev_weights[q] for q in range(4)]
-    pushed = spread_corners(error, weights, prev_lanes, prev_high, prev_below, rows)
+    pushed = spread_corners(error_prev, weights, prev_lanes, prev_high, prev_below, rows)
     after = stepped(field_ref, [base[c] + pulled[c] + pushed[c] for c in range(2)])
     for c in range(2):
         out[c] = after[c]
-    if last:
-        lane = lax.broadcasted_iota(jnp.int32, (1, LANES), 1)
-        end = 2 * ITERS - 1
-        newest = moments_of([((field_ref[0], field_ref[1]), after)], end)
-        sums = refs.pop(0)
-        sums[...] = jnp.broadcast_to(jnp.where(lane == end, newest, partial[...]), sums.shape)
-    else:
+    if not last:
+        even, even_b = mark(flags, 0), mark(flags, 1)
         messages, left = refs[:-1], refs[-1]
         send_on(even, even_b, two, after, (own_lanes, own_high), (prev_lanes, prev_blend), left, *messages)
 
@@ -533,11 +549,11 @@
 
     field_shape = (2, rows, cols)
     message = (2, nb, LANES)
-    size = rows * cols // LANES
+    size = rows * cols // WIDE
     common = [field_shape, (2,) + message, message, message] + [(2, cols)] * n_edges
     table = lambda *shape: jax.ShapeDtypeStruct(shape, BF16)
-    left = lambda sides: pltpu.VMEM((2 * sides * size, 2 * LANES), BF16)
-    lanes, mask, blends = (2 * LANES, slots), (size, slots), (2, size, slots)
+    left = lambda sides: pltpu.VMEM((4 * sides * size, WIDE), BF16)
+    lanes, mask, blends = (WIDE, slots), (size, slots), (2, size, slots)
     run = lambda kernel, shapes, scratch, *args: call(kernel, [VMEM] * len(args), shapes, scratch)(*args)
     next_field = lax.ppermute(rhs, "gz", [(i, (i - 1) % n_gz) for i in range(n_gz)])
     in_hbm = lambda *arrays: [pltpu.with_memory_space_constraint(a, pltpu.HBM) for a in arrays]
@@ -545,7 +561,7 @@
     rhs, across, down, hold, up, marks, own_lanes, own_high, *edges = call(
         functools.partial(prepare_kernel, two),
         [SMEM] + [HBM] * 7,
-        [field_shape, grid, grid, grid, (nb, 7 * LANES), (4, nb, LANES), table(*lanes), table(*mask)]
+        [field_shape, grid, grid, grid, (nb, 7 * LANES), (4, nb, LANES), table(*lanes), mask]
         + [(4, cols)] * n_edges,
         [
             left(1),
@@ -564,11 +580,12 @@
     base, rim, next_lanes, next_blend = run(
         early_kernel, [field_shape, (1, cols), table(*lanes), blends], [], *(marks, rhs, *stiff, up, *got_edges)
     )
+    (got_next,) = run(ahead_kernel, [message], [left(2)], next_lanes, next_blend, next_field)
     field, local, to0, to1, *rest = run(
         functools.partial(first_kernel, two),
-        common + [(4, nb, LANES), table(*lanes), table(*mask), table(*mask), blends],
-        [left(2), left(2)],
-        *(marks, rhs, base, up, own_lanes, own_high, next_lanes, next_blend, next_field, up0, up1),
+        common + [(4, nb, LANES), table(*lanes), mask, mask, blends],
+        [left(2)],
+        *(marks, rhs, base, up, own_lanes, own_high, got_next, up0, up1),
     )
     edges, prev = rest[:n_edges], rest[n_edges:]
 
@@ -581,19 +598,21 @@
             [],
             *(marks, field, *stiff, rim, *got_edges, *(basis if last else [])),
         )
+        if last:
+            (sums,) = run(sum_kernel, [(n_gz * n_xy, LANES)], [], marks, *partial, local, got0, got1)
+            sums = lax.all_to_all(sums.reshape(n_gz * n_xy, 1, LANES), ("gz", "xy"), 0, 0)
+            sums = sums.reshape(n_gz * n_xy, LANES)
         field_next, *rest = run(
             functools.partial(step_kernel, last, two),
-            [field_shape, (n_gz * n_xy, LANES)] if last else common,
+            [field_shape] if last else common,
             [] if last else [left(2)],
-            *(marks, field, base, own_lanes, own_high, *prev, local, got0, got1, *partial),
+            *(marks, field, base, own_lanes, own_high, *prev, local, got0, got1),
         )
         basis.append(field)
         field = field_next
         if not last:
             local, to0, to1, *edges = rest
     basis.append(field)
-    sums = lax.all_to_all(rest[0].reshape(n_gz * n_xy, 1, LANES), ("gz", "xy"), 0, 0)
-    sums = sums.reshape(n_gz * n_xy, LANES)
     solution_field, residual = call(finish_kernel, [VMEM] * (1 + len(basis)), [field_shape] * 2)(sums, *basis)
     return solution_field[:, None], residual[:, None]
 

time: 43.3 us -> 41.6 us (0.961)
  blocking collectives: 13.5 us -> 0 us
  starting transfers between devices: 11.4 us -> 17.9 us
  waiting for transfers between devices: 7.65 us -> 13.2 us
    all_to_all x1 -> x0, blocking collectives: 13.5 us -> none  [body(): lax.all_to_all(rest[0].reshape(n_gz * n_xy, 1, LANES), ('gz', 'xy'), 0, 0)]
    all_to_all x0 -> x1, starting transfers between devices: none -> 6.56 us  [body(): lax.all_to_all(sums.reshape(n_gz * n_xy, 1, LANES), ('gz', 'xy'), 0, 0)]
    all_to_all x0 -> x1, waiting for transfers between devices: none -> 6.16 us  [body(): lax.all_to_all(sums.reshape(n_gz * n_xy, 1, LANES), ('gz', 'xy'), 0, 0)]
    ppermute x6, waiting for transfers between devices: 6.29 us -> 5.7 us  [swapped_sections(): return lax.ppermute(block, ('gz', 'xy'), route)]
    pallas_call x6 -> x8, Pallas kernels: 6.81 us -> 6.49 us  [body(): call(kernel, [VMEM] * len(args), shapes, scratch)(*args)]
  transfers between devices with their start and end apart: 10 -> 11, of which waited for: 5 -> 6; matrix products, arithmetic and copies ran while one was open for 0% -> 0% of each run, Pallas kernels for 5% -> 9%
where the time goes in v6:
time: 41.6 us; the launch traced here: 41.4 us
  starting transfers between devices  17.9 us (43%)
  waiting for transfers between devices  13.2 us (32%)
  Pallas kernels  8.81 us (21%)
  between operations  1.4 us (3%)
    ppermute x1, starting transfers between devices, body(): lax.ppermute(rhs, 'gz', [(i, (i - 1) % n_gz) for i in range(n_gz)])  7.01 us
    all_to_all x1, starting transfers between devices, body(): lax.all_to_all(sums.reshape(n_gz * n_xy, 1, LANES), ('gz', 'xy'), 0, 0)  6.56 us
    pallas_call x8, Pallas kernels, body(): call(kernel, [VMEM] * len(args), shapes, scratch)(*args)  6.49 us
    all_to_all x1, waiting for transfers between devices, body(): lax.all_to_all(sums.reshape(n_gz * n_xy, 1, LANES), ('gz', 'xy'), 0, 0)  6.16 us
    ppermute x6, waiting for transfers between devices, swapped_sections(): return lax.ppermute(block, ('gz', 'xy'), route)  5.7 us
    ppermute x6, starting transfers between devices, swapped_sections(): return lax.ppermute(block, ('gz', 'xy'), route)  4.13 us
    pallas_call x1, Pallas kernels, body(): call(functools.partial(prepare_kernel, two), [SMEM] + [HBM] * 7, [field_s...  1.41 us
    ppermute x3, waiting for transfers between devices, swapped(): return lax.ppermute(block, axis, route) if route else None  1.37 us
  transfers between devices with their start and end apart: 11, of which 6 were waited for; matrix products, arithmetic and copies ran while one was open for 0% of the time, Pallas kernels for 9%

profile of v6, /device:TPU:0, one launch (start us, length us, event | category | flops | bytes accessed | tf_op | source)
XLA Modules:
  0.0 41.4 jit_solution(602301582934132839)
XLA Ops:
  0.6 7.0 %collective-permute-start.1 = (f32[2,8,2048]{2,1,0:T(8,128)}, f32[2,8,2048]{2,1,0:T(8,128)S(1)}, u32[]{:S(2)}, u32[]{:S(2)}) collective-permute-start(f32[2,8,2048]{2,1,0:T(8,128)} %bitcast.18), channel_id=1, source_target_pairs={{0,30},{2,0},{4,2},{6,4},{8,6},{10,8},{12,10},{14,12},{16,14},{18,... | collective-permute-start | bytes 393224 | tf_op jit(solution)/shard_map/ppermute | solution.py:558
  8.3 1.4 %shard_map.95 = (f32[2,8,2048]{2,1,0:T(8,128)S(1)}, f32[8,2048]{1,0:T(8,128)S(1)}, f32[8,2048]{1,0:T(8,128)S(1)}, f32[8,2048]{1,0:T(8,128)S(1)}, f32[8,896]{1,0:...) custom-call(s32[1,1]{1,0:T(1,128)S(6)} %copy.15.count, ...), custom_call_target="tpu_custom_call" | custom-call | tf_op jit(solution)/shard_map/pallas_call | solution.py:561
  9.7 0.1 collective-permute-start
  9.8 0.5 %collective-permute-start.3 = (f32[8,896]{1,0:T(8,128)S(1)}, f32[8,896]{1,0:T(8,128)S(1)}, u32[]{:S(2)}, u32[]{:S(2)}) collective-permute-start(f32[8,896]{1,0:T(8,128)S(1)} %get-tuple-element.39.up), channel_id=1, source_target_pairs={{2,4},{4,2},{3,5},{5,3},{6,8},{8,6},{7,9},{9,7},{10,12},{12,10},{1... | collective-permute-start | bytes 86024 | tf_op jit(solution)/shard_map/ppermute | solution.py:41
  10.3 0.0 collective-permute-start.2
  10.3 0.7 %collective-permute-done.refs_0_ = f32[4,2048]{1,0:T(4,128)S(1)} collective-permute-done((f32[4,2048]{1,0:T(4,128)S(1)}, f32[4,2048]{1,0:T(4,128)S(1)}, u32[]{:S(2)}, u32[]{:S(2)}) %collective-permute-start) | collective-permute-done | bytes 32800 | tf_op jit(solution)/shard_map/ppermute | solution.py:27
  11.0 0.4 %shard_map.96 = (f32[2,8,2048]{2,1,0:T(8,128)S(1)}, f32[1,2048]{1,0:T(1,128)S(1)}, bf16[256,1024]{1,0:T(8,128)(2,1)S(1)}, f32[2,64,1024]{2,1,0:T(8,128)S(1)}) custom-call(f32[4,8,128]{2,1,0:T(8,128)S(1)} %get-tuple-element.34.flags, f32[2,8,2048]{2,1,0:T(8,128)S(1)} %get-tuple-element.35.field_ref.refs_1_.refs_0_, f32[8,2048]{1,0:T(8,128)S(1)} %get-tuple-element.36.across, ...), custom_call_target="tpu_custom_call" | custom-call | tf_op jit(solution)/shard_map/pallas_call | solution.py:557
  11.4 0.0 collective-permute-done.1.next_field
  11.4 0.5 %shard_map.97.got_next = f32[2,8,128]{2,1,0:T(8,128)S(1)} custom-call(bf16[256,1024]{1,0:T(8,128)(2,1)S(1)} %get-tuple-element.44.next_lanes, f32[2,64,1024]{2,1,0:T(8,128)S(1)} %get-tuple-element.45.next_blend, f32[2,8,2048]{2,1,0:T(8,128)S(1)} %collective-permute-done.1.next_field), custom_call_target="tpu_custom_call" | custom-call | tf_op jit(solution)/shard_map/pallas_call | solution.py:557
  11.9 0.0 collective-permute-done.3.up1
  11.9 2.2 %collective-permute-done.2.up0 = f32[8,896]{1,0:T(8,128)S(1)} collective-permute-done((f32[8,896]{1,0:T(8,128)S(1)}, f32[8,896]{1,0:T(8,128)S(1)}, u32[]{:S(2)}, u32[]{:S(2)}) %collective-permute-start.2) | collective-permute-done | bytes 28704 | tf_op jit(solution)/shard_map/ppermute | solution.py:41
  14.2 1.9 %shard_map.98 = (f32[2,8,2048]{2,1,0:T(8,128)S(1)}, f32[2,2,8,128]{3,2,1,0:T(8,128)S(1)}, f32[2,8,128]{2,1,0:T(8,128)S(1)}, f32[2,8,128]{2,1,0:T(8,128)S(1)}, f3...) custom-call(f32[4,8,128]{2,1,0:T(8,128)S(1)} %get-tuple-element.34.f, ...), custom_call_target="tpu_custom_call" | custom-call | tf_op jit(solution)/shard_map/pallas_call | solution.py:557
  16.1 0.1 collective-permute-start.4
  16.1 0.1 collective-permute-start.5
  16.2 0.4 %collective-permute-start.6 = (f32[2,8,128]{2,1,0:T(8,128)S(1)}, f32[2,8,128]{2,1,0:T(8,128)S(1)}, u32[]{:S(2)}, u32[]{:S(2)}) collective-permute-start(f32[2,8,128]{2,1,0:T(8,128)S(1)} %get-tuple-element.56), channel_id=1, source_target_pairs={{2,4},{4,2},{3,5},{5,3},{6,8},{8,6},{7,9},{9,7},{10,12},{12,10},{1... | collective-permute-start | bytes 24584 | tf_op jit(solution)/shard_map/ppermute | solution.py:41
  16.6 0.7 %collective-permute-done.4.refs_0_ = f32[2,2048]{1,0:T(2,128)S(1)} collective-permute-done((f32[2,2048]{1,0:T(2,128)S(1)}, f32[2,2048]{1,0:T(2,128)S(1)}, u32[]{:S(2)}, u32[]{:S(2)}) %collective-permute-start.4) | collective-permute-done | bytes 16416 | tf_op jit(solution)/shard_map/ppermute | solution.py:27
  17.3 0.2 shard_map.99.base
  17.5 2.4 %collective-permute-done.5.got0 = f32[2,8,128]{2,1,0:T(8,128)S(1)} collective-permute-done((f32[2,8,128]{2,1,0:T(8,128)S(1)}, f32[2,8,128]{2,1,0:T(8,128)S(1)}, u32[]{:S(2)}, u32[]{:S(2)}) %collective-permute-start.5) | collective-permute-done | bytes 8224 | tf_op jit(solution)/shard_map/ppermute | solution.py:41
  19.9 0.0 collective-permute-done.6.got1
  19.9 1.5 %shard_map.100 = (f32[2,8,2048]{2,1,0:T(8,128)S(1)}, f32[2,2,8,128]{3,2,1,0:T(8,128)S(1)}, f32[2,8,128]{2,1,0:T(8,128)S(1)}, f32[2,8,128]{2,1,0:T(8,128)S(1)}, f32[2,2048]{1,0:T(2,128)S(1)}) custom-call(f32[4,8,128]{2,1,0:T(8,128)S(1)} %get-tuple-element.34.flags, f32[2,8,2048]{2,1,0:T(8,128)S(1)} %get-tuple-element.46.field_ref.refs_2_.refs_1_, ...), custom_call_target="tpu_custom_call" | custom-call | tf_op jit(solution)/shard_map/pallas_call | solution.py:557
  21.3 0.1 collective-permute-start.7
  21.4 3.0 %collective-permute-start.8 = (f32[2,8,128]{2,1,0:T(8,128)S(1)}, f32[2,8,128]{2,1,0:T(8,128)S(1)}, u32[]{:S(2)}, u32[]{:S(2)}) collective-permute-start(f32[2,8,128]{2,1,0:T(8,128)S(1)} %get-tuple-element.61), channel_id=1, source_target_pairs={{0,2},{2,0},{1,3},{3,1},{4,6},{6,4},{5,7},{7,5},{8,10},{10,8},{9,1... | collective-permute-start | bytes 24584 | tf_op jit(solution)/shard_map/ppermute | solution.py:41
  24.4 0.2 collective-permute-start.9
  24.6 0.0 collective-permute-done.7.refs_0_
  24.6 0.4 shard_map.101
  24.9 1.1 %collective-permute-done.8.got0 = f32[2,8,128]{2,1,0:T(8,128)S(1)} collective-permute-done((f32[2,8,128]{2,1,0:T(8,128)S(1)}, f32[2,8,128]{2,1,0:T(8,128)S(1)}, u32[]{:S(2)}, u32[]{:S(2)}) %collective-permute-start.8) | collective-permute-done | bytes 8224 | tf_op jit(solution)/shard_map/ppermute | solution.py:41
  26.0 0.0 collective-permute-done.9.got1
  26.0 0.7 %shard_map.102 = f32[32,128]{1,0:T(8,128)} custom-call(f32[4,8,128]{2,1,0:T(8,128)S(1)} %get-tuple-element.34.flags, f32[1,128]{1,0:T(1,128)S(1)} %get-tuple-element.59.partial, f32[2,2,8,128]{3,2,1,0:T(8,128)S(1)} %get-tuple-element.60.local, f32[2,8,128]{2,1,0:T(8,128)S(1)} %collective-permute-done.8.got0, f32[2,8,128]{2,1,0:T(8,128)S(1)} %collective-permute-done.9.got1), custom_call_target="tpu_custom_call" | custom-call | tf_op jit(solution)/shard_map/pallas_call | solution.py:557
  26.8 6.6 %all-to-all-start = ((f32[32,1,128]{2,1,0:T(1,128)}), f32[32,1,128]{2,1,0:T(1,128)S(1)}, u32[]{:S(2)}, u32[]{:S(2)}) async-start(f32[32,1,128]{2,1,0:T(1,128)} %bitcast.8), calls=%async_computation | async-start | bytes 32768 | tf_op jit(solution)/shard_map/all_to_all | solution.py:603
  33.4 0.9 %shard_map.103.refs_3_ = f32[2,8,2048]{2,1,0:T(8,128)S(1)} custom-call(f32[4,8,128]{2,1,0:T(8,128)S(1)} %get-tuple-element.34.flags, f32[2,8,2048]{2,1,0:T(8,128)S(1)} %get-tuple-element.57.field_ref.refs_2_, f32[2,8,2048]{2,1,0:T(8,128)S(1)} %get-tuple-element.63.base, bf16[256,1024]{1,0:T(8,128)(2,1)S(1)} %get-tuple-element.42.own_lanes, ...), custom_call_target="tpu_custom_call" | custom-call | tf_op jit(solution)/shard_map/pallas_call | solution.py:557
  34.3 6.2 %all-to-all-done = f32[32,1,128]{2,1,0:T(1,128)S(1)} async-done(((f32[32,1,128]{2,1,0:T(1,128)}), f32[32,1,128]{2,1,0:T(1,128)S(1)}, u32[]{:S(2)}, u32[]{:S(2)}) %all-to-all-start) | async-done | bytes 16416 | tf_op jit(solution)/shard_map/all_to_all | solution.py:603
  40.5 0.9 %shard_map.104 = (f32[2,8,2048]{2,1,0:T(8,128)}, f32[2,8,2048]{2,1,0:T(8,128)}) custom-call(f32[32,128]{1,0:T(8,128)S(1)} %bitcast.17, f32[2,8,2048]{2,1,0:T(8,128)S(1)} %get-tuple-element.35.field_ref.refs_1_.refs_0_, f32[2,8,2048]{2,1,0:T(8,128)S(1)} %get-tuple-element.46.field_ref.refs_2_.refs_1_, f32[2,8,2048]{2,1,0:T(8,128)S(1)} %get-tuple-element.57.field_ref.refs_2_, ...), custom_call_target="tpu_custom_call" | custom-call | tf_op jit(solution)/shard_map/pallas_call | solution.py:616
Async XLA Ops:
  0.6 10.8 %collective-permute-start.1 = (f32[2,8,2048]{2,1,0:T(8,128)}, f32[2,8,2048]{2,1,0:T(8,128)S(1)}, u32[]{:S(2)}, u32[]{:S(2)}) collective-permute-start(f32[2,8,2048]{2,1,0:T(8,128)} %bitcast.18), channel_id=1, source_target_pairs={{0,30},{2,0},{4,2},{6,4},{8,6},{10,8},{12,10},{14,12},{16,14},{18,... | collective-permute-start | bytes 393224 | tf_op jit(solution)/shard_map/ppermute | solution.py:558
  9.7 1.3 %collective-permute-start = (f32[4,2048]{1,0:T(4,128)S(1)}, f32[4,2048]{1,0:T(4,128)S(1)}, u32[]{:S(2)}, u32[]{:S(2)}) collective-permute-start(f32[4,2048]{1,0:T(4,128)S(1)} %get-tuple-element.40), channel_id=1, source_target_pairs={{0,1},{1,0},{2,3},{3,2},{4,5},{5,4},{6,7},{7,6},{8,9},{9,8},{10,11... | collective-permute-start | bytes 98312 | tf_op jit(solution)/shard_map/ppermute | solution.py:27
  9.8 2.1 %collective-permute-start.3 = (f32[8,896]{1,0:T(8,128)S(1)}, f32[8,896]{1,0:T(8,128)S(1)}, u32[]{:S(2)}, u32[]{:S(2)}) collective-permute-start(f32[8,896]{1,0:T(8,128)S(1)} %get-tuple-element.39.up), channel_id=1, source_target_pairs={{2,4},{4,2},{3,5},{5,3},{6,8},{8,6},{7,9},{9,7},{10,12},{12,10},{1... | collective-permute-start | bytes 86024 | tf_op jit(solution)/shard_map/ppermute | solution.py:41
  10.3 3.9 %collective-permute-start.2 = (f32[8,896]{1,0:T(8,128)S(1)}, f32[8,896]{1,0:T(8,128)S(1)}, u32[]{:S(2)}, u32[]{:S(2)}) collective-permute-start(f32[8,896]{1,0:T(8,128)S(1)} %get-tuple-element.39.up), channel_id=1, source_target_pairs={{0,2},{2,0},{1,3},{3,1},{4,6},{6,4},{5,7},{7,5},{8,10},{10,8},{9,1... | collective-permute-start | bytes 86024 | tf_op jit(solution)/shard_map/ppermute | solution.py:41
  16.1 1.2 %collective-permute-start.4 = (f32[2,2048]{1,0:T(2,128)S(1)}, f32[2,2048]{1,0:T(2,128)S(1)}, u32[]{:S(2)}, u32[]{:S(2)}) collective-permute-start(f32[2,2048]{1,0:T(2,128)S(1)} %get-tuple-element.48), channel_id=1, source_target_pairs={{0,1},{1,0},{2,3},{3,2},{4,5},{5,4},{6,7},{7,6},{8,9},{9,8},{10,11... | collective-permute-start | bytes 49160 | tf_op jit(solution)/shard_map/ppermute | solution.py:27
  16.1 3.7 %collective-permute-start.5 = (f32[2,8,128]{2,1,0:T(8,128)S(1)}, f32[2,8,128]{2,1,0:T(8,128)S(1)}, u32[]{:S(2)}, u32[]{:S(2)}) collective-permute-start(f32[2,8,128]{2,1,0:T(8,128)S(1)} %get-tuple-element.55), channel_id=1, source_target_pairs={{0,2},{2,0},{1,3},{3,1},{4,6},{6,4},{5,7},{7,5},{8,10},{10,8},{9,1... | collective-permute-start | bytes 24584 | tf_op jit(solution)/shard_map/ppermute | solution.py:41
  16.2 3.6 %collective-permute-start.6 = (f32[2,8,128]{2,1,0:T(8,128)S(1)}, f32[2,8,128]{2,1,0:T(8,128)S(1)}, u32[]{:S(2)}, u32[]{:S(2)}) collective-permute-start(f32[2,8,128]{2,1,0:T(8,128)S(1)} %get-tuple-element.56), channel_id=1, source_target_pairs={{2,4},{4,2},{3,5},{5,3},{6,8},{8,6},{7,9},{9,7},{10,12},{12,10},{1... | collective-permute-start | bytes 24584 | tf_op jit(solution)/shard_map/ppermute | solution.py:41
  21.3 3.2 %collective-permute-start.7 = (f32[2,2048]{1,0:T(2,128)S(1)}, f32[2,2048]{1,0:T(2,128)S(1)}, u32[]{:S(2)}, u32[]{:S(2)}) collective-permute-start(f32[2,2048]{1,0:T(2,128)S(1)} %get-tuple-element.58), channel_id=1, source_target_pairs={{0,1},{1,0},{2,3},{3,2},{4,5},{5,4},{6,7},{7,6},{8,9},{9,8},{10,11... | collective-permute-start | bytes 49160 | tf_op jit(solution)/shard_map/ppermute | solution.py:27
  21.4 4.6 %collective-permute-start.8 = (f32[2,8,128]{2,1,0:T(8,128)S(1)}, f32[2,8,128]{2,1,0:T(8,128)S(1)}, u32[]{:S(2)}, u32[]{:S(2)}) collective-permute-start(f32[2,8,128]{2,1,0:T(8,128)S(1)} %get-tuple-element.61), channel_id=1, source_target_pairs={{0,2},{2,0},{1,3},{3,1},{4,6},{6,4},{5,7},{7,5},{8,10},{10,8},{9,1... | collective-permute-start | bytes 24584 | tf_op jit(solution)/shard_map/ppermute | solution.py:41
  24.4 1.6 %collective-permute-start.9 = (f32[2,8,128]{2,1,0:T(8,128)S(1)}, f32[2,8,128]{2,1,0:T(8,128)S(1)}, u32[]{:S(2)}, u32[]{:S(2)}) collective-permute-start(f32[2,8,128]{2,1,0:T(8,128)S(1)} %get-tuple-element.62), channel_id=1, source_target_pairs={{2,4},{4,2},{3,5},{5,3},{6,8},{8,6},{7,9},{9,7},{10,12},{12,10},{1... | collective-permute-start | bytes 24584 | tf_op jit(solution)/shard_map/ppermute | solution.py:41
  26.8 13.7 %all-to-all-start = ((f32[32,1,128]{2,1,0:T(1,128)}), f32[32,1,128]{2,1,0:T(1,128)S(1)}, u32[]{:S(2)}, u32[]{:S(2)}) async-start(f32[32,1,128]{2,1,0:T(1,128)} %bitcast.8), calls=%async_computation | async-start | bytes 32768 | tf_op jit(solution)/shard_map/all_to_all | solution.py:603

commit v7 on v6

--- a/solution.py
+++ b/solution.py
@@ -1,4 +1,5 @@
 import functools
+import math
 
 import jax
 import jax.numpy as jnp
@@ -372,17 +373,22 @@
     )
 
 
-def moments_of(pairs, start=0):
+def moment_scale(slots):
+    bound = GAIN * (8 * 3.0 + 0.2 + 4 * slots) + SHIFT
+    return 0.5 ** math.ceil(2.5 * math.log2(bound))
+
+
+def moments_of(pairs, scale, start=0):
     lane = lax.broadcasted_iota(jnp.int32, (1, LANES), 1)
     total = jnp.zeros((1, LANES), F32)
     for i, (u, w) in enumerate(pairs):
-        s = u[0] * w[0] + u[1] * w[1]
+        s = (u[0] * scale) * (w[0] * scale) + (u[1] * scale) * (w[1] * scale)
         s = jnp.sum(jnp.sum(s, axis=0, keepdims=True), axis=1, keepdims=True)
         total = total + jnp.where(lane == start + i, s, 0.0)
     return total
 
 
-def between_kernel(last, n_edges, flags, field_ref, across, down, hold, rim, *refs):
+def between_kernel(last, n_edges, scale, flags, field_ref, across, down, hold, rim, *refs):
     refs = list(refs)
     edge_refs = [refs.pop(0) for _ in range(n_edges)]
     earlier = [refs.pop(0) for _ in range(ITERS - 1)] if last else []
@@ -394,7 +400,9 @@
         base[c] = image[c]
     if last:
         basis = [(ref[0], ref[1]) for ref in earlier] + [field, image]
-        refs.pop(0)[...] = moments_of([(basis[i // 2], basis[i - i // 2]) for i in range(2 * ITERS)])
+        refs.pop(0)[...] = moments_of(
+            [(basis[i // 2], basis[i - i // 2]) for i in range(2 * ITERS)], scale
+        )
 
 
 def errors_of(flags, local, got0, got1):
@@ -407,9 +415,10 @@
     )
 
 
-def sum_kernel(flags, partial, local, got0, got1, sums):
+def sum_kernel(scale, flags, partial, local, got0, got1, sums):
     own, prev = errors_of(flags, local, got0, got1)
-    s = own[0] * local[0, 0] + own[1] * local[0, 1] + prev[0] * local[1, 0] + prev[1] * local[1, 1]
+    pairs = [(own[c], local[0, c]) for c in range(2)] + [(prev[c], local[1, c]) for c in range(2)]
+    s = sum((a * scale) * (b * scale) for a, b in pairs)
     s = jnp.sum(jnp.sum(s, axis=0, keepdims=True), axis=1, keepdims=True)
     lane = lax.broadcasted_iota(jnp.int32, (1, LANES), 1)
     at = 2 * ITERS - 1
@@ -549,6 +558,7 @@
 
     field_shape = (2, rows, cols)
     message = (2, nb, LANES)
+    scale = moment_scale(slots)
     size = rows * cols // WIDE
     common = [field_shape, (2,) + message, message, message] + [(2, cols)] * n_edges
     table = lambda *shape: jax.ShapeDtypeStruct(shape, BF16)
@@ -593,13 +603,21 @@
         last = step == ITERS - 1
         got0, got1, got_edges = exchange(to0, to1, edges)
         base, *partial = run(
-            functools.partial(between_kernel, last, n_edges),
+            functools.partial(between_kernel, last, n_edges, scale),
             [field_shape] + ([(1, LANES)] if last else []),
             [],
             *(marks, field, *stiff, rim, *got_edges, *(basis if last else [])),
         )
         if last:
-            (sums,) = run(sum_kernel, [(n_gz * n_xy, LANES)], [], marks, *partial, local, got0, got1)
+            (sums,) = run(
+                functools.partial(sum_kernel, scale),
+                [(n_gz * n_xy, LANES)],
+                [],
+                marks, *partial,
+                local,
+                got0,
+                got1,
+            )
             sums = lax.all_to_all(sums.reshape(n_gz * n_xy, 1, LANES), ("gz", "xy"), 0, 0)
             sums = sums.reshape(n_gz * n_xy, LANES)
         field_next, *rest = run(

time: 41.6 us -> 41.6 us (level)
  no operation moved by 1% of the time
where the time goes in v7:
time: 41.6 us; the launch traced here: 41.4 us
  starting transfers between devices  17.9 us (43%)
  waiting for transfers between devices  13.2 us (32%)
  Pallas kernels  8.84 us (21%)
  between operations  1.4 us (3%)
    ppermute x1, starting transfers between devices, body(): lax.ppermute(rhs, 'gz', [(i, (i - 1) % n_gz) for i in range(n_gz)])  7.01 us
    all_to_all x1, starting transfers between devices, body(): lax.all_to_all(sums.reshape(n_gz * n_xy, 1, LANES), ('gz', 'xy'), 0, 0)  6.56 us
    pallas_call x8, Pallas kernels, body(): call(kernel, [VMEM] * len(args), shapes, scratch)(*args)  6.52 us
    all_to_all x1, waiting for transfers between devices, body(): lax.all_to_all(sums.reshape(n_gz * n_xy, 1, LANES), ('gz', 'xy'), 0, 0)  6.17 us
    ppermute x6, waiting for transfers between devices, swapped_sections(): return lax.ppermute(block, ('gz', 'xy'), route)  5.67 us
    ppermute x6, starting transfers between devices, swapped_sections(): return lax.ppermute(block, ('gz', 'xy'), route)  4.13 us
    pallas_call x1, Pallas kernels, body(): call(functools.partial(prepare_kernel, two), [SMEM] + [HBM] * 7, [field_s...  1.41 us
    ppermute x3, waiting for transfers between devices, swapped(): return lax.ppermute(block, axis, route) if route else None  1.37 us
  transfers between devices with their start and end apart: 11, of which 6 were waited for; matrix products, arithmetic and copies ran while one was open for 0% of the time, Pallas kernels for 9%

profile of v7, /device:TPU:0, one launch (start us, length us, event | category | flops | bytes accessed | tf_op | source)
XLA Modules:
  0.0 41.4 jit_solution(18377449973138513)
XLA Ops:
  0.6 7.0 %collective-permute-start.1 = (f32[2,8,2048]{2,1,0:T(8,128)}, f32[2,8,2048]{2,1,0:T(8,128)S(1)}, u32[]{:S(2)}, u32[]{:S(2)}) collective-permute-start(f32[2,8,2048]{2,1,0:T(8,128)} %bitcast.18), channel_id=1, source_target_pairs={{0,30},{2,0},{4,2},{6,4},{8,6},{10,8},{12,10},{14,12},{16,14},{18,... | collective-permute-start | bytes 393224 | tf_op jit(solution)/shard_map/ppermute | solution.py:568
  8.3 1.4 %shard_map.95 = (f32[2,8,2048]{2,1,0:T(8,128)S(1)}, f32[8,2048]{1,0:T(8,128)S(1)}, f32[8,2048]{1,0:T(8,128)S(1)}, f32[8,2048]{1,0:T(8,128)S(1)}, f32[8,896]{1,0:...) custom-call(s32[1,1]{1,0:T(1,128)S(6)} %copy.15.count, ...), custom_call_target="tpu_custom_call" | custom-call | tf_op jit(solution)/shard_map/pallas_call | solution.py:571
  9.7 0.1 collective-permute-start
  9.8 0.5 %collective-permute-start.3 = (f32[8,896]{1,0:T(8,128)S(1)}, f32[8,896]{1,0:T(8,128)S(1)}, u32[]{:S(2)}, u32[]{:S(2)}) collective-permute-start(f32[8,896]{1,0:T(8,128)S(1)} %get-tuple-element.39.up), channel_id=1, source_target_pairs={{2,4},{4,2},{3,5},{5,3},{6,8},{8,6},{7,9},{9,7},{10,12},{12,10},{1... | collective-permute-start | bytes 86024 | tf_op jit(solution)/shard_map/ppermute | solution.py:42
  10.3 0.0 collective-permute-start.2
  10.3 0.7 %collective-permute-done.refs_0_ = f32[4,2048]{1,0:T(4,128)S(1)} collective-permute-done((f32[4,2048]{1,0:T(4,128)S(1)}, f32[4,2048]{1,0:T(4,128)S(1)}, u32[]{:S(2)}, u32[]{:S(2)}) %collective-permute-start) | collective-permute-done | bytes 32800 | tf_op jit(solution)/shard_map/ppermute | solution.py:28
  11.0 0.4 %shard_map.96 = (f32[2,8,2048]{2,1,0:T(8,128)S(1)}, f32[1,2048]{1,0:T(1,128)S(1)}, bf16[256,1024]{1,0:T(8,128)(2,1)S(1)}, f32[2,64,1024]{2,1,0:T(8,128)S(1)}) custom-call(f32[4,8,128]{2,1,0:T(8,128)S(1)} %get-tuple-element.34.flags, f32[2,8,2048]{2,1,0:T(8,128)S(1)} %get-tuple-element.35.field_ref.refs_1_.refs_0_, f32[8,2048]{1,0:T(8,128)S(1)} %get-tuple-element.36.across, ...), custom_call_target="tpu_custom_call" | custom-call | tf_op jit(solution)/shard_map/pallas_call | solution.py:567
  11.4 0.0 collective-permute-done.1.next_field
  11.4 0.5 %shard_map.97.got_next = f32[2,8,128]{2,1,0:T(8,128)S(1)} custom-call(bf16[256,1024]{1,0:T(8,128)(2,1)S(1)} %get-tuple-element.44.next_lanes, f32[2,64,1024]{2,1,0:T(8,128)S(1)} %get-tuple-element.45.next_blend, f32[2,8,2048]{2,1,0:T(8,128)S(1)} %collective-permute-done.1.next_field), custom_call_target="tpu_custom_call" | custom-call | tf_op jit(solution)/shard_map/pallas_call | solution.py:567
  11.9 0.0 collective-permute-done.3.up1
  11.9 2.2 %collective-permute-done.2.up0 = f32[8,896]{1,0:T(8,128)S(1)} collective-permute-done((f32[8,896]{1,0:T(8,128)S(1)}, f32[8,896]{1,0:T(8,128)S(1)}, u32[]{:S(2)}, u32[]{:S(2)}) %collective-permute-start.2) | collective-permute-done | bytes 28704 | tf_op jit(solution)/shard_map/ppermute | solution.py:42
  14.2 1.9 %shard_map.98 = (f32[2,8,2048]{2,1,0:T(8,128)S(1)}, f32[2,2,8,128]{3,2,1,0:T(8,128)S(1)}, f32[2,8,128]{2,1,0:T(8,128)S(1)}, f32[2,8,128]{2,1,0:T(8,128)S(1)}, f3...) custom-call(f32[4,8,128]{2,1,0:T(8,128)S(1)} %get-tuple-element.34.f, ...), custom_call_target="tpu_custom_call" | custom-call | tf_op jit(solution)/shard_map/pallas_call | solution.py:567
  16.1 0.1 collective-permute-start.4
  16.1 0.1 collective-permute-start.5
  16.2 0.4 %collective-permute-start.6 = (f32[2,8,128]{2,1,0:T(8,128)S(1)}, f32[2,8,128]{2,1,0:T(8,128)S(1)}, u32[]{:S(2)}, u32[]{:S(2)}) collective-permute-start(f32[2,8,128]{2,1,0:T(8,128)S(1)} %get-tuple-element.56), channel_id=1, source_target_pairs={{2,4},{4,2},{3,5},{5,3},{6,8},{8,6},{7,9},{9,7},{10,12},{12,10},{1... | collective-permute-start | bytes 24584 | tf_op jit(solution)/shard_map/ppermute | solution.py:42
  16.6 0.7 %collective-permute-done.4.refs_0_ = f32[2,2048]{1,0:T(2,128)S(1)} collective-permute-done((f32[2,2048]{1,0:T(2,128)S(1)}, f32[2,2048]{1,0:T(2,128)S(1)}, u32[]{:S(2)}, u32[]{:S(2)}) %collective-permute-start.4) | collective-permute-done | bytes 16416 | tf_op jit(solution)/shard_map/ppermute | solution.py:28
  17.3 0.2 shard_map.99.base
  17.5 2.4 %collective-permute-done.5.got0 = f32[2,8,128]{2,1,0:T(8,128)S(1)} collective-permute-done((f32[2,8,128]{2,1,0:T(8,128)S(1)}, f32[2,8,128]{2,1,0:T(8,128)S(1)}, u32[]{:S(2)}, u32[]{:S(2)}) %collective-permute-start.5) | collective-permute-done | bytes 8224 | tf_op jit(solution)/shard_map/ppermute | solution.py:42
  19.9 0.0 collective-permute-done.6.got1
  19.9 1.5 %shard_map.100 = (f32[2,8,2048]{2,1,0:T(8,128)S(1)}, f32[2,2,8,128]{3,2,1,0:T(8,128)S(1)}, f32[2,8,128]{2,1,0:T(8,128)S(1)}, f32[2,8,128]{2,1,0:T(8,128)S(1)}, f32[2,2048]{1,0:T(2,128)S(1)}) custom-call(f32[4,8,128]{2,1,0:T(8,128)S(1)} %get-tuple-element.34.flags, f32[2,8,2048]{2,1,0:T(8,128)S(1)} %get-tuple-element.46.field_ref.refs_2_.refs_1_, ...), custom_call_target="tpu_custom_call" | custom-call | tf_op jit(solution)/shard_map/pallas_call | solution.py:567
  21.3 0.1 collective-permute-start.7
  21.4 3.0 %collective-permute-start.8 = (f32[2,8,128]{2,1,0:T(8,128)S(1)}, f32[2,8,128]{2,1,0:T(8,128)S(1)}, u32[]{:S(2)}, u32[]{:S(2)}) collective-permute-start(f32[2,8,128]{2,1,0:T(8,128)S(1)} %get-tuple-element.61), channel_id=1, source_target_pairs={{0,2},{2,0},{1,3},{3,1},{4,6},{6,4},{5,7},{7,5},{8,10},{10,8},{9,1... | collective-permute-start | bytes 24584 | tf_op jit(solution)/shard_map/ppermute | solution.py:42
  24.4 0.2 collective-permute-start.9
  24.6 0.0 collective-permute-done.7.refs_0_
  24.6 0.4 shard_map.101
  25.0 1.1 %collective-permute-done.8.got0 = f32[2,8,128]{2,1,0:T(8,128)S(1)} collective-permute-done((f32[2,8,128]{2,1,0:T(8,128)S(1)}, f32[2,8,128]{2,1,0:T(8,128)S(1)}, u32[]{:S(2)}, u32[]{:S(2)}) %collective-permute-start.8) | collective-permute-done | bytes 8224 | tf_op jit(solution)/shard_map/ppermute | solution.py:42
  26.0 0.0 collective-permute-done.9.got1
  26.0 0.7 %shard_map.102 = f32[32,128]{1,0:T(8,128)} custom-call(f32[4,8,128]{2,1,0:T(8,128)S(1)} %get-tuple-element.34.flags, f32[1,128]{1,0:T(1,128)S(1)} %get-tuple-element.59.partial, f32[2,2,8,128]{3,2,1,0:T(8,128)S(1)} %get-tuple-element.60.local, f32[2,8,128]{2,1,0:T(8,128)S(1)} %collective-permute-done.8.got0, f32[2,8,128]{2,1,0:T(8,128)S(1)} %collective-permute-done.9.got1), custom_call_target="tpu_custom_call" | custom-call | tf_op jit(solution)/shard_map/pallas_call | solution.py:567
  26.8 6.6 %all-to-all-start = ((f32[32,1,128]{2,1,0:T(1,128)}), f32[32,1,128]{2,1,0:T(1,128)S(1)}, u32[]{:S(2)}, u32[]{:S(2)}) async-start(f32[32,1,128]{2,1,0:T(1,128)} %bitcast.8), calls=%async_computation | async-start | bytes 32768 | tf_op jit(solution)/shard_map/all_to_all | solution.py:621
  33.4 0.9 %shard_map.103.refs_3_ = f32[2,8,2048]{2,1,0:T(8,128)S(1)} custom-call(f32[4,8,128]{2,1,0:T(8,128)S(1)} %get-tuple-element.34.flags, f32[2,8,2048]{2,1,0:T(8,128)S(1)} %get-tuple-element.57.field_ref.refs_2_, f32[2,8,2048]{2,1,0:T(8,128)S(1)} %get-tuple-element.63.base, bf16[256,1024]{1,0:T(8,128)(2,1)S(1)} %get-tuple-element.42.own_lanes, ...), custom_call_target="tpu_custom_call" | custom-call | tf_op jit(solution)/shard_map/pallas_call | solution.py:567
  34.3 6.2 %all-to-all-done = f32[32,1,128]{2,1,0:T(1,128)S(1)} async-done(((f32[32,1,128]{2,1,0:T(1,128)}), f32[32,1,128]{2,1,0:T(1,128)S(1)}, u32[]{:S(2)}, u32[]{:S(2)}) %all-to-all-start) | async-done | bytes 16416 | tf_op jit(solution)/shard_map/all_to_all | solution.py:621
  40.5 0.9 %shard_map.104 = (f32[2,8,2048]{2,1,0:T(8,128)}, f32[2,8,2048]{2,1,0:T(8,128)}) custom-call(f32[32,128]{1,0:T(8,128)S(1)} %bitcast.17, f32[2,8,2048]{2,1,0:T(8,128)S(1)} %get-tuple-element.35.field_ref.refs_1_.refs_0_, f32[2,8,2048]{2,1,0:T(8,128)S(1)} %get-tuple-element.46.field_ref.refs_2_.refs_1_, f32[2,8,2048]{2,1,0:T(8,128)S(1)} %get-tuple-element.57.field_ref.refs_2_, ...), custom_call_target="tpu_custom_call" | custom-call | tf_op jit(solution)/shard_map/pallas_call | solution.py:634
Async XLA Ops:
  0.6 10.8 %collective-permute-start.1 = (f32[2,8,2048]{2,1,0:T(8,128)}, f32[2,8,2048]{2,1,0:T(8,128)S(1)}, u32[]{:S(2)}, u32[]{:S(2)}) collective-permute-start(f32[2,8,2048]{2,1,0:T(8,128)} %bitcast.18), channel_id=1, source_target_pairs={{0,30},{2,0},{4,2},{6,4},{8,6},{10,8},{12,10},{14,12},{16,14},{18,... | collective-permute-start | bytes 393224 | tf_op jit(solution)/shard_map/ppermute | solution.py:568
  9.7 1.3 %collective-permute-start = (f32[4,2048]{1,0:T(4,128)S(1)}, f32[4,2048]{1,0:T(4,128)S(1)}, u32[]{:S(2)}, u32[]{:S(2)}) collective-permute-start(f32[4,2048]{1,0:T(4,128)S(1)} %get-tuple-element.40), channel_id=1, source_target_pairs={{0,1},{1,0},{2,3},{3,2},{4,5},{5,4},{6,7},{7,6},{8,9},{9,8},{10,11... | collective-permute-start | bytes 98312 | tf_op jit(solution)/shard_map/ppermute | solution.py:28
  9.8 2.1 %collective-permute-start.3 = (f32[8,896]{1,0:T(8,128)S(1)}, f32[8,896]{1,0:T(8,128)S(1)}, u32[]{:S(2)}, u32[]{:S(2)}) collective-permute-start(f32[8,896]{1,0:T(8,128)S(1)} %get-tuple-element.39.up), channel_id=1, source_target_pairs={{2,4},{4,2},{3,5},{5,3},{6,8},{8,6},{7,9},{9,7},{10,12},{12,10},{1... | collective-permute-start | bytes 86024 | tf_op jit(solution)/shard_map/ppermute | solution.py:42
  10.3 3.9 %collective-permute-start.2 = (f32[8,896]{1,0:T(8,128)S(1)}, f32[8,896]{1,0:T(8,128)S(1)}, u32[]{:S(2)}, u32[]{:S(2)}) collective-permute-start(f32[8,896]{1,0:T(8,128)S(1)} %get-tuple-element.39.up), channel_id=1, source_target_pairs={{0,2},{2,0},{1,3},{3,1},{4,6},{6,4},{5,7},{7,5},{8,10},{10,8},{9,1... | collective-permute-start | bytes 86024 | tf_op jit(solution)/shard_map/ppermute | solution.py:42
  16.1 1.2 %collective-permute-start.4 = (f32[2,2048]{1,0:T(2,128)S(1)}, f32[2,2048]{1,0:T(2,128)S(1)}, u32[]{:S(2)}, u32[]{:S(2)}) collective-permute-start(f32[2,2048]{1,0:T(2,128)S(1)} %get-tuple-element.48), channel_id=1, source_target_pairs={{0,1},{1,0},{2,3},{3,2},{4,5},{5,4},{6,7},{7,6},{8,9},{9,8},{10,11... | collective-permute-start | bytes 49160 | tf_op jit(solution)/shard_map/ppermute | solution.py:28
  16.1 3.7 %collective-permute-start.5 = (f32[2,8,128]{2,1,0:T(8,128)S(1)}, f32[2,8,128]{2,1,0:T(8,128)S(1)}, u32[]{:S(2)}, u32[]{:S(2)}) collective-permute-start(f32[2,8,128]{2,1,0:T(8,128)S(1)} %get-tuple-element.55), channel_id=1, source_target_pairs={{0,2},{2,0},{1,3},{3,1},{4,6},{6,4},{5,7},{7,5},{8,10},{10,8},{9,1... | collective-permute-start | bytes 24584 | tf_op jit(solution)/shard_map/ppermute | solution.py:42
  16.2 3.6 %collective-permute-start.6 = (f32[2,8,128]{2,1,0:T(8,128)S(1)}, f32[2,8,128]{2,1,0:T(8,128)S(1)}, u32[]{:S(2)}, u32[]{:S(2)}) collective-permute-start(f32[2,8,128]{2,1,0:T(8,128)S(1)} %get-tuple-element.56), channel_id=1, source_target_pairs={{2,4},{4,2},{3,5},{5,3},{6,8},{8,6},{7,9},{9,7},{10,12},{12,10},{1... | collective-permute-start | bytes 24584 | tf_op jit(solution)/shard_map/ppermute | solution.py:42
  21.3 3.2 %collective-permute-start.7 = (f32[2,2048]{1,0:T(2,128)S(1)}, f32[2,2048]{1,0:T(2,128)S(1)}, u32[]{:S(2)}, u32[]{:S(2)}) collective-permute-start(f32[2,2048]{1,0:T(2,128)S(1)} %get-tuple-element.58), channel_id=1, source_target_pairs={{0,1},{1,0},{2,3},{3,2},{4,5},{5,4},{6,7},{7,6},{8,9},{9,8},{10,11... | collective-permute-start | bytes 49160 | tf_op jit(solution)/shard_map/ppermute | solution.py:28
  21.4 4.6 %collective-permute-start.8 = (f32[2,8,128]{2,1,0:T(8,128)S(1)}, f32[2,8,128]{2,1,0:T(8,128)S(1)}, u32[]{:S(2)}, u32[]{:S(2)}) collective-permute-start(f32[2,8,128]{2,1,0:T(8,128)S(1)} %get-tuple-element.61), channel_id=1, source_target_pairs={{0,2},{2,0},{1,3},{3,1},{4,6},{6,4},{5,7},{7,5},{8,10},{10,8},{9,1... | collective-permute-start | bytes 24584 | tf_op jit(solution)/shard_map/ppermute | solution.py:42
  24.4 1.6 %collective-permute-start.9 = (f32[2,8,128]{2,1,0:T(8,128)S(1)}, f32[2,8,128]{2,1,0:T(8,128)S(1)}, u32[]{:S(2)}, u32[]{:S(2)}) collective-permute-start(f32[2,8,128]{2,1,0:T(8,128)S(1)} %get-tuple-element.62), channel_id=1, source_target_pairs={{2,4},{4,2},{3,5},{5,3},{6,8},{8,6},{7,9},{9,7},{10,12},{12,10},{1... | collective-permute-start | bytes 24584 | tf_op jit(solution)/shard_map/ppermute | solution.py:42
  26.8 13.7 %all-to-all-start = ((f32[32,1,128]{2,1,0:T(1,128)}), f32[32,1,128]{2,1,0:T(1,128)S(1)}, u32[]{:S(2)}, u32[]{:S(2)}) async-start(f32[32,1,128]{2,1,0:T(1,128)} %bitcast.8), calls=%async_computation | async-start | bytes 32768 | tf_op jit(solution)/shard_map/all_to_all | solution.py:621

commit v8 on v7

--- a/solution.py
+++ b/solution.py
@@ -166,6 +166,16 @@
 
 
 def spread_own(values, lanes_ref, high_ref, rows):
+    high = high_ref.shape[0]
+    parts = [scaled(high_ref, part.astype(F32)).astype(BF16) for c in range(2) for part in split2(values[c])]
+    out = lax.dot_general(jnp.concatenate(parts, axis=0), lanes_ref[...], NT, preferred_element_type=F32)
+    return [
+        wide(out[2 * c * high : (2 * c + 1) * high] + out[(2 * c + 1) * high : (2 * c + 2) * high], rows)
+        for c in range(2)
+    ]
+
+
+def spread_own_apart(values, lanes_ref, high_ref, rows):
     high = high_ref.shape[0]
     result = []
     for c in range(2):
@@ -352,7 +362,7 @@
     own = [tile_of(up, c) for c in range(2)]
     got_prev = [tile_of(got_up, c) for c in range(2)]
     live = flags[3]
-    pulled = spread_own([live * (own[c] - got_next[c]) for c in range(2)], own_lanes, own_high, rows)
+    pulled = spread_own_apart([live * (own[c] - got_next[c]) for c in range(2)], own_lanes, own_high, rows)
     error = [mid[c] - got_prev[c] for c in range(2)]
     pushed = spread_corners(error, weights, prev_lanes, prev_high, prev_below, rows)
     after = stepped(field_ref, [base[c] + pulled[c] + pushed[c] for c in range(2)])
@@ -428,8 +438,6 @@
 
 
 def step_kernel(
-    last,
-    two,
     flags,
     field_ref,
     base,
@@ -444,7 +452,6 @@
     got0,
     got1,
     out,
-    *refs,
 ):
     rows = field_ref.shape[1]
     error, error_prev = errors_of(flags, local, got0, got1)
@@ -454,10 +461,20 @@
     after = stepped(field_ref, [base[c] + pulled[c] + pushed[c] for c in range(2)])
     for c in range(2):
         out[c] = after[c]
-    if not last:
-        even, even_b = mark(flags, 0), mark(flags, 1)
-        messages, left = refs[:-1], refs[-1]
-        send_on(even, even_b, two, after, (own_lanes, own_high), (prev_lanes, prev_blend), left, *messages)
+
+
+def send_kernel(two, flags, field_ref, own_lanes, own_high, prev_lanes, prev_blend, *refs):
+    messages, left = refs[:-1], refs[-1]
+    send_on(
+        mark(flags, 0),
+        mark(flags, 1),
+        two,
+        [field_ref[0], field_ref[1]],
+        (own_lanes, own_high),
+        (prev_lanes, prev_blend),
+        left,
+        *messages,
+    )
 
 
 def conjugate(moments):
@@ -620,16 +637,18 @@
             )
             sums = lax.all_to_all(sums.reshape(n_gz * n_xy, 1, LANES), ("gz", "xy"), 0, 0)
             sums = sums.reshape(n_gz * n_xy, LANES)
-        field_next, *rest = run(
-            functools.partial(step_kernel, last, two),
-            [field_shape] if last else common,
-            [] if last else [left(2)],
-            *(marks, field, base, own_lanes, own_high, *prev, local, got0, got1),
+        (field_next,) = run(
+            step_kernel, [field_shape], [], *(marks, field, base, own_lanes, own_high, *prev, local, got0, got1)
         )
         basis.append(field)
         field = field_next
         if not last:
-            local, to0, to1, *edges = rest
+            local, to0, to1, *edges = run(
+                functools.partial(send_kernel, two),
+                common[1:],
+                [left(2)],
+                *(marks, field, own_lanes, own_high, prev[1], prev[4]),
+            )
     basis.append(field)
     solution_field, residual = call(finish_kernel, [VMEM] * (1 + len(basis)), [field_shape] * 2)(sums, *basis)
     return solution_field[:, None], residual[:, None]

time: 41.6 us -> 41.4 us (level)
    pallas_call x8 -> x9, Pallas kernels: 6.52 us -> 6.15 us  [body(): call(kernel, [VMEM] * len(args), shapes, scratch)(*args)]
where the time goes in v8:
time: 41.4 us; the launch traced here: 41.2 us
  starting transfers between devices  17.9 us (43%)
  waiting for transfers between devices  13.4 us (32%)
  Pallas kernels  8.46 us (20%)
  between operations  1.41 us (3%)
    ppermute x1, starting transfers between devices, body(): lax.ppermute(rhs, 'gz', [(i, (i - 1) % n_gz) for i in range(n_gz)])  7.01 us
    all_to_all x1, starting transfers between devices, body(): lax.all_to_all(sums.reshape(n_gz * n_xy, 1, LANES), ('gz', 'xy'), 0, 0)  6.56 us
    all_to_all x1, waiting for transfers between devices, body(): lax.all_to_all(sums.reshape(n_gz * n_xy, 1, LANES), ('gz', 'xy'), 0, 0)  6.37 us
    pallas_call x9, Pallas kernels, body(): call(kernel, [VMEM] * len(args), shapes, scratch)(*args)  6.15 us
    ppermute x6, waiting for transfers between devices, swapped_sections(): return lax.ppermute(block, ('gz', 'xy'), route)  5.67 us
    ppermute x6, starting transfers between devices, swapped_sections(): return lax.ppermute(block, ('gz', 'xy'), route)  4.13 us
    pallas_call x1, Pallas kernels, body(): call(functools.partial(prepare_kernel, two), [SMEM] + [HBM] * 7, [field_s...  1.41 us
    ppermute x3, waiting for transfers between devices, swapped(): return lax.ppermute(block, axis, route) if route else None  1.37 us
  transfers between devices with their start and end apart: 11, of which 6 were waited for; matrix products, arithmetic and copies ran while one was open for 0% of the time, Pallas kernels for 9%

profile of v8, /device:TPU:0, one launch (start us, length us, event | category | flops | bytes accessed | tf_op | source)
XLA Modules:
  0.0 41.2 jit_solution(11757218346694633001)
XLA Ops:
  0.6 7.0 %collective-permute-start.1 = (f32[2,8,2048]{2,1,0:T(8,128)}, f32[2,8,2048]{2,1,0:T(8,128)S(1)}, u32[]{:S(2)}, u32[]{:S(2)}) collective-permute-start(f32[2,8,2048]{2,1,0:T(8,128)} %bitcast.18), channel_id=1, source_target_pairs={{0,30},{2,0},{4,2},{6,4},{8,6},{10,8},{12,10},{14,12},{16,14},{18,... | collective-permute-start | bytes 393224 | tf_op jit(solution)/shard_map/ppermute | solution.py:585
  8.3 1.4 %shard_map.95 = (f32[2,8,2048]{2,1,0:T(8,128)S(1)}, f32[8,2048]{1,0:T(8,128)S(1)}, f32[8,2048]{1,0:T(8,128)S(1)}, f32[8,2048]{1,0:T(8,128)S(1)}, f32[8,896]{1,0:...) custom-call(s32[1,1]{1,0:T(1,128)S(6)} %copy.15.count, ...), custom_call_target="tpu_custom_call" | custom-call | tf_op jit(solution)/shard_map/pallas_call | solution.py:588
  9.7 0.1 collective-permute-start
  9.8 0.5 %collective-permute-start.3 = (f32[8,896]{1,0:T(8,128)S(1)}, f32[8,896]{1,0:T(8,128)S(1)}, u32[]{:S(2)}, u32[]{:S(2)}) collective-permute-start(f32[8,896]{1,0:T(8,128)S(1)} %get-tuple-element.38.up), channel_id=1, source_target_pairs={{2,4},{4,2},{3,5},{5,3},{6,8},{8,6},{7,9},{9,7},{10,12},{12,10},{1... | collective-permute-start | bytes 86024 | tf_op jit(solution)/shard_map/ppermute | solution.py:42
  10.3 0.0 collective-permute-start.2
  10.3 0.7 %collective-permute-done.refs_0_ = f32[4,2048]{1,0:T(4,128)S(1)} collective-permute-done((f32[4,2048]{1,0:T(4,128)S(1)}, f32[4,2048]{1,0:T(4,128)S(1)}, u32[]{:S(2)}, u32[]{:S(2)}) %collective-permute-start) | collective-permute-done | bytes 32800 | tf_op jit(solution)/shard_map/ppermute | solution.py:28
  11.0 0.4 %shard_map.96 = (f32[2,8,2048]{2,1,0:T(8,128)S(1)}, f32[1,2048]{1,0:T(1,128)S(1)}, bf16[256,1024]{1,0:T(8,128)(2,1)S(1)}, f32[2,64,1024]{2,1,0:T(8,128)S(1)}) custom-call(f32[4,8,128]{2,1,0:T(8,128)S(1)} %get-tuple-element.33.flags, f32[2,8,2048]{2,1,0:T(8,128)S(1)} %get-tuple-element.34.field_ref.refs_1_.refs_0_, f32[8,2048]{1,0:T(8,128)S(1)} %get-tuple-element.35.across, ...), custom_call_target="tpu_custom_call" | custom-call | tf_op jit(solution)/shard_map/pallas_call | solution.py:584
  11.4 0.0 collective-permute-done.1.next_field
  11.4 0.5 %shard_map.97.got_next = f32[2,8,128]{2,1,0:T(8,128)S(1)} custom-call(bf16[256,1024]{1,0:T(8,128)(2,1)S(1)} %get-tuple-element.43.next_lanes, f32[2,64,1024]{2,1,0:T(8,128)S(1)} %get-tuple-element.44.next_blend, f32[2,8,2048]{2,1,0:T(8,128)S(1)} %collective-permute-done.1.next_field), custom_call_target="tpu_custom_call" | custom-call | tf_op jit(solution)/shard_map/pallas_call | solution.py:584
  11.9 0.0 collective-permute-done.3.up1
  11.9 2.2 %collective-permute-done.2.up0 = f32[8,896]{1,0:T(8,128)S(1)} collective-permute-done((f32[8,896]{1,0:T(8,128)S(1)}, f32[8,896]{1,0:T(8,128)S(1)}, u32[]{:S(2)}, u32[]{:S(2)}) %collective-permute-start.2) | collective-permute-done | bytes 28704 | tf_op jit(solution)/shard_map/ppermute | solution.py:42
  14.2 1.9 %shard_map.98 = (f32[2,8,2048]{2,1,0:T(8,128)S(1)}, f32[2,2,8,128]{3,2,1,0:T(8,128)S(1)}, f32[2,8,128]{2,1,0:T(8,128)S(1)}, f32[2,8,128]{2,1,0:T(8,128)S(1)}, f3...) custom-call(f32[4,8,128]{2,1,0:T(8,128)S(1)} %get-tuple-element.33.f, ...), custom_call_target="tpu_custom_call" | custom-call | tf_op jit(solution)/shard_map/pallas_call | solution.py:584
  16.1 0.1 collective-permute-start.4
  16.1 0.1 collective-permute-start.5
  16.2 0.4 %collective-permute-start.6 = (f32[2,8,128]{2,1,0:T(8,128)S(1)}, f32[2,8,128]{2,1,0:T(8,128)S(1)}, u32[]{:S(2)}, u32[]{:S(2)}) collective-permute-start(f32[2,8,128]{2,1,0:T(8,128)S(1)} %get-tuple-element.55), channel_id=1, source_target_pairs={{2,4},{4,2},{3,5},{5,3},{6,8},{8,6},{7,9},{9,7},{10,12},{12,10},{1... | collective-permute-start | bytes 24584 | tf_op jit(solution)/shard_map/ppermute | solution.py:42
  16.6 0.7 %collective-permute-done.4.refs_0_ = f32[2,2048]{1,0:T(2,128)S(1)} collective-permute-done((f32[2,2048]{1,0:T(2,128)S(1)}, f32[2,2048]{1,0:T(2,128)S(1)}, u32[]{:S(2)}, u32[]{:S(2)}) %collective-permute-start.4) | collective-permute-done | bytes 16416 | tf_op jit(solution)/shard_map/ppermute | solution.py:28
  17.3 0.2 shard_map.99.base
  17.5 2.4 %collective-permute-done.5.got0 = f32[2,8,128]{2,1,0:T(8,128)S(1)} collective-permute-done((f32[2,8,128]{2,1,0:T(8,128)S(1)}, f32[2,8,128]{2,1,0:T(8,128)S(1)}, u32[]{:S(2)}, u32[]{:S(2)}) %collective-permute-start.5) | collective-permute-done | bytes 8224 | tf_op jit(solution)/shard_map/ppermute | solution.py:42
  19.9 0.0 collective-permute-done.6.got1
  19.9 0.7 %shard_map.100.field_ref.refs_2_ = f32[2,8,2048]{2,1,0:T(8,128)S(1)} custom-call(f32[4,8,128]{2,1,0:T(8,128)S(1)} %get-tuple-element.33.flags, f32[2,8,2048]{2,1,0:T(8,128)S(1)} %get-tuple-element.45.field_ref.refs_2_.refs_1_, f32[2,8,2048]{2,1,0:T(8,128)S(1)} %shard_map.99.base, bf16[256,1024]{1,0:T(8,128)(2,1)S(1)} %get-tuple-element.41.own_lanes, ...), custom_call_target="tpu_custom_call" | custom-call | tf_op jit(solution)/shard_map/pallas_call | solution.py:584
  20.6 0.6 %shard_map.101 = (f32[2,2,8,128]{3,2,1,0:T(8,128)S(1)}, f32[2,8,128]{2,1,0:T(8,128)S(1)}, f32[2,8,128]{2,1,0:T(8,128)S(1)}, f32[2,2048]{1,0:T(2,128)S(1)}) custom-call(f32[4,8,128]{2,1,0:T(8,128)S(1)} %get-tuple-element.33.flags, f32[2,8,2048]{2,1,0:T(8,128)S(1)} %shard_map.100.field_ref.refs_2_, bf16[256,1024]{1,0:T(8,128)(2,1)S(1)} %get-tuple-element.41.own_lanes, ...), custom_call_target="tpu_custom_call" | custom-call | tf_op jit(solution)/shard_map/pallas_call | solution.py:584
  21.2 0.1 collective-permute-start.7
  21.3 3.0 %collective-permute-start.8 = (f32[2,8,128]{2,1,0:T(8,128)S(1)}, f32[2,8,128]{2,1,0:T(8,128)S(1)}, u32[]{:S(2)}, u32[]{:S(2)}) collective-permute-start(f32[2,8,128]{2,1,0:T(8,128)S(1)} %get-tuple-element.59), channel_id=1, source_target_pairs={{0,2},{2,0},{1,3},{3,1},{4,6},{6,4},{5,7},{7,5},{8,10},{10,8},{9,1... | collective-permute-start | bytes 24584 | tf_op jit(solution)/shard_map/ppermute | solution.py:42
  24.3 0.2 collective-permute-start.9
  24.4 0.0 collective-permute-done.7.refs_0_
  24.4 0.4 shard_map.102
  24.8 1.1 %collective-permute-done.8.got0 = f32[2,8,128]{2,1,0:T(8,128)S(1)} collective-permute-done((f32[2,8,128]{2,1,0:T(8,128)S(1)}, f32[2,8,128]{2,1,0:T(8,128)S(1)}, u32[]{:S(2)}, u32[]{:S(2)}) %collective-permute-start.8) | collective-permute-done | bytes 8224 | tf_op jit(solution)/shard_map/ppermute | solution.py:42
  25.9 0.7 %shard_map.103 = f32[32,128]{1,0:T(8,128)} custom-call(f32[4,8,128]{2,1,0:T(8,128)S(1)} %get-tuple-element.33.flags, f32[1,128]{1,0:T(1,128)S(1)} %get-tuple-element.57.partial, f32[2,2,8,128]{3,2,1,0:T(8,128)S(1)} %get-tuple-element.58.local, f32[2,8,128]{2,1,0:T(8,128)S(1)} %collective-permute-done.8.got0, f32[2,8,128]{2,1,0:T(8,128)S(1)} %collective-permute-done.9.got1), custom_call_target="tpu_custom_call" | custom-call | tf_op jit(solution)/shard_map/pallas_call | solution.py:584
  26.6 6.6 %all-to-all-start = ((f32[32,1,128]{2,1,0:T(1,128)}), f32[32,1,128]{2,1,0:T(1,128)S(1)}, u32[]{:S(2)}, u32[]{:S(2)}) async-start(f32[32,1,128]{2,1,0:T(1,128)} %bitcast.8), calls=%async_computation | async-start | bytes 32768 | tf_op jit(solution)/shard_map/all_to_all | solution.py:638
  33.2 0.7 %shard_map.104.refs_3_ = f32[2,8,2048]{2,1,0:T(8,128)S(1)} custom-call(f32[4,8,128]{2,1,0:T(8,128)S(1)} %get-tuple-element.33.flags, f32[2,8,2048]{2,1,0:T(8,128)S(1)} %shard_map.100.field_ref.refs_2_, f32[2,8,2048]{2,1,0:T(8,128)S(1)} %get-tuple-element.61.base, bf16[256,1024]{1,0:T(8,128)(2,1)S(1)} %get-tuple-element.41.own_lanes, ...), custom_call_target="tpu_custom_call" | custom-call | tf_op jit(solution)/shard_map/pallas_call | solution.py:584
  33.9 6.4 %all-to-all-done = f32[32,1,128]{2,1,0:T(1,128)S(1)} async-done(((f32[32,1,128]{2,1,0:T(1,128)}), f32[32,1,128]{2,1,0:T(1,128)S(1)}, u32[]{:S(2)}, u32[]{:S(2)}) %all-to-all-start) | async-done | bytes 16416 | tf_op jit(solution)/shard_map/all_to_all | solution.py:638
  40.3 0.9 %shard_map.105 = (f32[2,8,2048]{2,1,0:T(8,128)}, f32[2,8,2048]{2,1,0:T(8,128)}) custom-call(f32[32,128]{1,0:T(8,128)S(1)} %bitcast.17, f32[2,8,2048]{2,1,0:T(8,128)S(1)} %get-tuple-element.34.field_ref.refs_1_.refs_0_, f32[2,8,2048]{2,1,0:T(8,128)S(1)} %get-tuple-element.45.field_ref.refs_2_.refs_1_, f32[2,8,2048]{2,1,0:T(8,128)S(1)} %shard_map.100.field_ref.refs_2_, ...), custom_call_target="tpu_custom_call" | custom-call | tf_op jit(solution)/shard_map/pallas_call | solution.py:653
  (1 shorter events, 0.0 us)
Async XLA Ops:
  0.6 10.8 %collective-permute-start.1 = (f32[2,8,2048]{2,1,0:T(8,128)}, f32[2,8,2048]{2,1,0:T(8,128)S(1)}, u32[]{:S(2)}, u32[]{:S(2)}) collective-permute-start(f32[2,8,2048]{2,1,0:T(8,128)} %bitcast.18), channel_id=1, source_target_pairs={{0,30},{2,0},{4,2},{6,4},{8,6},{10,8},{12,10},{14,12},{16,14},{18,... | collective-permute-start | bytes 393224 | tf_op jit(solution)/shard_map/ppermute | solution.py:585
  9.7 1.3 %collective-permute-start = (f32[4,2048]{1,0:T(4,128)S(1)}, f32[4,2048]{1,0:T(4,128)S(1)}, u32[]{:S(2)}, u32[]{:S(2)}) collective-permute-start(f32[4,2048]{1,0:T(4,128)S(1)} %get-tuple-element.39), channel_id=1, source_target_pairs={{0,1},{1,0},{2,3},{3,2},{4,5},{5,4},{6,7},{7,6},{8,9},{9,8},{10,11... | collective-permute-start | bytes 98312 | tf_op jit(solution)/shard_map/ppermute | solution.py:28
  9.8 2.1 %collective-permute-start.3 = (f32[8,896]{1,0:T(8,128)S(1)}, f32[8,896]{1,0:T(8,128)S(1)}, u32[]{:S(2)}, u32[]{:S(2)}) collective-permute-start(f32[8,896]{1,0:T(8,128)S(1)} %get-tuple-element.38.up), channel_id=1, source_target_pairs={{2,4},{4,2},{3,5},{5,3},{6,8},{8,6},{7,9},{9,7},{10,12},{12,10},{1... | collective-permute-start | bytes 86024 | tf_op jit(solution)/shard_map/ppermute | solution.py:42
  10.3 3.9 %collective-permute-start.2 = (f32[8,896]{1,0:T(8,128)S(1)}, f32[8,896]{1,0:T(8,128)S(1)}, u32[]{:S(2)}, u32[]{:S(2)}) collective-permute-start(f32[8,896]{1,0:T(8,128)S(1)} %get-tuple-element.38.up), channel_id=1, source_target_pairs={{0,2},{2,0},{1,3},{3,1},{4,6},{6,4},{5,7},{7,5},{8,10},{10,8},{9,1... | collective-permute-start | bytes 86024 | tf_op jit(solution)/shard_map/ppermute | solution.py:42
  16.1 1.2 %collective-permute-start.4 = (f32[2,2048]{1,0:T(2,128)S(1)}, f32[2,2048]{1,0:T(2,128)S(1)}, u32[]{:S(2)}, u32[]{:S(2)}) collective-permute-start(f32[2,2048]{1,0:T(2,128)S(1)} %get-tuple-element.47), channel_id=1, source_target_pairs={{0,1},{1,0},{2,3},{3,2},{4,5},{5,4},{6,7},{7,6},{8,9},{9,8},{10,11... | collective-permute-start | bytes 49160 | tf_op jit(solution)/shard_map/ppermute | solution.py:28
  16.1 3.7 %collective-permute-start.5 = (f32[2,8,128]{2,1,0:T(8,128)S(1)}, f32[2,8,128]{2,1,0:T(8,128)S(1)}, u32[]{:S(2)}, u32[]{:S(2)}) collective-permute-start(f32[2,8,128]{2,1,0:T(8,128)S(1)} %get-tuple-element.54), channel_id=1, source_target_pairs={{0,2},{2,0},{1,3},{3,1},{4,6},{6,4},{5,7},{7,5},{8,10},{10,8},{9,1... | collective-permute-start | bytes 24584 | tf_op jit(solution)/shard_map/ppermute | solution.py:42
  16.2 3.6 %collective-permute-start.6 = (f32[2,8,128]{2,1,0:T(8,128)S(1)}, f32[2,8,128]{2,1,0:T(8,128)S(1)}, u32[]{:S(2)}, u32[]{:S(2)}) collective-permute-start(f32[2,8,128]{2,1,0:T(8,128)S(1)} %get-tuple-element.55), channel_id=1, source_target_pairs={{2,4},{4,2},{3,5},{5,3},{6,8},{8,6},{7,9},{9,7},{10,12},{12,10},{1... | collective-permute-start | bytes 24584 | tf_op jit(solution)/shard_map/ppermute | solution.py:42
  21.2 3.2 %collective-permute-start.7 = (f32[2,2048]{1,0:T(2,128)S(1)}, f32[2,2048]{1,0:T(2,128)S(1)}, u32[]{:S(2)}, u32[]{:S(2)}) collective-permute-start(f32[2,2048]{1,0:T(2,128)S(1)} %get-tuple-element.56), channel_id=1, source_target_pairs={{0,1},{1,0},{2,3},{3,2},{4,5},{5,4},{6,7},{7,6},{8,9},{9,8},{10,11... | collective-permute-start | bytes 49160 | tf_op jit(solution)/shard_map/ppermute | solution.py:28
  21.3 4.6 %collective-permute-start.8 = (f32[2,8,128]{2,1,0:T(8,128)S(1)}, f32[2,8,128]{2,1,0:T(8,128)S(1)}, u32[]{:S(2)}, u32[]{:S(2)}) collective-permute-start(f32[2,8,128]{2,1,0:T(8,128)S(1)} %get-tuple-element.59), channel_id=1, source_target_pairs={{0,2},{2,0},{1,3},{3,1},{4,6},{6,4},{5,7},{7,5},{8,10},{10,8},{9,1... | collective-permute-start | bytes 24584 | tf_op jit(solution)/shard_map/ppermute | solution.py:42
  24.3 1.6 %collective-permute-start.9 = (f32[2,8,128]{2,1,0:T(8,128)S(1)}, f32[2,8,128]{2,1,0:T(8,128)S(1)}, u32[]{:S(2)}, u32[]{:S(2)}) collective-permute-start(f32[2,8,128]{2,1,0:T(8,128)S(1)} %get-tuple-element.60), channel_id=1, source_target_pairs={{2,4},{4,2},{3,5},{5,3},{6,8},{8,6},{7,9},{9,7},{10,12},{12,10},{1... | collective-permute-start | bytes 24584 | tf_op jit(solution)/shard_map/ppermute | solution.py:42
  26.6 13.7 %all-to-all-start = ((f32[32,1,128]{2,1,0:T(1,128)}), f32[32,1,128]{2,1,0:T(1,128)S(1)}, u32[]{:S(2)}, u32[]{:S(2)}) async-start(f32[32,1,128]{2,1,0:T(1,128)} %bitcast.8), calls=%async_computation | async-start | bytes 32768 | tf_op jit(solution)/shard_map/all_to_all | solution.py:638

commit v9 on v8

--- a/solution.py
+++ b/solution.py
@@ -126,14 +126,11 @@
     for k in range(0, slots, CHUNK):
         hot = lanes_ref[:, k : k + CHUNK]
         mask = high_ref[:, k : k + CHUNK]
+        rows_of = [left_ref[c * stride : c * stride + 2 * high, :] for c in range(2)]
+        got = jnp.dot(jnp.concatenate(rows_of, axis=0), hot, preferred_element_type=F32)
         for c in range(2):
-            got = jnp.dot(
-                left_ref[c * stride : c * stride + 2 * high, :],
-                hot,
-                preferred_element_type=F32,
-            )
-            value = mask * (got[:high] + got[high:])
-            found[c].append(jnp.sum(value, axis=0, keepdims=True))
+            part = got[2 * c * high : 2 * (c + 1) * high]
+            found[c].append(jnp.sum(mask * (part[:high] + part[high:]), axis=0, keepdims=True))
     return jnp.stack([as_tiles(f) for f in found])
 
 

time: 41.4 us -> 41.4 us (level)
  no operation moved by 1% of the time
where the time goes in v9:
time: 41.4 us; the launch traced here: 41.2 us
  starting transfers between devices  17.9 us (43%)
  waiting for transfers between devices  13.4 us (32%)
  Pallas kernels  8.45 us (20%)
  between operations  1.41 us (3%)
    ppermute x1, starting transfers between devices, body(): lax.ppermute(rhs, 'gz', [(i, (i - 1) % n_gz) for i in range(n_gz)])  7.01 us
    all_to_all x1, starting transfers between devices, body(): lax.all_to_all(sums.reshape(n_gz * n_xy, 1, LANES), ('gz', 'xy'), 0, 0)  6.56 us
    all_to_all x1, waiting for transfers between devices, body(): lax.all_to_all(sums.reshape(n_gz * n_xy, 1, LANES), ('gz', 'xy'), 0, 0)  6.37 us
    pallas_call x9, Pallas kernels, body(): call(kernel, [VMEM] * len(args), shapes, scratch)(*args)  6.14 us
    ppermute x6, waiting for transfers between devices, swapped_sections(): return lax.ppermute(block, ('gz', 'xy'), route)  5.67 us
    ppermute x6, starting transfers between devices, swapped_sections(): return lax.ppermute(block, ('gz', 'xy'), route)  4.13 us
    pallas_call x1, Pallas kernels, body(): call(functools.partial(prepare_kernel, two), [SMEM] + [HBM] * 7, [field_s...  1.4 us
    ppermute x3, waiting for transfers between devices, swapped(): return lax.ppermute(block, axis, route) if route else None  1.37 us
  transfers between devices with their start and end apart: 11, of which 6 were waited for; matrix products, arithmetic and copies ran while one was open for 0% of the time, Pallas kernels for 9%

profile of v9, /device:TPU:0, one launch (start us, length us, event | category | flops | bytes accessed | tf_op | source)
XLA Modules:
  0.0 41.2 jit_solution(13090733000353439837)
XLA Ops:
  0.6 7.0 %collective-permute-start.1 = (f32[2,8,2048]{2,1,0:T(8,128)}, f32[2,8,2048]{2,1,0:T(8,128)S(1)}, u32[]{:S(2)}, u32[]{:S(2)}) collective-permute-start(f32[2,8,2048]{2,1,0:T(8,128)} %bitcast.18), channel_id=1, source_target_pairs={{0,30},{2,0},{4,2},{6,4},{8,6},{10,8},{12,10},{14,12},{16,14},{18,... | collective-permute-start | bytes 393224 | tf_op jit(solution)/shard_map/ppermute | solution.py:582
  8.3 1.4 %shard_map.95 = (f32[2,8,2048]{2,1,0:T(8,128)S(1)}, f32[8,2048]{1,0:T(8,128)S(1)}, f32[8,2048]{1,0:T(8,128)S(1)}, f32[8,2048]{1,0:T(8,128)S(1)}, f32[8,896]{1,0:...) custom-call(s32[1,1]{1,0:T(1,128)S(6)} %copy.15.count, ...), custom_call_target="tpu_custom_call" | custom-call | tf_op jit(solution)/shard_map/pallas_call | solution.py:585
  9.7 0.1 collective-permute-start
  9.8 0.5 %collective-permute-start.3 = (f32[8,896]{1,0:T(8,128)S(1)}, f32[8,896]{1,0:T(8,128)S(1)}, u32[]{:S(2)}, u32[]{:S(2)}) collective-permute-start(f32[8,896]{1,0:T(8,128)S(1)} %get-tuple-element.38.up), channel_id=1, source_target_pairs={{2,4},{4,2},{3,5},{5,3},{6,8},{8,6},{7,9},{9,7},{10,12},{12,10},{1... | collective-permute-start | bytes 86024 | tf_op jit(solution)/shard_map/ppermute | solution.py:42
  10.3 0.0 collective-permute-start.2
  10.3 0.7 %collective-permute-done.refs_0_ = f32[4,2048]{1,0:T(4,128)S(1)} collective-permute-done((f32[4,2048]{1,0:T(4,128)S(1)}, f32[4,2048]{1,0:T(4,128)S(1)}, u32[]{:S(2)}, u32[]{:S(2)}) %collective-permute-start) | collective-permute-done | bytes 32800 | tf_op jit(solution)/shard_map/ppermute | solution.py:28
  11.0 0.4 %shard_map.96 = (f32[2,8,2048]{2,1,0:T(8,128)S(1)}, f32[1,2048]{1,0:T(1,128)S(1)}, bf16[256,1024]{1,0:T(8,128)(2,1)S(1)}, f32[2,64,1024]{2,1,0:T(8,128)S(1)}) custom-call(f32[4,8,128]{2,1,0:T(8,128)S(1)} %get-tuple-element.33.flags, f32[2,8,2048]{2,1,0:T(8,128)S(1)} %get-tuple-element.34.field_ref.refs_1_.refs_0_, f32[8,2048]{1,0:T(8,128)S(1)} %get-tuple-element.35.across, ...), custom_call_target="tpu_custom_call" | custom-call | tf_op jit(solution)/shard_map/pallas_call | solution.py:581
  11.4 0.0 collective-permute-done.1.next_field
  11.4 0.5 %shard_map.97.got_next = f32[2,8,128]{2,1,0:T(8,128)S(1)} custom-call(bf16[256,1024]{1,0:T(8,128)(2,1)S(1)} %get-tuple-element.43.next_lanes, f32[2,64,1024]{2,1,0:T(8,128)S(1)} %get-tuple-element.44.next_blend, f32[2,8,2048]{2,1,0:T(8,128)S(1)} %collective-permute-done.1.next_field), custom_call_target="tpu_custom_call" | custom-call | tf_op jit(solution)/shard_map/pallas_call | solution.py:581
  11.9 0.0 collective-permute-done.3.up1
  11.9 2.2 %collective-permute-done.2.up0 = f32[8,896]{1,0:T(8,128)S(1)} collective-permute-done((f32[8,896]{1,0:T(8,128)S(1)}, f32[8,896]{1,0:T(8,128)S(1)}, u32[]{:S(2)}, u32[]{:S(2)}) %collective-permute-start.2) | collective-permute-done | bytes 28704 | tf_op jit(solution)/shard_map/ppermute | solution.py:42
  14.2 1.9 %shard_map.98 = (f32[2,8,2048]{2,1,0:T(8,128)S(1)}, f32[2,2,8,128]{3,2,1,0:T(8,128)S(1)}, f32[2,8,128]{2,1,0:T(8,128)S(1)}, f32[2,8,128]{2,1,0:T(8,128)S(1)}, f3...) custom-call(f32[4,8,128]{2,1,0:T(8,128)S(1)} %get-tuple-element.33.f, ...), custom_call_target="tpu_custom_call" | custom-call | tf_op jit(solution)/shard_map/pallas_call | solution.py:581
  16.1 0.1 collective-permute-start.4
  16.1 0.1 collective-permute-start.5
  16.2 0.4 %collective-permute-start.6 = (f32[2,8,128]{2,1,0:T(8,128)S(1)}, f32[2,8,128]{2,1,0:T(8,128)S(1)}, u32[]{:S(2)}, u32[]{:S(2)}) collective-permute-start(f32[2,8,128]{2,1,0:T(8,128)S(1)} %get-tuple-element.55), channel_id=1, source_target_pairs={{2,4},{4,2},{3,5},{5,3},{6,8},{8,6},{7,9},{9,7},{10,12},{12,10},{1... | collective-permute-start | bytes 24584 | tf_op jit(solution)/shard_map/ppermute | solution.py:42
  16.6 0.7 %collective-permute-done.4.refs_0_ = f32[2,2048]{1,0:T(2,128)S(1)} collective-permute-done((f32[2,2048]{1,0:T(2,128)S(1)}, f32[2,2048]{1,0:T(2,128)S(1)}, u32[]{:S(2)}, u32[]{:S(2)}) %collective-permute-start.4) | collective-permute-done | bytes 16416 | tf_op jit(solution)/shard_map/ppermute | solution.py:28
  17.3 0.2 shard_map.99.base
  17.5 2.4 %collective-permute-done.5.got0 = f32[2,8,128]{2,1,0:T(8,128)S(1)} collective-permute-done((f32[2,8,128]{2,1,0:T(8,128)S(1)}, f32[2,8,128]{2,1,0:T(8,128)S(1)}, u32[]{:S(2)}, u32[]{:S(2)}) %collective-permute-start.5) | collective-permute-done | bytes 8224 | tf_op jit(solution)/shard_map/ppermute | solution.py:42
  19.8 0.0 collective-permute-done.6.got1
  19.9 0.7 %shard_map.100.field_ref.refs_2_ = f32[2,8,2048]{2,1,0:T(8,128)S(1)} custom-call(f32[4,8,128]{2,1,0:T(8,128)S(1)} %get-tuple-element.33.flags, f32[2,8,2048]{2,1,0:T(8,128)S(1)} %get-tuple-element.45.field_ref.refs_2_.refs_1_, f32[2,8,2048]{2,1,0:T(8,128)S(1)} %shard_map.99.base, bf16[256,1024]{1,0:T(8,128)(2,1)S(1)} %get-tuple-element.41.own_lanes, ...), custom_call_target="tpu_custom_call" | custom-call | tf_op jit(solution)/shard_map/pallas_call | solution.py:581
  20.6 0.6 %shard_map.101 = (f32[2,2,8,128]{3,2,1,0:T(8,128)S(1)}, f32[2,8,128]{2,1,0:T(8,128)S(1)}, f32[2,8,128]{2,1,0:T(8,128)S(1)}, f32[2,2048]{1,0:T(2,128)S(1)}) custom-call(f32[4,8,128]{2,1,0:T(8,128)S(1)} %get-tuple-element.33.flags, f32[2,8,2048]{2,1,0:T(8,128)S(1)} %shard_map.100.field_ref.refs_2_, bf16[256,1024]{1,0:T(8,128)(2,1)S(1)} %get-tuple-element.41.own_lanes, ...), custom_call_target="tpu_custom_call" | custom-call | tf_op jit(solution)/shard_map/pallas_call | solution.py:581
  21.2 0.1 collective-permute-start.7
  21.3 3.0 %collective-permute-start.8 = (f32[2,8,128]{2,1,0:T(8,128)S(1)}, f32[2,8,128]{2,1,0:T(8,128)S(1)}, u32[]{:S(2)}, u32[]{:S(2)}) collective-permute-start(f32[2,8,128]{2,1,0:T(8,128)S(1)} %get-tuple-element.59), channel_id=1, source_target_pairs={{0,2},{2,0},{1,3},{3,1},{4,6},{6,4},{5,7},{7,5},{8,10},{10,8},{9,1... | collective-permute-start | bytes 24584 | tf_op jit(solution)/shard_map/ppermute | solution.py:42
  24.2 0.2 collective-permute-start.9
  24.4 0.0 collective-permute-done.7.refs_0_
  24.4 0.4 shard_map.102
  24.8 1.1 %collective-permute-done.8.got0 = f32[2,8,128]{2,1,0:T(8,128)S(1)} collective-permute-done((f32[2,8,128]{2,1,0:T(8,128)S(1)}, f32[2,8,128]{2,1,0:T(8,128)S(1)}, u32[]{:S(2)}, u32[]{:S(2)}) %collective-permute-start.8) | collective-permute-done | bytes 8224 | tf_op jit(solution)/shard_map/ppermute | solution.py:42
  25.9 0.7 %shard_map.103 = f32[32,128]{1,0:T(8,128)} custom-call(f32[4,8,128]{2,1,0:T(8,128)S(1)} %get-tuple-element.33.flags, f32[1,128]{1,0:T(1,128)S(1)} %get-tuple-element.57.partial, f32[2,2,8,128]{3,2,1,0:T(8,128)S(1)} %get-tuple-element.58.local, f32[2,8,128]{2,1,0:T(8,128)S(1)} %collective-permute-done.8.got0, f32[2,8,128]{2,1,0:T(8,128)S(1)} %collective-permute-done.9.got1), custom_call_target="tpu_custom_call" | custom-call | tf_op jit(solution)/shard_map/pallas_call | solution.py:581
  26.6 6.6 %all-to-all-start = ((f32[32,1,128]{2,1,0:T(1,128)}), f32[32,1,128]{2,1,0:T(1,128)S(1)}, u32[]{:S(2)}, u32[]{:S(2)}) async-start(f32[32,1,128]{2,1,0:T(1,128)} %bitcast.8), calls=%async_computation | async-start | bytes 32768 | tf_op jit(solution)/shard_map/all_to_all | solution.py:635
  33.2 0.7 %shard_map.104.refs_3_ = f32[2,8,2048]{2,1,0:T(8,128)S(1)} custom-call(f32[4,8,128]{2,1,0:T(8,128)S(1)} %get-tuple-element.33.flags, f32[2,8,2048]{2,1,0:T(8,128)S(1)} %shard_map.100.field_ref.refs_2_, f32[2,8,2048]{2,1,0:T(8,128)S(1)} %get-tuple-element.61.base, bf16[256,1024]{1,0:T(8,128)(2,1)S(1)} %get-tuple-element.41.own_lanes, ...), custom_call_target="tpu_custom_call" | custom-call | tf_op jit(solution)/shard_map/pallas_call | solution.py:581
  33.9 6.4 %all-to-all-done = f32[32,1,128]{2,1,0:T(1,128)S(1)} async-done(((f32[32,1,128]{2,1,0:T(1,128)}), f32[32,1,128]{2,1,0:T(1,128)S(1)}, u32[]{:S(2)}, u32[]{:S(2)}) %all-to-all-start) | async-done | bytes 16416 | tf_op jit(solution)/shard_map/all_to_all | solution.py:635
  40.3 0.9 %shard_map.105 = (f32[2,8,2048]{2,1,0:T(8,128)}, f32[2,8,2048]{2,1,0:T(8,128)}) custom-call(f32[32,128]{1,0:T(8,128)S(1)} %bitcast.17, f32[2,8,2048]{2,1,0:T(8,128)S(1)} %get-tuple-element.34.field_ref.refs_1_.refs_0_, f32[2,8,2048]{2,1,0:T(8,128)S(1)} %get-tuple-element.45.field_ref.refs_2_.refs_1_, f32[2,8,2048]{2,1,0:T(8,128)S(1)} %shard_map.100.field_ref.refs_2_, ...), custom_call_target="tpu_custom_call" | custom-call | tf_op jit(solution)/shard_map/pallas_call | solution.py:650
  (1 shorter events, 0.0 us)
Async XLA Ops:
  0.6 10.8 %collective-permute-start.1 = (f32[2,8,2048]{2,1,0:T(8,128)}, f32[2,8,2048]{2,1,0:T(8,128)S(1)}, u32[]{:S(2)}, u32[]{:S(2)}) collective-permute-start(f32[2,8,2048]{2,1,0:T(8,128)} %bitcast.18), channel_id=1, source_target_pairs={{0,30},{2,0},{4,2},{6,4},{8,6},{10,8},{12,10},{14,12},{16,14},{18,... | collective-permute-start | bytes 393224 | tf_op jit(solution)/shard_map/ppermute | solution.py:582
  9.7 1.3 %collective-permute-start = (f32[4,2048]{1,0:T(4,128)S(1)}, f32[4,2048]{1,0:T(4,128)S(1)}, u32[]{:S(2)}, u32[]{:S(2)}) collective-permute-start(f32[4,2048]{1,0:T(4,128)S(1)} %get-tuple-element.39), channel_id=1, source_target_pairs={{0,1},{1,0},{2,3},{3,2},{4,5},{5,4},{6,7},{7,6},{8,9},{9,8},{10,11... | collective-permute-start | bytes 98312 | tf_op jit(solution)/shard_map/ppermute | solution.py:28
  9.8 2.1 %collective-permute-start.3 = (f32[8,896]{1,0:T(8,128)S(1)}, f32[8,896]{1,0:T(8,128)S(1)}, u32[]{:S(2)}, u32[]{:S(2)}) collective-permute-start(f32[8,896]{1,0:T(8,128)S(1)} %get-tuple-element.38.up), channel_id=1, source_target_pairs={{2,4},{4,2},{3,5},{5,3},{6,8},{8,6},{7,9},{9,7},{10,12},{12,10},{1... | collective-permute-start | bytes 86024 | tf_op jit(solution)/shard_map/ppermute | solution.py:42
  10.3 3.9 %collective-permute-start.2 = (f32[8,896]{1,0:T(8,128)S(1)}, f32[8,896]{1,0:T(8,128)S(1)}, u32[]{:S(2)}, u32[]{:S(2)}) collective-permute-start(f32[8,896]{1,0:T(8,128)S(1)} %get-tuple-element.38.up), channel_id=1, source_target_pairs={{0,2},{2,0},{1,3},{3,1},{4,6},{6,4},{5,7},{7,5},{8,10},{10,8},{9,1... | collective-permute-start | bytes 86024 | tf_op jit(solution)/shard_map/ppermute | solution.py:42
  16.1 1.2 %collective-permute-start.4 = (f32[2,2048]{1,0:T(2,128)S(1)}, f32[2,2048]{1,0:T(2,128)S(1)}, u32[]{:S(2)}, u32[]{:S(2)}) collective-permute-start(f32[2,2048]{1,0:T(2,128)S(1)} %get-tuple-element.47), channel_id=1, source_target_pairs={{0,1},{1,0},{2,3},{3,2},{4,5},{5,4},{6,7},{7,6},{8,9},{9,8},{10,11... | collective-permute-start | bytes 49160 | tf_op jit(solution)/shard_map/ppermute | solution.py:28
  16.1 3.7 %collective-permute-start.5 = (f32[2,8,128]{2,1,0:T(8,128)S(1)}, f32[2,8,128]{2,1,0:T(8,128)S(1)}, u32[]{:S(2)}, u32[]{:S(2)}) collective-permute-start(f32[2,8,128]{2,1,0:T(8,128)S(1)} %get-tuple-element.54), channel_id=1, source_target_pairs={{0,2},{2,0},{1,3},{3,1},{4,6},{6,4},{5,7},{7,5},{8,10},{10,8},{9,1... | collective-permute-start | bytes 24584 | tf_op jit(solution)/shard_map/ppermute | solution.py:42
  16.2 3.6 %collective-permute-start.6 = (f32[2,8,128]{2,1,0:T(8,128)S(1)}, f32[2,8,128]{2,1,0:T(8,128)S(1)}, u32[]{:S(2)}, u32[]{:S(2)}) collective-permute-start(f32[2,8,128]{2,1,0:T(8,128)S(1)} %get-tuple-element.55), channel_id=1, source_target_pairs={{2,4},{4,2},{3,5},{5,3},{6,8},{8,6},{7,9},{9,7},{10,12},{12,10},{1... | collective-permute-start | bytes 24584 | tf_op jit(solution)/shard_map/ppermute | solution.py:42
  21.2 3.2 %collective-permute-start.7 = (f32[2,2048]{1,0:T(2,128)S(1)}, f32[2,2048]{1,0:T(2,128)S(1)}, u32[]{:S(2)}, u32[]{:S(2)}) collective-permute-start(f32[2,2048]{1,0:T(2,128)S(1)} %get-tuple-element.56), channel_id=1, source_target_pairs={{0,1},{1,0},{2,3},{3,2},{4,5},{5,4},{6,7},{7,6},{8,9},{9,8},{10,11... | collective-permute-start | bytes 49160 | tf_op jit(solution)/shard_map/ppermute | solution.py:28
  21.3 4.6 %collective-permute-start.8 = (f32[2,8,128]{2,1,0:T(8,128)S(1)}, f32[2,8,128]{2,1,0:T(8,128)S(1)}, u32[]{:S(2)}, u32[]{:S(2)}) collective-permute-start(f32[2,8,128]{2,1,0:T(8,128)S(1)} %get-tuple-element.59), channel_id=1, source_target_pairs={{0,2},{2,0},{1,3},{3,1},{4,6},{6,4},{5,7},{7,5},{8,10},{10,8},{9,1... | collective-permute-start | bytes 24584 | tf_op jit(solution)/shard_map/ppermute | solution.py:42
  24.2 1.6 %collective-permute-start.9 = (f32[2,8,128]{2,1,0:T(8,128)S(1)}, f32[2,8,128]{2,1,0:T(8,128)S(1)}, u32[]{:S(2)}, u32[]{:S(2)}) collective-permute-start(f32[2,8,128]{2,1,0:T(8,128)S(1)} %get-tuple-element.60), channel_id=1, source_target_pairs={{2,4},{4,2},{3,5},{5,3},{6,8},{8,6},{7,9},{9,7},{10,12},{12,10},{1... | collective-permute-start | bytes 24584 | tf_op jit(solution)/shard_map/ppermute | solution.py:42
  26.6 13.7 %all-to-all-start = ((f32[32,1,128]{2,1,0:T(1,128)}), f32[32,1,128]{2,1,0:T(1,128)S(1)}, u32[]{:S(2)}, u32[]{:S(2)}) async-start(f32[32,1,128]{2,1,0:T(1,128)} %bitcast.8), calls=%async_computation | async-start | bytes 32768 | tf_op jit(solution)/shard_map/all_to_all | solution.py:635
